TPU v7x, 512 devices: a whole 4x8x8 slice. The times are simulated.
512 devices in a mesh: slab: 512 (over z, x, y, core).
Axes of the slice: x: 4, y: 8, z: 8, core: 2. Of those that a mesh axis runs over, the one named last changes fastest.
Arguments:
- start_vectors: float32 [2, 512, 256, 256], P(None, 'slab'), may hold values from -6 to 6
- levels: int32 [512, 256, 256], P('slab'), may hold values from 0 to 15
- energies: float32 [16], replicated, may hold values from -4 to 4
Outputs:
- cheb_field: float32 [2, 512, 256, 256], P(None, 'slab')
- lanczos_diag: float32 [2, 8], replicated
- lanczos_off: float32 [2, 7], replicated
- moments: float32 [2, 6], replicated
All inputs are finite; a program needn't handle non-finite values.
Results may differ from a plain program's by a relative error of at most 0.0001.
Values sent between devices are 32-bit elements; how exact they have to be, the bound alone decides.
No kernel may reach another device: no remote copies, remote signals or barrier semaphores. Data moves between devices by JAX's collectives and lax.ppermute only.
A program may use at most 64 MiB of HBM per device.

v0:
```python
import jax
import jax.numpy as jnp
from jax import lax
from jax.sharding import Mesh
from jax.sharding import PartitionSpec as P

LANCZOS = 8
SLAB = ("slab_0", "slab_1", "slab_2", "slab_3")


def from_behind(block, axis, distance):
    devices = range(lax.axis_size(axis))
    route = [((i - distance) % len(devices), i) for i in devices]
    return lax.ppermute(block, axis, route)


def one_axis_at_a_time(value, axes):
    for axis in axes:
        value = lax.psum(value, axis)
    return value


def inner(first, second):
    return jnp.sum(first * second, axis=(1, 2, 3))


def expand(values):
    return values[:, None, None, None]


def in_plane(field):
    beside = jnp.roll(field, 1, 2) + jnp.roll(field, -1, 2)
    return beside + jnp.roll(field, 1, 3) + jnp.roll(field, -1, 3)


def hamiltonian(field, onsite):
    below_plane = from_behind(field, SLAB, 1)
    above_plane = from_behind(field, SLAB, -1)
    inside = in_plane(field)
    below = jnp.concatenate([below_plane, field[:, :-1]], axis=1)
    above = jnp.concatenate([field[:, 1:], above_plane], axis=1)
    beside = inside + below + above
    return onsite[None] * field - beside


def shards(start_vectors, levels, energies):
    level_ids = lax.broadcasted_iota(jnp.int32, (energies.shape[0], 1, 1, 1), 0)
    onsite = jnp.sum(
        jnp.where(levels[None] == level_ids, energies[:, None, None, None], 0.0), axis=0
    )
    vec_count = start_vectors.shape[0]
    norm0 = one_axis_at_a_time(inner(start_vectors, start_vectors), SLAB)
    vector = start_vectors / expand(jnp.sqrt(norm0))
    previous = jnp.zeros_like(vector)
    beta_prev = jnp.zeros((vec_count,), jnp.float32)
    alphas = []
    betas = []
    for step in range(LANCZOS):
        work = hamiltonian(vector, onsite) - expand(beta_prev) * previous
        alpha, square = (
            one_axis_at_a_time(inner(vector, work), SLAB),
            one_axis_at_a_time(inner(work, work), SLAB),
        )
        alphas.append(alpha)
        if step < LANCZOS - 1:
            work = work - expand(alpha) * vector
            beta = jnp.sqrt(square - alpha * alpha)
            betas.append(beta)
            previous, vector, beta_prev = (vector, work / expand(beta), beta)
    diag = jnp.stack(alphas, axis=1)
    offd = jnp.stack(betas, axis=1)
    zero_col = jnp.zeros((vec_count, 1), jnp.float32)
    left = jnp.concatenate([zero_col, offd], axis=1)
    right = jnp.concatenate([offd, zero_col], axis=1)
    emin = jnp.min(diag - left - right, axis=1)
    emax = jnp.max(diag + left + right, axis=1)
    center = expand((emax + emin) * 0.5)
    half = expand(0.55 * (emax - emin))

    def scaled(field):
        return (hamiltonian(field, onsite) - center * field) / half

    term1 = scaled(start_vectors)
    term2 = 2.0 * scaled(term1) - start_vectors
    term3 = 2.0 * scaled(term2) - term1
    local = jnp.stack(
        [
            inner(start_vectors, term1),
            inner(start_vectors, term2),
            inner(term2, term2),
            inner(start_vectors, term3),
            inner(term3, term2),
            inner(term3, term3),
        ],
        axis=0,
    )
    sums = one_axis_at_a_time(local, SLAB)
    moments = (
        jnp.stack(
            [
                sums[0],
                sums[1],
                sums[3],
                2.0 * sums[2] - norm0,
                2.0 * sums[4] - sums[0],
                2.0 * sums[5] - norm0,
            ],
            axis=1,
        )
        / norm0[:, None]
    )
    return (term3, diag, offd, moments)


def solution(mesh):
    split = Mesh(mesh.devices.reshape(8, 4, 8, 2), ("slab_0", "slab_1", "slab_2", "slab_3"))
    in_specs = (P(None, SLAB, None, None), P(SLAB, None, None), P())
    out_specs = (P(None, SLAB, None, None), P(), P(), P())
    return jax.shard_map(
        shards, mesh=split, in_specs=in_specs, out_specs=out_specs, check_vma=False
    )
```

profile of v0, /device:TPU:1, one launch (start us, length us, event | category | flops | bytes accessed | tf_op | source)
XLA Modules:
  0.0 615.6 jit_solution(13365147373036719849)
XLA Ops:
  1.9 20.2 %psum.476 = f32[2]{0:T(128)S(1)} all-reduce(f32[2]{0:T(128)S(1)} %multiply_reduce_fusion.20), channel_id=1, replica_groups=mesh['slab_0'=8,'slab_1'=4,'slab_2'=8,'slab_3'=2] {'slab_0'}, use_global_device_ids=true, to_apply=%region_2.3 | all-reduce | flops 2 | bytes 16 | tf_op jit(solution)/shard_map/psum | solution.py:19
  22.1 8.5 %psum.477 = f32[2]{0:T(128)S(1)} all-reduce(f32[2]{0:T(128)S(1)} %psum.476), channel_id=1, replica_groups=mesh['slab_0'=8,'slab_1'=4,'slab_2'=8,'slab_3'=2] {'slab_1'}, use_global_device_ids=true, to_apply=%region_3.4 | all-reduce | flops 2 | bytes 16 | tf_op jit(solution)/shard_map/psum | solution.py:19
  30.6 13.8 %psum.478 = f32[2]{0:T(128)S(1)} all-reduce(f32[2]{0:T(128)S(1)} %psum.477), channel_id=1, replica_groups=mesh['slab_0'=8,'slab_1'=4,'slab_2'=8,'slab_3'=2] {'slab_2'}, use_global_device_ids=true, to_apply=%region_4.5 | all-reduce | flops 2 | bytes 16 | tf_op jit(solution)/shard_map/psum | solution.py:19
  44.4 12.3 %psum.479 = f32[2]{0:T(128)S(1)} all-reduce(f32[2]{0:T(128)S(1)} %psum.478), channel_id=1, replica_groups=mesh['slab_0'=8,'slab_1'=4,'slab_2'=8,'slab_3'=2] {'slab_3'}, use_global_device_ids=true, to_apply=%region_5.6 | all-reduce | flops 2 | bytes 16 | tf_op jit(solution)/shard_map/psum | solution.py:19
  64.5 7.6 %collective-permute-start.1 = (f32[2,1,256,256]{3,2,1,0:T(8,128)S(1)}, f32[2,1,256,256]{3,2,1,0:T(8,128)}, u32[]{:S(2)}, u32[]{:S(2)}) collective-permute-start(f32[2,1,256,256]{3,2,1,0:T(8,128)S(1)} %copy-done), channel_id=1, source_target_pairs={{1,0},{2,1},{3,2},{4,3},{5,4},{6,5},{7,6},{8,7},{9,8},{10,9},{11,1... | collective-permute-start | bytes 1572872 | tf_op jit(solution)/shard_map/ppermute | solution.py:14
  75.7 11.3 %all-reduce.13 = (f32[2]{0:T(128)S(1)}, f32[2]{0:T(128)S(1)}) all-reduce(f32[2]{0:T(128)S(1)} %get-tuple-element.27, f32[2]{0:T(128)S(1)} %get-tuple-element.26), channel_id=1, replica_groups=mesh['slab_0'=8,'slab_1'=4,'slab_2'=8,'slab_3'=2] {'slab_0'}, use_global_device_ids=true, to_apply=%region_12.13 | all-reduce | flops 4 | bytes 32 | tf_op jit(solution)/shard_map/psum | solution.py:19
  93.0 17.5 %all-reduce.6 = (f32[2]{0:T(128)S(1)}, f32[2]{0:T(128)S(1)}) all-reduce(f32[2]{0:T(128)S(1)} %get-tuple-element.74, f32[2]{0:T(128)S(1)} %get-tuple-element.75), channel_id=1, replica_groups=mesh['slab_0'=8,'slab_1'=4,'slab_2'=8,'slab_3'=2] {'slab_2'}, use_global_device_ids=true, to_apply=%region_14.15 | all-reduce | flops 4 | bytes 32 | tf_op jit(solution)/shard_map/psum | solution.py:19
  110.5 10.5 %all-reduce.27 = (f32[2]{0:T(128)S(1)}, f32[2]{0:T(128)S(1)}) all-reduce(f32[2]{0:T(128)S(1)} %get-tuple-element.46, f32[2]{0:T(128)S(1)} %get-tuple-element.47), channel_id=1, replica_groups=mesh['slab_0'=8,'slab_1'=4,'slab_2'=8,'slab_3'=2] {'slab_3'}, use_global_device_ids=true, to_apply=%region_15.16 | all-reduce | flops 4 | bytes 32 | tf_op jit(solution)/shard_map/psum | solution.py:19
  137.7 12.4 %all-reduce.12 = (f32[2]{0:T(128)S(1)}, f32[2]{0:T(128)S(1)}) all-reduce(f32[2]{0:T(128)S(1)} %get-tuple-element.25, f32[2]{0:T(128)S(1)} %get-tuple-element.24), channel_id=1, replica_groups=mesh['slab_0'=8,'slab_1'=4,'slab_2'=8,'slab_3'=2] {'slab_0'}, use_global_device_ids=true, to_apply=%region_22.23 | all-reduce | flops 4 | bytes 32 | tf_op jit(solution)/shard_map/psum | solution.py:19
  150.1 7.5 %all-reduce.19 = (f32[2]{0:T(128)S(1)}, f32[2]{0:T(128)S(1)}) all-reduce(f32[2]{0:T(128)S(1)} %get-tuple-element.58, f32[2]{0:T(128)S(1)} %get-tuple-element.59), channel_id=1, replica_groups=mesh['slab_0'=8,'slab_1'=4,'slab_2'=8,'slab_3'=2] {'slab_1'}, use_global_device_ids=true, to_apply=%region_23.24 | all-reduce | flops 4 | bytes 32 | tf_op jit(solution)/shard_map/psum | solution.py:19
  157.6 18.5 %all-reduce.5 = (f32[2]{0:T(128)S(1)}, f32[2]{0:T(128)S(1)}) all-reduce(f32[2]{0:T(128)S(1)} %get-tuple-element.72, f32[2]{0:T(128)S(1)} %get-tuple-element.73), channel_id=1, replica_groups=mesh['slab_0'=8,'slab_1'=4,'slab_2'=8,'slab_3'=2] {'slab_2'}, use_global_device_ids=true, to_apply=%region_24.25 | all-reduce | flops 4 | bytes 32 | tf_op jit(solution)/shard_map/psum | solution.py:19
  196.6 11.6 %all-reduce.11 = (f32[2]{0:T(128)S(1)}, f32[2]{0:T(128)S(1)}) all-reduce(f32[2]{0:T(128)S(1)} %get-tuple-element.23, f32[2]{0:T(128)S(1)} %get-tuple-element.22), channel_id=1, replica_groups=mesh['slab_0'=8,'slab_1'=4,'slab_2'=8,'slab_3'=2] {'slab_0'}, use_global_device_ids=true, to_apply=%region_32.33 | all-reduce | flops 4 | bytes 32 | tf_op jit(solution)/shard_map/psum | solution.py:19
  208.2 7.5 %all-reduce.18 = (f32[2]{0:T(128)S(1)}, f32[2]{0:T(128)S(1)}) all-reduce(f32[2]{0:T(128)S(1)} %get-tuple-element.56, f32[2]{0:T(128)S(1)} %get-tuple-element.57), channel_id=1, replica_groups=mesh['slab_0'=8,'slab_1'=4,'slab_2'=8,'slab_3'=2] {'slab_1'}, use_global_device_ids=true, to_apply=%region_33.34 | all-reduce | flops 4 | bytes 32 | tf_op jit(solution)/shard_map/psum | solution.py:19
  215.8 19.2 %all-reduce.4 = (f32[2]{0:T(128)S(1)}, f32[2]{0:T(128)S(1)}) all-reduce(f32[2]{0:T(128)S(1)} %get-tuple-element.70, f32[2]{0:T(128)S(1)} %get-tuple-element.71), channel_id=1, replica_groups=mesh['slab_0'=8,'slab_1'=4,'slab_2'=8,'slab_3'=2] {'slab_2'}, use_global_device_ids=true, to_apply=%region_34.35 | all-reduce | flops 4 | bytes 32 | tf_op jit(solution)/shard_map/psum | solution.py:19
  254.8 12.4 %all-reduce.10 = (f32[2]{0:T(128)S(1)}, f32[2]{0:T(128)S(1)}) all-reduce(f32[2]{0:T(128)S(1)} %get-tuple-element.21, f32[2]{0:T(128)S(1)} %get-tuple-element.20), channel_id=1, replica_groups=mesh['slab_0'=8,'slab_1'=4,'slab_2'=8,'slab_3'=2] {'slab_0'}, use_global_device_ids=true, to_apply=%region_42.43 | all-reduce | flops 4 | bytes 32 | tf_op jit(solution)/shard_map/psum | solution.py:19
  267.2 7.5 %all-reduce.17 = (f32[2]{0:T(128)S(1)}, f32[2]{0:T(128)S(1)}) all-reduce(f32[2]{0:T(128)S(1)} %get-tuple-element.54, f32[2]{0:T(128)S(1)} %get-tuple-element.55), channel_id=1, replica_groups=mesh['slab_0'=8,'slab_1'=4,'slab_2'=8,'slab_3'=2] {'slab_1'}, use_global_device_ids=true, to_apply=%region_43.44 | all-reduce | flops 4 | bytes 32 | tf_op jit(solution)/shard_map/psum | solution.py:19
  274.7 18.5 %all-reduce.3 = (f32[2]{0:T(128)S(1)}, f32[2]{0:T(128)S(1)}) all-reduce(f32[2]{0:T(128)S(1)} %get-tuple-element.68, f32[2]{0:T(128)S(1)} %get-tuple-element.69), channel_id=1, replica_groups=mesh['slab_0'=8,'slab_1'=4,'slab_2'=8,'slab_3'=2] {'slab_2'}, use_global_device_ids=true, to_apply=%region_44.45 | all-reduce | flops 4 | bytes 32 | tf_op jit(solution)/shard_map/psum | solution.py:19
  313.7 11.6 %all-reduce.9 = (f32[2]{0:T(128)S(1)}, f32[2]{0:T(128)S(1)}) all-reduce(f32[2]{0:T(128)S(1)} %get-tuple-element.19, f32[2]{0:T(128)S(1)} %get-tuple-element.18), channel_id=1, replica_groups=mesh['slab_0'=8,'slab_1'=4,'slab_2'=8,'slab_3'=2] {'slab_0'}, use_global_device_ids=true, to_apply=%region_52.53 | all-reduce | flops 4 | bytes 32 | tf_op jit(solution)/shard_map/psum | solution.py:19
  325.3 7.5 %all-reduce.16 = (f32[2]{0:T(128)S(1)}, f32[2]{0:T(128)S(1)}) all-reduce(f32[2]{0:T(128)S(1)} %get-tuple-element.52, f32[2]{0:T(128)S(1)} %get-tuple-element.53), channel_id=1, replica_groups=mesh['slab_0'=8,'slab_1'=4,'slab_2'=8,'slab_3'=2] {'slab_1'}, use_global_device_ids=true, to_apply=%region_53.54 | all-reduce | flops 4 | bytes 32 | tf_op jit(solution)/shard_map/psum | solution.py:19
  332.8 19.2 %all-reduce.2 = (f32[2]{0:T(128)S(1)}, f32[2]{0:T(128)S(1)}) all-reduce(f32[2]{0:T(128)S(1)} %get-tuple-element.66, f32[2]{0:T(128)S(1)} %get-tuple-element.67), channel_id=1, replica_groups=mesh['slab_0'=8,'slab_1'=4,'slab_2'=8,'slab_3'=2] {'slab_2'}, use_global_device_ids=true, to_apply=%region_54.55 | all-reduce | flops 4 | bytes 32 | tf_op jit(solution)/shard_map/psum | solution.py:19
  371.8 12.4 %all-reduce.8 = (f32[2]{0:T(128)S(1)}, f32[2]{0:T(128)S(1)}) all-reduce(f32[2]{0:T(128)S(1)} %get-tuple-element.17, f32[2]{0:T(128)S(1)} %get-tuple-element.16), channel_id=1, replica_groups=mesh['slab_0'=8,'slab_1'=4,'slab_2'=8,'slab_3'=2] {'slab_0'}, use_global_device_ids=true, to_apply=%region_62.63 | all-reduce | flops 4 | bytes 32 | tf_op jit(solution)/shard_map/psum | solution.py:19
  384.2 7.5 %all-reduce.15 = (f32[2]{0:T(128)S(1)}, f32[2]{0:T(128)S(1)}) all-reduce(f32[2]{0:T(128)S(1)} %get-tuple-element.50, f32[2]{0:T(128)S(1)} %get-tuple-element.51), channel_id=1, replica_groups=mesh['slab_0'=8,'slab_1'=4,'slab_2'=8,'slab_3'=2] {'slab_1'}, use_global_device_ids=true, to_apply=%region_63.64 | all-reduce | flops 4 | bytes 32 | tf_op jit(solution)/shard_map/psum | solution.py:19
  391.8 18.5 %all-reduce.1 = (f32[2]{0:T(128)S(1)}, f32[2]{0:T(128)S(1)}) all-reduce(f32[2]{0:T(128)S(1)} %get-tuple-element.64, f32[2]{0:T(128)S(1)} %get-tuple-element.65), channel_id=1, replica_groups=mesh['slab_0'=8,'slab_1'=4,'slab_2'=8,'slab_3'=2] {'slab_2'}, use_global_device_ids=true, to_apply=%region_64.65 | all-reduce | flops 4 | bytes 32 | tf_op jit(solution)/shard_map/psum | solution.py:19
  431.6 11.6 %all-reduce.7 = (f32[2]{0:T(128)S(1)}, f32[2]{0:T(128)S(1)}) all-reduce(f32[2]{0:T(128)S(1)} %get-tuple-element.15, f32[2]{0:T(128)S(1)} %get-tuple-element.14), channel_id=1, replica_groups=mesh['slab_0'=8,'slab_1'=4,'slab_2'=8,'slab_3'=2] {'slab_0'}, use_global_device_ids=true, to_apply=%region_72.73 | all-reduce | flops 4 | bytes 32 | tf_op jit(solution)/shard_map/psum | solution.py:19
  443.2 7.6 %all-reduce.14 = (f32[2]{0:T(128)S(1)}, f32[2]{0:T(128)S(1)}) all-reduce(f32[2]{0:T(128)S(1)} %get-tuple-element.48, f32[2]{0:T(128)S(1)} %get-tuple-element.49), channel_id=1, replica_groups=mesh['slab_0'=8,'slab_1'=4,'slab_2'=8,'slab_3'=2] {'slab_1'}, use_global_device_ids=true, to_apply=%region_73.74 | all-reduce | flops 4 | bytes 32 | tf_op jit(solution)/shard_map/psum | solution.py:19
  450.8 19.1 %all-reduce = (f32[2]{0:T(128)S(1)}, f32[2]{0:T(128)S(1)}) all-reduce(f32[2]{0:T(128)S(1)} %get-tuple-element.62, f32[2]{0:T(128)S(1)} %get-tuple-element.63), channel_id=1, replica_groups=mesh['slab_0'=8,'slab_1'=4,'slab_2'=8,'slab_3'=2] {'slab_2'}, use_global_device_ids=true, to_apply=%region_74.75 | all-reduce | flops 4 | bytes 32 | tf_op jit(solution)/shard_map/psum | solution.py:19
  490.9 12.4 %psum.536 = f32[2]{0:T(128)S(1)} all-reduce(f32[2]{0:T(128)S(1)} %fusion.69), channel_id=1, replica_groups=mesh['slab_0'=8,'slab_1'=4,'slab_2'=8,'slab_3'=2] {'slab_0'}, use_global_device_ids=true, to_apply=%region_77.78 | all-reduce | flops 2 | bytes 16 | tf_op jit(solution)/shard_map/psum | solution.py:19
  503.4 7.5 %psum.537 = f32[2]{0:T(128)S(1)} all-reduce(f32[2]{0:T(128)S(1)} %psum.536), channel_id=1, replica_groups=mesh['slab_0'=8,'slab_1'=4,'slab_2'=8,'slab_3'=2] {'slab_1'}, use_global_device_ids=true, to_apply=%region_78.79 | all-reduce | flops 2 | bytes 16 | tf_op jit(solution)/shard_map/psum | solution.py:19
  511.0 18.5 %psum.538 = f32[2]{0:T(128)S(1)} all-reduce(f32[2]{0:T(128)S(1)} %psum.537), channel_id=1, replica_groups=mesh['slab_0'=8,'slab_1'=4,'slab_2'=8,'slab_3'=2] {'slab_2'}, use_global_device_ids=true, to_apply=%region_79.80 | all-reduce | flops 2 | bytes 16 | tf_op jit(solution)/shard_map/psum | solution.py:19
  565.2 11.9 %psum.540 = f32[6,2]{0,1:T(2,128)S(1)} all-reduce(f32[6,2]{0,1:T(2,128)S(1)} %stack.105), channel_id=1, replica_groups=mesh['slab_0'=8,'slab_1'=4,'slab_2'=8,'slab_3'=2] {'slab_0'}, use_global_device_ids=true, to_apply=%region_89.90 | all-reduce | flops 12 | bytes 96 | tf_op jit(solution)/shard_map/psum | solution.py:19
  577.1 7.4 %psum.541 = f32[6,2]{0,1:T(2,128)S(1)} all-reduce(f32[6,2]{0,1:T(2,128)S(1)} %psum.540), channel_id=1, replica_groups=mesh['slab_0'=8,'slab_1'=4,'slab_2'=8,'slab_3'=2] {'slab_1'}, use_global_device_ids=true, to_apply=%region_90.91 | all-reduce | flops 12 | bytes 96 | tf_op jit(solution)/shard_map/psum | solution.py:19
  584.5 24.9 %psum.542 = f32[6,2]{0,1:T(2,128)S(1)} all-reduce(f32[6,2]{0,1:T(2,128)S(1)} %psum.541), channel_id=1, replica_groups=mesh['slab_0'=8,'slab_1'=4,'slab_2'=8,'slab_3'=2] {'slab_2'}, use_global_device_ids=true, to_apply=%region_91.92 | all-reduce | flops 12 | bytes 96 | tf_op jit(solution)/shard_map/psum | solution.py:19
  (208 shorter events, 199.7 us)
Async XLA Ops:
  0.6 56.1 %copy-start = (f32[2,1,256,256]{3,2,1,0:T(8,128)S(1)}, f32[2,1,256,256]{3,2,1,0:T(8,128)}, u32[]{:S(2)}) copy-start(f32[2,1,256,256]{3,2,1,0:T(8,128)} %param.3) | copy-start | bytes 1572868
  56.9 18.3 %collective-permute-start.2 = (f32[2,1,256,256]{3,2,1,0:T(8,128)S(1)}, f32[2,1,256,256]{3,2,1,0:T(8,128)S(1)}, u32[]{:S(2)}, u32[]{:S(2)}) collective-permute-start(f32[2,1,256,256]{3,2,1,0:T(8,128)S(1)} %broadcast_divide_fusion), channel_id=1, source_target_pairs={{511,0},{0,1},{1,2},{2,3},{3,4},{4,5},{5,6},{6,7},{7,8},{8,9},{9,1... | collective-permute-start | bytes 1572872 | tf_op jit(solution)/shard_map/ppermute | solution.py:14
  58.9 16.3 %collective-permute-start.3 = (f32[2,1,256,256]{3,2,1,0:T(8,128)S(1)}, f32[2,1,256,256]{3,2,1,0:T(8,128)S(1)}, u32[]{:S(2)}, u32[]{:S(2)}) collective-permute-start(f32[2,1,256,256]{3,2,1,0:T(8,128)S(1)} %broadcast_divide_fusion), channel_id=1, source_target_pairs={{1,0},{2,1},{3,2},{4,3},{5,4},{6,5},{7,6},{8,7},{9,8},{10,9},{11,1... | collective-permute-start | bytes 1572872 | tf_op jit(solution)/shard_map/ppermute | solution.py:14
  61.2 472.5 %collective-permute-start = (f32[2,1,256,256]{3,2,1,0:T(8,128)S(1)}, f32[2,1,256,256]{3,2,1,0:T(8,128)}, u32[]{:S(2)}, u32[]{:S(2)}) collective-permute-start(f32[2,1,256,256]{3,2,1,0:T(8,128)S(1)} %copy-done), channel_id=1, source_target_pairs={{511,0},{0,1},{1,2},{2,3},{3,4},{4,5},{5,6},{6,7},{7,8},{8,9},{9,1... | collective-permute-start | bytes 1572872 | tf_op jit(solution)/shard_map/ppermute | solution.py:14
  64.5 469.3 %collective-permute-start.1 = (f32[2,1,256,256]{3,2,1,0:T(8,128)S(1)}, f32[2,1,256,256]{3,2,1,0:T(8,128)}, u32[]{:S(2)}, u32[]{:S(2)}) collective-permute-start(f32[2,1,256,256]{3,2,1,0:T(8,128)S(1)} %copy-done), channel_id=1, source_target_pairs={{1,0},{2,1},{3,2},{4,3},{5,4},{6,5},{7,6},{8,7},{9,8},{10,9},{11,1... | collective-permute-start | bytes 1572872 | tf_op jit(solution)/shard_map/ppermute | solution.py:14
  121.2 10.0 %collective-permute-start.4 = (f32[2,1,256,256]{3,2,1,0:T(8,128)S(1)}, f32[2,1,256,256]{3,2,1,0:T(8,128)S(1)}, u32[]{:S(2)}, u32[]{:S(2)}) collective-permute-start(f32[2,1,256,256]{3,2,1,0:T(8,128)S(1)} %subtract_divide_fusion.6), channel_id=1, source_target_pairs={{511,0},{0,1},{1,2},{2,3},{3,4},{4,5},{5,6},{6,7},{7,8},{8,9},{9,1... | collective-permute-start | bytes 1572872 | tf_op jit(solution)/shard_map/ppermute | solution.py:14
  125.1 10.8 %collective-permute-start.5 = (f32[2,1,256,256]{3,2,1,0:T(8,128)S(1)}, f32[2,1,256,256]{3,2,1,0:T(8,128)}, u32[]{:S(2)}, u32[]{:S(2)}) collective-permute-start(f32[2,1,256,256]{3,2,1,0:T(8,128)S(1)} %subtract_divide_fusion.6), channel_id=1, source_target_pairs={{1,0},{2,1},{3,2},{4,3},{5,4},{6,5},{7,6},{8,7},{9,8},{10,9},{11,1... | collective-permute-start | bytes 1572872 | tf_op jit(solution)/shard_map/ppermute | solution.py:14
  128.2 7.7 %copy-start.2 = (f32[2,1,256,1]{3,2,1,0:T(8,128)S(1)}, f32[2,1,256,1]{3,2,1,0:T(8,128)}, u32[]{:S(2)}) copy-start(f32[2,1,256,1]{3,2,1,0:T(8,128)} %get-tuple-element.166) | copy-start | bytes 6148
  180.1 10.0 %collective-permute-start.6 = (f32[2,1,256,256]{3,2,1,0:T(8,128)S(1)}, f32[2,1,256,256]{3,2,1,0:T(8,128)S(1)}, u32[]{:S(2)}, u32[]{:S(2)}) collective-permute-start(f32[2,1,256,256]{3,2,1,0:T(8,128)S(1)} %subtract_divide_fusion.5), channel_id=1, source_target_pairs={{511,0},{0,1},{1,2},{2,3},{3,4},{4,5},{5,6},{6,7},{7,8},{8,9},{9,1... | collective-permute-start | bytes 1572872 | tf_op jit(solution)/shard_map/ppermute | solution.py:14
  184.0 10.8 %collective-permute-start.7 = (f32[2,1,256,256]{3,2,1,0:T(8,128)S(1)}, f32[2,1,256,256]{3,2,1,0:T(8,128)}, u32[]{:S(2)}, u32[]{:S(2)}) collective-permute-start(f32[2,1,256,256]{3,2,1,0:T(8,128)S(1)} %subtract_divide_fusion.5), channel_id=1, source_target_pairs={{1,0},{2,1},{3,2},{4,3},{5,4},{6,5},{7,6},{8,7},{9,8},{10,9},{11,1... | collective-permute-start | bytes 1572872 | tf_op jit(solution)/shard_map/ppermute | solution.py:14
  187.1 7.7 %copy-start.4 = (f32[2,1,256,1]{3,2,1,0:T(8,128)S(1)}, f32[2,1,256,1]{3,2,1,0:T(8,128)}, u32[]{:S(2)}) copy-start(f32[2,1,256,1]{3,2,1,0:T(8,128)} %get-tuple-element.158) | copy-start | bytes 6148
  187.1 7.7 %copy-start.5 = (f32[2,1,256,1]{3,2,1,0:T(8,128)S(1)}, f32[2,1,256,1]{3,2,1,0:T(8,128)}, u32[]{:S(2)}) copy-start(f32[2,1,256,1]{3,2,1,0:T(8,128)} %get-tuple-element.159) | copy-start | bytes 6148
  238.3 10.0 %collective-permute-start.8 = (f32[2,1,256,256]{3,2,1,0:T(8,128)S(1)}, f32[2,1,256,256]{3,2,1,0:T(8,128)S(1)}, u32[]{:S(2)}, u32[]{:S(2)}) collective-permute-start(f32[2,1,256,256]{3,2,1,0:T(8,128)S(1)} %subtract_divide_fusion.4), channel_id=1, source_target_pairs={{511,0},{0,1},{1,2},{2,3},{3,4},{4,5},{5,6},{6,7},{7,8},{8,9},{9,1... | collective-permute-start | bytes 1572872 | tf_op jit(solution)/shard_map/ppermute | solution.py:14
  242.2 10.8 %collective-permute-start.9 = (f32[2,1,256,256]{3,2,1,0:T(8,128)S(1)}, f32[2,1,256,256]{3,2,1,0:T(8,128)}, u32[]{:S(2)}, u32[]{:S(2)}) collective-permute-start(f32[2,1,256,256]{3,2,1,0:T(8,128)S(1)} %subtract_divide_fusion.4), channel_id=1, source_target_pairs={{1,0},{2,1},{3,2},{4,3},{5,4},{6,5},{7,6},{8,7},{9,8},{10,9},{11,1... | collective-permute-start | bytes 1572872 | tf_op jit(solution)/shard_map/ppermute | solution.py:14
  245.2 7.7 %copy-start.6 = (f32[2,1,256,1]{3,2,1,0:T(8,128)S(1)}, f32[2,1,256,1]{3,2,1,0:T(8,128)}, u32[]{:S(2)}) copy-start(f32[2,1,256,1]{3,2,1,0:T(8,128)} %get-tuple-element.150) | copy-start | bytes 6148
  297.2 10.0 %collective-permute-start.10 = (f32[2,1,256,256]{3,2,1,0:T(8,128)S(1)}, f32[2,1,256,256]{3,2,1,0:T(8,128)S(1)}, u32[]{:S(2)}, u32[]{:S(2)}) collective-permute-start(f32[2,1,256,256]{3,2,1,0:T(8,128)S(1)} %subtract_divide_fusion.3), channel_id=1, source_target_pairs={{511,0},{0,1},{1,2},{2,3},{3,4},{4,5},{5,6},{6,7},{7,8},{8,9},{9,1... | collective-permute-start | bytes 1572872 | tf_op jit(solution)/shard_map/ppermute | solution.py:14
  301.1 10.8 %collective-permute-start.11 = (f32[2,1,256,256]{3,2,1,0:T(8,128)S(1)}, f32[2,1,256,256]{3,2,1,0:T(8,128)}, u32[]{:S(2)}, u32[]{:S(2)}) collective-permute-start(f32[2,1,256,256]{3,2,1,0:T(8,128)S(1)} %subtract_divide_fusion.3), channel_id=1, source_target_pairs={{1,0},{2,1},{3,2},{4,3},{5,4},{6,5},{7,6},{8,7},{9,8},{10,9},{11,1... | collective-permute-start | bytes 1572872 | tf_op jit(solution)/shard_map/ppermute | solution.py:14
  304.2 7.7 %copy-start.8 = (f32[2,1,256,1]{3,2,1,0:T(8,128)S(1)}, f32[2,1,256,1]{3,2,1,0:T(8,128)}, u32[]{:S(2)}) copy-start(f32[2,1,256,1]{3,2,1,0:T(8,128)} %get-tuple-element.142) | copy-start | bytes 6148
  355.3 10.0 %collective-permute-start.12 = (f32[2,1,256,256]{3,2,1,0:T(8,128)S(1)}, f32[2,1,256,256]{3,2,1,0:T(8,128)S(1)}, u32[]{:S(2)}, u32[]{:S(2)}) collective-permute-start(f32[2,1,256,256]{3,2,1,0:T(8,128)S(1)} %subtract_divide_fusion.2), channel_id=1, source_target_pairs={{511,0},{0,1},{1,2},{2,3},{3,4},{4,5},{5,6},{6,7},{7,8},{8,9},{9,1... | collective-permute-start | bytes 1572872 | tf_op jit(solution)/shard_map/ppermute | solution.py:14
  359.2 10.8 %collective-permute-start.13 = (f32[2,1,256,256]{3,2,1,0:T(8,128)S(1)}, f32[2,1,256,256]{3,2,1,0:T(8,128)}, u32[]{:S(2)}, u32[]{:S(2)}) collective-permute-start(f32[2,1,256,256]{3,2,1,0:T(8,128)S(1)} %subtract_divide_fusion.2), channel_id=1, source_target_pairs={{1,0},{2,1},{3,2},{4,3},{5,4},{6,5},{7,6},{8,7},{9,8},{10,9},{11,1... | collective-permute-start | bytes 1572872 | tf_op jit(solution)/shard_map/ppermute | solution.py:14
  362.3 7.7 %copy-start.10 = (f32[2,1,256,1]{3,2,1,0:T(8,128)S(1)}, f32[2,1,256,1]{3,2,1,0:T(8,128)}, u32[]{:S(2)}) copy-start(f32[2,1,256,1]{3,2,1,0:T(8,128)} %get-tuple-element.134) | copy-start | bytes 6148
  414.3 10.0 %collective-permute-start.14 = (f32[2,1,256,256]{3,2,1,0:T(8,128)S(1)}, f32[2,1,256,256]{3,2,1,0:T(8,128)}, u32[]{:S(2)}, u32[]{:S(2)}) collective-permute-start(f32[2,1,256,256]{3,2,1,0:T(8,128)S(1)} %subtract_divide_fusion.1), channel_id=1, source_target_pairs={{511,0},{0,1},{1,2},{2,3},{3,4},{4,5},{5,6},{6,7},{7,8},{8,9},{9,1... | collective-permute-start | bytes 1572872 | tf_op jit(solution)/shard_map/ppermute | solution.py:14
  418.1 10.9 %collective-permute-start.15 = (f32[2,1,256,256]{3,2,1,0:T(8,128)S(1)}, f32[2,1,256,256]{3,2,1,0:T(8,128)}, u32[]{:S(2)}, u32[]{:S(2)}) collective-permute-start(f32[2,1,256,256]{3,2,1,0:T(8,128)S(1)} %subtract_divide_fusion.1), channel_id=1, source_target_pairs={{1,0},{2,1},{3,2},{4,3},{5,4},{6,5},{7,6},{8,7},{9,8},{10,9},{11,1... | collective-permute-start | bytes 1572872 | tf_op jit(solution)/shard_map/ppermute | solution.py:14
  474.3 10.0 %collective-permute-start.16 = (f32[2,1,256,256]{3,2,1,0:T(8,128)S(1)}, f32[2,1,256,256]{3,2,1,0:T(8,128)S(1)}, u32[]{:S(2)}, u32[]{:S(2)}) collective-permute-start(f32[2,1,256,256]{3,2,1,0:T(8,128)S(1)} %subtract_divide_fusion), channel_id=1, source_target_pairs={{511,0},{0,1},{1,2},{2,3},{3,4},{4,5},{5,6},{6,7},{7,8},{8,9},{9,1... | collective-permute-start | bytes 1572872 | tf_op jit(solution)/shard_map/ppermute | solution.py:14
  478.2 10.8 %collective-permute-start.17 = (f32[2,1,256,256]{3,2,1,0:T(8,128)S(1)}, f32[2,1,256,256]{3,2,1,0:T(8,128)}, u32[]{:S(2)}, u32[]{:S(2)}) collective-permute-start(f32[2,1,256,256]{3,2,1,0:T(8,128)S(1)} %subtract_divide_fusion), channel_id=1, source_target_pairs={{1,0},{2,1},{3,2},{4,3},{5,4},{6,5},{7,6},{8,7},{9,8},{10,9},{11,1... | collective-permute-start | bytes 1572872 | tf_op jit(solution)/shard_map/ppermute | solution.py:14
  481.2 7.8 %copy-start.12 = (f32[2,1,256,1]{3,2,1,0:T(8,128)S(1)}, f32[2,1,256,1]{3,2,1,0:T(8,128)}, u32[]{:S(2)}) copy-start(f32[2,1,256,1]{3,2,1,0:T(8,128)} %get-tuple-element.118) | copy-start | bytes 6148
  481.2 7.8 %copy-start.13 = (f32[2,1,256,1]{3,2,1,0:T(8,128)S(1)}, f32[2,1,256,1]{3,2,1,0:T(8,128)}, u32[]{:S(2)}) copy-start(f32[2,1,256,1]{3,2,1,0:T(8,128)} %get-tuple-element.119) | copy-start | bytes 6148
  489.0 44.7 %copy-start.1 = (f32[2,1,255,256]{3,2,1,0:T(8,128)S(1)}, f32[2,1,255,256]{3,2,1,0:T(8,128)}, u32[]{:S(2)}) copy-start(f32[2,1,255,256]{3,2,1,0:T(8,128)} %get-tuple-element.182) | copy-start | bytes 1566724
  535.6 10.0 %collective-permute-start.18 = (f32[2,1,256,256]{3,2,1,0:T(8,128)S(1)}, f32[2,1,256,256]{3,2,1,0:T(8,128)S(1)}, u32[]{:S(2)}, u32[]{:S(2)}) collective-permute-start(f32[2,1,256,256]{3,2,1,0:T(8,128)S(1)} %fusion.6), channel_id=1, source_target_pairs={{511,0},{0,1},{1,2},{2,3},{3,4},{4,5},{5,6},{6,7},{7,8},{8,9},{9,1... | collective-permute-start | bytes 1572872 | tf_op jit(solution)/shard_map/ppermute | solution.py:14
  539.5 10.8 %collective-permute-start.19 = (f32[2,1,256,256]{3,2,1,0:T(8,128)S(1)}, f32[2,1,256,256]{3,2,1,0:T(8,128)S(1)}, u32[]{:S(2)}, u32[]{:S(2)}) collective-permute-start(f32[2,1,256,256]{3,2,1,0:T(8,128)S(1)} %fusion.6), channel_id=1, source_target_pairs={{1,0},{2,1},{3,2},{4,3},{5,4},{6,5},{7,6},{8,7},{9,8},{10,9},{11,1... | collective-permute-start | bytes 1572872 | tf_op jit(solution)/shard_map/ppermute | solution.py:14
  550.8 8.0 %collective-permute-start.20 = (f32[2,1,256,256]{3,2,1,0:T(8,128)S(1)}, f32[2,1,256,256]{3,2,1,0:T(8,128)S(1)}, u32[]{:S(2)}, u32[]{:S(2)}) collective-permute-start(f32[2,1,256,256]{3,2,1,0:T(8,128)S(1)} %multiply_subtract_fusion.1), channel_id=1, source_target_pairs={{511,0},{0,1},{1,2},{2,3},{3,4},{4,5},{5,6},{6,7},{7,8},{8,9},{9,1... | collective-permute-start | bytes 1572872 | tf_op jit(solution)/shard_map/ppermute | solution.py:14
  552.7 10.5 %collective-permute-start.21 = (f32[2,1,256,256]{3,2,1,0:T(8,128)S(1)}, f32[2,1,256,256]{3,2,1,0:T(8,128)S(1)}, u32[]{:S(2)}, u32[]{:S(2)}) collective-permute-start(f32[2,1,256,256]{3,2,1,0:T(8,128)S(1)} %multiply_subtract_fusion.1), channel_id=1, source_target_pairs={{1,0},{2,1},{3,2},{4,3},{5,4},{6,5},{7,6},{8,7},{9,8},{10,9},{11,1... | collective-permute-start | bytes 1572872 | tf_op jit(solution)/shard_map/ppermute | solution.py:14
  (13 other events, 62.9 us)
where the time goes:
time: 617 us; the launch traced here: 616 us
  blocking collectives  442 us (72%)
  starting transfers between devices  68.7 us (11%)
  waiting for transfers between devices  66.6 us (11%)
  other arithmetic  22.6 us (4%)
  local copies, waits for them, and re-layouts  14.3 us (2%)
    psum x40, blocking collectives, one_axis_at_a_time(): value = lax.psum(value, axis)  442 us
    ppermute x22, starting transfers between devices, from_behind(): return lax.ppermute(block, axis, route)  68.7 us
    ppermute x22, waiting for transfers between devices, from_behind(): return lax.ppermute(block, axis, route)  66.6 us
    reduce_sum x10, other arithmetic, inner(): return jnp.sum(first * second, axis=(1, 2, 3))  16.6 us
  transfers between devices with their start and end apart: 22, of which 18 were waited for; matrix products, arithmetic and copies ran while one was open for 5% of the time, Pallas kernels for 0%

commit v1 on v0

v1 whole, which is shorter than its diff:
```python
import functools

import jax
import jax.numpy as jnp
from jax import lax
from jax.experimental import pallas as pl
from jax.experimental.pallas import tpu as pltpu
from jax.sharding import Mesh
from jax.sharding import PartitionSpec as P

LANCZOS = 8
SLAB = ("slab_0", "slab_1", "slab_2", "slab_3")
ROWS = 32
NUDGE = 1e-3
ROUNDING = 2e-7
TOLERANCE = 2e-5
VMEM = pl.BlockSpec(memory_space=pltpu.VMEM)
SMEM = pl.BlockSpec(memory_space=pltpu.SMEM)
PARAMS = pltpu.CompilerParams(vmem_limit_bytes=24 * 1024 * 1024)


def from_behind(block, axis, distance):
    devices = range(lax.axis_size(axis))
    route = [((i - distance) % len(devices), i) for i in devices]
    return lax.ppermute(block, axis, route)


def one_axis_at_a_time(value, axes):
    for axis in axes:
        value = lax.psum(value, axis)
    return value


def inner(first, second):
    return jnp.sum(first * second, axis=(1, 2, 3))


def expand(values):
    return values[:, None, None, None]


def hamiltonian(field, onsite):
    below = from_behind(field, SLAB, 1)
    above = from_behind(field, SLAB, -1)
    beside = jnp.roll(field, 1, 2) + jnp.roll(field, -1, 2)
    beside = beside + jnp.roll(field, 1, 3) + jnp.roll(field, -1, 3)
    return onsite[None] * field - (beside + below + above)


def stepwise(start_vectors, levels, energies):
    level_ids = lax.broadcasted_iota(jnp.int32, (energies.shape[0], 1, 1, 1), 0)
    onsite = jnp.sum(
        jnp.where(levels[None] == level_ids, energies[:, None, None, None], 0.0), axis=0
    )
    vec_count = start_vectors.shape[0]
    norm0 = one_axis_at_a_time(inner(start_vectors, start_vectors), SLAB)

    def lanczos(state, step):
        vector, previous, beta_prev = state
        work = hamiltonian(vector, onsite) - expand(beta_prev) * previous
        alpha = one_axis_at_a_time(inner(vector, work), SLAB)
        work = work - expand(alpha) * vector
        beta = jnp.sqrt(one_axis_at_a_time(inner(work, work), SLAB))
        return (work / expand(beta), vector, beta), (alpha, beta)

    vector = start_vectors / expand(jnp.sqrt(norm0))
    _, (alphas, betas) = lax.scan(
        lanczos,
        (vector, jnp.zeros_like(vector), jnp.zeros((vec_count,), jnp.float32)),
        None,
        length=LANCZOS,
    )
    diag = alphas.T
    offd = betas[: LANCZOS - 1].T
    zero_col = jnp.zeros((vec_count, 1), jnp.float32)
    left = jnp.concatenate([zero_col, offd], axis=1)
    right = jnp.concatenate([offd, zero_col], axis=1)
    emin = jnp.min(diag - left - right, axis=1)
    emax = jnp.max(diag + left + right, axis=1)
    center = expand((emax + emin) * 0.5)
    half = expand(0.55 * (emax - emin))

    def scaled(field):
        return (hamiltonian(field, onsite) - center * field) / half

    term1 = scaled(start_vectors)
    term2 = 2.0 * scaled(term1) - start_vectors
    term3 = 2.0 * scaled(term2) - term1
    local = jnp.stack(
        [
            inner(start_vectors, term1),
            inner(start_vectors, term2),
            inner(start_vectors, term3),
            inner(term2, term2),
            inner(term3, term2),
            inner(term3, term3),
        ],
        axis=0,
    )
    sums = one_axis_at_a_time(local, SLAB)
    moments = (
        jnp.stack(
            [
                sums[0],
                sums[1],
                sums[2],
                2.0 * sums[3] - norm0,
                2.0 * sums[4] - sums[0],
                2.0 * sums[5] - norm0,
            ],
            axis=1,
        )
        / norm0[:, None]
    )
    return (term3, diag, offd, moments)


def onsite_kernel(energies_ref, base_ref, levels_ref, out_ref):
    shift, inverse = base_ref[0], base_ref[1]

    def rows_of(chunk, carry):
        rows = pl.ds(chunk * ROWS, ROWS)
        level = levels_ref[0, rows]
        value = jnp.zeros(level.shape, jnp.float32)
        for index in range(energies_ref.shape[0]):
            value = jnp.where(
                level == index, (energies_ref[index] - shift) * inverse, value
            )
        out_ref[0, rows] = value
        return carry

    lax.fori_loop(0, 256 // ROWS, rows_of, 0)


def advance(below, current, above, onsite, previous, inverse, chunk):
    rows = pl.ds(chunk * ROWS, ROWS)
    before = pl.ds(pl.multiple_of((chunk * ROWS + 248) % 256, 8), 8)
    after = pl.ds(pl.multiple_of((chunk * ROWS + ROWS) % 256, 8), 8)
    middle = current[rows]
    tall = jnp.concatenate([current[before], middle, current[after]], axis=0)
    beside = pltpu.roll(tall, 1, 0)[8 : 8 + ROWS]
    beside = beside + pltpu.roll(tall, ROWS + 15, 0)[8 : 8 + ROWS]
    beside = beside + (pltpu.roll(middle, 1, 1) + pltpu.roll(middle, 255, 1))
    beside = beside + (below[rows] + above[rows])
    result = onsite[rows] * middle - inverse * beside
    if previous is not None:
        result = result - previous[rows]
    return result, middle


def folded(values):
    total = values[:, :128] + values[:, 128:]
    return jnp.sum(total.reshape(ROWS // 8, 8, 128), axis=0)


def round_kernel(first, last, base_ref, *refs):
    refs = list(refs)
    low, own, high = refs[:3]
    refs = refs[3:]
    if first:
        sites = refs.pop(0)
        planes_on = [low.at[2], sites.at[0], sites.at[1], high.at[2]]
        before = [None] * 4
    else:
        onsite, prior = refs[:2]
        refs = refs[2:]
        planes_on = [onsite.at[j] for j in range(4)]
        before = [prior.at[j] for j in range(4)]
    if first:
        one, two, kept, sums = refs
    elif last:
        sums, one = refs
        two = None
    else:
        one, two, sums = refs
    inverse = base_ref[1]
    planes = [low.at[0], low.at[1], own.at[0], own.at[1], high.at[0], high.at[1]]
    zero = jnp.zeros((8, 128), jnp.float32)

    def first_half(chunk, carry):
        square0, cross0, square1 = carry
        rows = pl.ds(chunk * ROWS, ROWS)
        for j in range(4):
            new, middle = advance(
                planes[j], planes[j + 1], planes[j + 2], planes_on[j], before[j],
                inverse, chunk,
            )
            one[j, rows] = new
            if first:
                kept[j, rows] = planes_on[j][rows]
            if j in (1, 2):
                if first:
                    square0 = square0 + folded(middle * middle)
                cross0 = cross0 + folded(new * middle)
                square1 = square1 + folded(new * new)
        return square0, cross0, square1

    square0, cross0, square1 = lax.fori_loop(
        0, 256 // ROWS, first_half, (zero, zero, zero)
    )

    def second_half(chunk, carry):
        cross1, square2 = carry
        rows = pl.ds(chunk * ROWS, ROWS)
        for j in range(2):
            new, middle = advance(
                one.at[j], one.at[j + 1], one.at[j + 2], planes_on[j + 1],
                planes[j + 2], inverse, chunk,
            )
            if two is not None:
                two[j, rows] = new
                square2 = square2 + folded(new * new)
            cross1 = cross1 + folded(new * middle)
        return cross1, square2

    cross1, square2 = lax.fori_loop(0, 256 // ROWS, second_half, (zero, zero))
    for index, value in enumerate((square0, cross0, square1, cross1, square2)):
        sums[index] = value


def shape(*dims):
    return jax.ShapeDtypeStruct(dims, jnp.float32)


ROUND_COST = pl.CostEstimate(flops=4_000_000, bytes_accessed=5_000_000, transcendentals=0)


def first_round(base, low, own, high, sites):
    return pl.pallas_call(
        functools.partial(round_kernel, True, False),
        out_shape=(
            shape(4, 256, 256), shape(2, 256, 256), shape(4, 256, 256), shape(5, 8, 128),
        ),
        in_specs=[SMEM] + [VMEM] * 4,
        out_specs=(VMEM,) * 4,
        compiler_params=PARAMS,
        cost_estimate=ROUND_COST,
        name="first_round",
    )(base, low, own, high, sites)


def middle_round(base, low, own, high, onsite, prior):
    return pl.pallas_call(
        functools.partial(round_kernel, False, False),
        out_shape=(shape(4, 256, 256), shape(2, 256, 256), shape(5, 8, 128)),
        in_specs=[SMEM] + [VMEM] * 5,
        out_specs=(VMEM,) * 3,
        compiler_params=PARAMS,
        cost_estimate=ROUND_COST,
        name="middle_round",
    )(base, low, own, high, onsite, prior)


def last_round(base, low, own, high, onsite, prior):
    return pl.pallas_call(
        functools.partial(round_kernel, False, True),
        out_shape=shape(5, 8, 128),
        in_specs=[SMEM] + [VMEM] * 5,
        out_specs=VMEM,
        scratch_shapes=[pltpu.VMEM((4, 256, 256), jnp.float32)],
        compiler_params=PARAMS,
        cost_estimate=ROUND_COST,
        name="last_round",
    )(base, low, own, high, onsite, prior)


def pack_kernel(a_ref, b_ref, c_ref, d_ref, out_ref):
    lane = lax.broadcasted_iota(jnp.int32, (8, 128), 1)
    row = jnp.zeros((8, 128), jnp.float32)
    for index, ref in enumerate((a_ref, b_ref, c_ref, d_ref)):
        places = [None, 8 + 2 * index, 2 * index + 1, 9 + 2 * index, 2 * index + 2]
        if index == 0:
            places[0] = 0
        if index == 3:
            places[4] = None
        for entry, place in enumerate(places):
            if place is None:
                continue
            total = jnp.sum(jnp.sum(ref[entry], axis=0, keepdims=True), axis=1, keepdims=True)
            row = jnp.where(lane == place, total, row)
    out_ref[...] = row[:1]


def pack(sums):
    return pl.pallas_call(
        pack_kernel,
        out_shape=shape(1, 128),
        in_specs=[VMEM] * 4,
        out_specs=VMEM,
        compiler_params=PARAMS,
        name="pack_sums",
    )(*sums)


def finish_kernel(
    base_ref, side_ref, rows_ref, p0, p1, p2, p3,
    field_ref, diag_ref, offd_ref, moments_ref, good_ref,
):
    shift, scale = base_ref[0], base_ref[2]
    lane = lax.broadcasted_iota(jnp.int32, (2, 128), 1)
    rows = rows_ref[...]
    sub = lax.broadcasted_iota(jnp.int32, rows.shape, 0)
    even = jnp.sum(jnp.where(sub % 2 == 0, rows, 0.0), axis=0, keepdims=True)
    odd = jnp.sum(jnp.where(sub % 2 == 1, rows, 0.0), axis=0, keepdims=True)
    total = jnp.concatenate([even, odd], axis=0)

    def column(index):
        return jnp.broadcast_to(total[:, index : index + 1], (2, 128))

    plain = [column(index) for index in range(8)]
    largest = [jnp.maximum(plain[k], plain[min(k + 1, 7)]) for k in range(8)]
    square = [
        plain[k] + jnp.where(lane == k + 1, NUDGE * plain[k], 0.0) for k in range(8)
    ]
    cross = [
        column(8 + k) + jnp.where(lane == k + 9, NUDGE * largest[k], 0.0) for k in range(8)
    ]
    moment = []
    for k in range(8):
        moment.append(square[k] - square[k - 1] if k else square[k])
        moment.append(cross[k] - cross[k - 1] if k else cross[k])
    norm0 = moment[0]
    sigma = [value / norm0 for value in moment]
    normal = list(sigma)
    zero = jnp.zeros_like(norm0)
    older = [zero] * len(sigma)
    alphas, betas = [], []
    weight = zero
    for k in range(LANCZOS):
        size = len(sigma)
        pushed = [
            (sigma[l + 1] + sigma[l - 1]) if l else sigma[1] for l in range(size - 1)
        ]
        ratio = (pushed[k] - weight * older[k]) / sigma[k]
        alphas.append(ratio)
        if k < LANCZOS - 1:
            fresh = [
                pushed[l] - ratio * sigma[l] - weight * older[l] for l in range(size - 1)
            ]
            weight = fresh[k + 1] / sigma[k]
            betas.append(jnp.sqrt(weight))
            older, sigma = sigma, fresh
    alphas = [scale * value + shift for value in alphas]
    betas = [scale * value for value in betas]

    def spread(values):
        error, norm = zero, zero
        for value in values:
            exact = jnp.broadcast_to(value[:, :1], value.shape)
            error = error + jnp.square(
                jnp.broadcast_to(
                    jnp.sum(jnp.abs(value - exact), axis=1, keepdims=True), value.shape
                )
            )
            norm = norm + jnp.square(exact)
        error = jnp.sum(error, axis=0, keepdims=True)
        norm = jnp.sum(norm, axis=0, keepdims=True)
        allowed = TOLERANCE * NUDGE / ROUNDING
        return jnp.where(error <= allowed * allowed * norm, 1, 0)

    fits = jnp.minimum(spread(alphas), spread(betas))
    good_ref[0] = jnp.min(fits)

    lows, highs = [], []
    for k in range(LANCZOS):
        left = betas[k - 1] if k else zero
        right = betas[k] if k < LANCZOS - 1 else zero
        lows.append(alphas[k] - left - right)
        highs.append(alphas[k] + left + right)
    emin = functools.reduce(jnp.minimum, lows)
    emax = functools.reduce(jnp.maximum, highs)
    center = (emax + emin) * 0.5
    half = 0.55 * (emax - emin)
    offset = (shift - center) / half
    factor = scale / half

    def apply(coefs):
        out = []
        for l in range(len(coefs) + 1):
            value = zero
            if l < len(coefs):
                value = value + offset * coefs[l]
            if l + 1 < len(coefs):
                value = value + factor * coefs[l + 1]
            if l:
                value = value + factor * coefs[l - 1]
            out.append(value)
        return out

    terms = [[zero + 1.0]]
    terms.append(apply(terms[0]))
    for m in range(2, 7):
        nxt = apply(terms[-1])
        old = terms[-2]
        terms.append(
            [2.0 * v - (old[l] if l < len(old) else zero) for l, v in enumerate(nxt)]
        )
    diag, offd, out = zero, zero, zero
    for k in range(LANCZOS):
        diag = jnp.where(lane == k, jnp.broadcast_to(alphas[k][:, :1], lane.shape), diag)
        if k < LANCZOS - 1:
            offd = jnp.where(lane == k, jnp.broadcast_to(betas[k][:, :1], lane.shape), offd)
    for m in range(1, 7):
        value = functools.reduce(
            jnp.add, [c * normal[l] for l, c in enumerate(terms[m])]
        )
        out = jnp.where(lane == m - 1, jnp.broadcast_to(value[:, :1], lane.shape), out)
    diag_ref[...] = diag[:, :8]
    offd_ref[...] = offd[:, :7]
    moments_ref[...] = out[:, :6]

    upper = side_ref[0] == 1
    weights = []
    for l in range(4):
        value = jnp.broadcast_to(terms[3][l][:, :1], lane.shape)
        pick = jnp.where(upper, value[1:2], value[0:1])
        weights.append(jnp.concatenate([pick, pick], axis=1))
    sources = [
        [p0.at[0], p0.at[1]],
        [p1.at[1], p1.at[2]],
        [p2.at[0], p2.at[1]],
        [p3.at[1], p3.at[2]],
    ]

    def combine(chunk, carry):
        at = pl.ds(chunk * ROWS, ROWS)
        for j in range(2):
            value = weights[0] * sources[0][j][at]
            for l in range(1, 4):
                value = value + weights[l] * sources[l][j][at]
            field_ref[j, at] = value
        return carry

    lax.fori_loop(0, 256 // ROWS, combine, 0)


def finish(base, side, rows, p0, p1, p2, p3):
    return pl.pallas_call(
        finish_kernel,
        out_shape=(
            shape(2, 256, 256), shape(2, 8), shape(2, 7), shape(2, 6),
            jax.ShapeDtypeStruct((1,), jnp.int32),
        ),
        in_specs=[SMEM, SMEM] + [VMEM] * 5,
        out_specs=(VMEM,) * 4 + (SMEM,),
        compiler_params=PARAMS,
        name="finish",
    )(base, side, rows, p0, p1, p2, p3)


def gathered(row, axes, count):
    copies = jnp.broadcast_to(row[None], (count,) + row.shape)
    return lax.all_to_all(copies, axes, 0, 0, tiled=True).reshape(count, 128)


def shards(start_vectors, levels, energies):
    mean = jnp.mean(energies)
    scale = 1.05 * jnp.sqrt(6.0 + jnp.mean(jnp.square(energies - mean)))
    base = jnp.stack([mean, 1.0 / scale, scale])
    side = lax.axis_index("slab_3").astype(jnp.int32).reshape(1)

    sites_here = pl.pallas_call(
        onsite_kernel,
        out_shape=shape(1, 256, 256),
        in_specs=[SMEM, SMEM, VMEM],
        out_specs=VMEM,
        compiler_params=PARAMS,
        name="onsite",
    )(energies, base, levels)
    own = lax.all_to_all(start_vectors, "slab_3", 0, 1, tiled=True)[0]
    sites = lax.all_gather(sites_here, "slab_3", axis=0, tiled=True)
    upward = jnp.concatenate([own, sites[1:2]], axis=0)
    downward = jnp.concatenate([own, sites[0:1]], axis=0)
    low = from_behind(upward, SLAB, 2)
    high = from_behind(downward, SLAB, -2)
    p1, p2, onsite, sums0 = first_round(base, low, own, high, sites)
    low, high = from_behind(p2, SLAB, 2), from_behind(p2, SLAB, -2)
    p3, p4, sums1 = middle_round(base, low, p2, high, onsite, p1)
    low, high = from_behind(p4, SLAB, 2), from_behind(p4, SLAB, -2)
    p5, p6, sums2 = middle_round(base, low, p4, high, onsite, p3)
    low, high = from_behind(p6, SLAB, 2), from_behind(p6, SLAB, -2)
    sums3 = last_round(base, low, p6, high, onsite, p5)
    row = pack((sums0, sums1, sums2, sums3))
    rows = gathered(row, ("slab_0", "slab_1"), 32)
    rows = gathered(jnp.sum(rows, axis=0, keepdims=True), ("slab_2", "slab_3"), 16)
    field, diag, offd, moments, good = finish(base, side, rows, own, p1, p2, p3)

    def accept(field, diag, offd, moments, *_):
        out = lax.all_to_all(field[None], "slab_3", 1, 0, tiled=True)
        return (out, diag, offd, moments)

    def redo(field, diag, offd, moments, *inputs):
        return stepwise(*inputs)

    return lax.cond(
        good[0] == 1, accept, redo,
        field, diag, offd, moments, start_vectors, levels, energies,
    )


def solution(mesh):
    split = Mesh(mesh.devices.reshape(8, 4, 8, 2), SLAB)
    in_specs = (P(None, SLAB, None, None), P(SLAB, None, None), P())
    out_specs = (P(None, SLAB, None, None), P(), P(), P())
    return jax.shard_map(
        shards, mesh=split, in_specs=in_specs, out_specs=out_specs, check_vma=False
    )
```

time: 617 us -> 161 us (0.26)
  blocking collectives: 442 us -> 19.3 us
  other arithmetic: 22.6 us -> 1.43 us
  waiting for transfers between devices: 66.6 us -> 52 us
  Pallas kernels: 0 us -> 13.6 us
  local copies, waits for them, and re-layouts: 14.3 us -> 1.47 us
    psum x40 -> x0, blocking collectives: 442 us -> none  [one_axis_at_a_time(): value = lax.psum(value, axis)]
    all_to_all x0 -> x2, starting transfers between devices: none -> 23.4 us  [the longest x1 13 us: gathered(): return lax.all_to_all(copies, axes, 0, 0, tiled=True).reshape(count, 128)]
    ppermute x22 -> x8, starting transfers between devices: 68.7 us -> 46.7 us  [from_behind(): return lax.ppermute(block, axis, route)]
    ppermute x22 -> x8, waiting for transfers between devices: 66.6 us -> 45 us  [from_behind(): return lax.ppermute(block, axis, route)]
    all_to_all x0 -> x2, blocking collectives: none -> 17.1 us  [the longest x1 11.6 us: gathered(): return lax.all_to_all(copies, axes, 0, 0, tiled=True).reshape(count, 128)]
    reduce_sum x11 -> x3, other arithmetic: 17.1 us -> 1.22 us  [the longest x1 0.6 us: shards(): scale = 1.05 * jnp.sqrt(6.0 + jnp.mean(jnp.square(energies - mean)))]
    pallas_call x0 -> x7, Pallas kernels: none -> 13.6 us  [the longest x2 5.36 us: middle_round(): pl.pallas_call(functools.partial(round_kernel, False, False), out_shape=(...]
    slice x44 -> x1, local copies, waits for them, and re-layouts: 10.8 us -> 0.03 us  [shards(): downward = jnp.concatenate([own, sites[0:1]], axis=0)]
  transfers between devices with their start and end apart: 22 -> 10, of which waited for: 18 -> 9; matrix products, arithmetic and copies ran while one was open for 5% -> 1% of each run, Pallas kernels for 0% -> 1%
where the time goes in v1:
time: 161 us
  starting transfers between devices  70.1 us (44%)
  waiting for transfers between devices  52 us (32%)
  blocking collectives  19.3 us (12%)
  Pallas kernels  13.6 us (8%)
  between operations  2.85 us (2%)
    ppermute x8, starting transfers between devices, from_behind(): return lax.ppermute(block, axis, route)  46.7 us
    ppermute x8, waiting for transfers between devices, from_behind(): return lax.ppermute(block, axis, route)  45 us
    all_to_all x1, starting transfers between devices, gathered(): return lax.all_to_all(copies, axes, 0, 0, tiled=True).reshape(count, 128)  13 us
    all_to_all x1, blocking collectives, gathered(): return lax.all_to_all(copies, axes, 0, 0, tiled=True).reshape(count, 128)  11.6 us
    all_to_all x1, starting transfers between devices, shards(): own = lax.all_to_all(start_vectors, 'slab_3', 0, 1, tiled=True)[0]  10.5 us
    all_to_all x1, waiting for transfers between devices, gathered(): return lax.all_to_all(copies, axes, 0, 0, tiled=True).reshape(count, 128)  7.05 us
    all_to_all x1, blocking collectives, accept(): out = lax.all_to_all(field[None], 'slab_3', 1, 0, tiled=True)  5.49 us
    pallas_call x2, Pallas kernels, middle_round(): pl.pallas_call(functools.partial(round_kernel, False, False), out_shape=(...  5.36 us
  transfers between devices with their start and end apart: 10, of which 9 were waited for; matrix products, arithmetic and copies ran while one was open for 1% of the time, Pallas kernels for 1%

profile of v1, /device:TPU:1, one launch (start us, length us, event | category | flops | bytes accessed | tf_op | source)
XLA Modules:
  0.0 160.8 jit_solution(1433483978965322690)
XLA Ops:
  0.7 10.5 %all-to-all-start.1 = ((f32[2,1,256,256]{3,2,1,0:T(8,128)}), f32[2,1,256,256]{3,2,1,0:T(8,128)S(1)}, u32[]{:S(2)}, u32[]{:S(2)}) async-start(f32[2,1,256,256]{3,2,1,0:T(8,128)} %param.7), calls=%async_computation.1 | async-start | bytes 1048576 | tf_op jit(solution)/shard_map/all_to_all | solution.py:470
  12.4 0.6 multiply_reduce_fusion.12
  13.8 0.9 onsite.1
  14.7 2.2 %all_gather.3.refs_3_ = f32[2,256,256]{2,1,0:T(8,128)S(1)} all-gather(f32[1,256,256]{2,1,0:T(8,128)S(1)} %onsite.1), channel_id=1, replica_groups=mesh['slab_0'=8,'slab_1'=4,'slab_2'=8,'slab_3'=2] {'slab_3'}, dimensions={0}, use_global_device_ids=true | all-gather | bytes 786432 | tf_op jit(solution)/shard_map/all_gather | solution.py:471
  17.1 1.9 %collective-permute-start.8 = (f32[3,256,256]{2,1,0:T(8,128)S(1)}, f32[3,256,256]{2,1,0:T(8,128)S(1)}, u32[]{:S(2)}, u32[]{:S(2)}) collective-permute-start(f32[3,256,256]{2,1,0:T(8,128)S(1)} %get-tuple-element.247), channel_id=1, source_target_pairs={{510,0},{511,1},{0,2},{1,3},{2,4},{3,5},{4,6},{5,7},{6,8},{7,9},{8... | collective-permute-start | bytes 2359304 | tf_op jit(solution)/shard_map/ppermute | solution.py:25
  19.0 10.4 %collective-permute-start.9 = (f32[3,256,256]{2,1,0:T(8,128)S(1)}, f32[3,256,256]{2,1,0:T(8,128)S(1)}, u32[]{:S(2)}, u32[]{:S(2)}) collective-permute-start(f32[3,256,256]{2,1,0:T(8,128)S(1)} %get-tuple-element.246), channel_id=1, source_target_pairs={{2,0},{3,1},{4,2},{5,3},{6,4},{7,5},{8,6},{9,7},{10,8},{11,9},{12,... | collective-permute-start | bytes 2359304 | tf_op jit(solution)/shard_map/ppermute | solution.py:25
  29.4 15.8 %collective-permute-done.8.refs_0_ = f32[3,256,256]{2,1,0:T(8,128)S(1)} collective-permute-done((f32[3,256,256]{2,1,0:T(8,128)S(1)}, f32[3,256,256]{2,1,0:T(8,128)S(1)}, u32[]{:S(2)}, u32[]{:S(2)}) %collective-permute-start.8) | collective-permute-done | bytes 786464 | tf_op jit(solution)/shard_map/ppermute | solution.py:25
  45.3 0.9 collective-permute-done.9.refs_2_
  46.2 2.6 %first_round.1 = (f32[4,256,256]{2,1,0:T(8,128)S(1)}, f32[2,256,256]{2,1,0:T(8,128)S(1)}, f32[4,256,256]{2,1,0:T(8,128)S(1)}, f32[5,8,128]{2,1,0:T(8,128)S(1)}) custom-call(f32[3]{0:T(128)S(1)} %pad_maximum_fusion.2.base_ref, f32[3,256,256]{2,1,0:T(8,128)S(1)} %collective-permute-done.8.refs_0_, f32[2,256,256]{2,1,0:T(8,128)S(1)} %bitcast.51, ...), custom_call_target="tpu_custom_call" | custom-call | flops 4000000 | bytes 5000000 | tf_op jit(solution)/shard_map/first_round/pallas_call | solution.py:229
  48.8 1.9 %collective-permute-start.10 = (f32[2,256,256]{2,1,0:T(8,128)S(1)}, f32[2,256,256]{2,1,0:T(8,128)S(1)}, u32[]{:S(2)}, u32[]{:S(2)}) collective-permute-start(f32[2,256,256]{2,1,0:T(8,128)S(1)} %get-tuple-element.79.refs_1_.p2), channel_id=1, source_target_pairs={{510,0},{511,1},{0,2},{1,3},{2,4},{3,5},{4,6},{5,7},{6,8},{7,9},{8... | collective-permute-start | bytes 1572872 | tf_op jit(solution)/shard_map/ppermute | solution.py:25
  50.7 9.5 %collective-permute-start.11 = (f32[2,256,256]{2,1,0:T(8,128)S(1)}, f32[2,256,256]{2,1,0:T(8,128)S(1)}, u32[]{:S(2)}, u32[]{:S(2)}) collective-permute-start(f32[2,256,256]{2,1,0:T(8,128)S(1)} %get-tuple-element.79.refs_1_.p2), channel_id=1, source_target_pairs={{2,0},{3,1},{4,2},{5,3},{6,4},{7,5},{8,6},{9,7},{10,8},{11,9},{12,... | collective-permute-start | bytes 1572872 | tf_op jit(solution)/shard_map/ppermute | solution.py:25
  60.3 9.4 %collective-permute-done.10.refs_0_ = f32[2,256,256]{2,1,0:T(8,128)S(1)} collective-permute-done((f32[2,256,256]{2,1,0:T(8,128)S(1)}, f32[2,256,256]{2,1,0:T(8,128)S(1)}, u32[]{:S(2)}, u32[]{:S(2)}) %collective-permute-start.10) | collective-permute-done | bytes 524320 | tf_op jit(solution)/shard_map/ppermute | solution.py:25
  69.7 0.9 collective-permute-done.11.refs_2_
  70.6 2.7 %middle_round.2 = (f32[4,256,256]{2,1,0:T(8,128)S(1)}, f32[2,256,256]{2,1,0:T(8,128)S(1)}, f32[5,8,128]{2,1,0:T(8,128)S(1)}) custom-call(f32[3]{0:T(128)S(1)} %pad_maximum_fusion.2.base_ref, f32[2,256,256]{2,1,0:T(8,128)S(1)} %collective-permute-done.10.refs_0_, f32[2,256,256]{2,1,0:T(8,128)S(1)} %get-tuple-element.79.refs_1_.p2, ...), custom_call_target="tpu_custom_call" | custom-call | flops 4000000 | bytes 5000000 | tf_op jit(solution)/shard_map/middle_round/pallas_call | solution.py:243
  73.3 1.9 %collective-permute-start.12 = (f32[2,256,256]{2,1,0:T(8,128)S(1)}, f32[2,256,256]{2,1,0:T(8,128)S(1)}, u32[]{:S(2)}, u32[]{:S(2)}) collective-permute-start(f32[2,256,256]{2,1,0:T(8,128)S(1)} %get-tuple-element.83.refs_1_), channel_id=1, source_target_pairs={{510,0},{511,1},{0,2},{1,3},{2,4},{3,5},{4,6},{5,7},{6,8},{7,9},{8... | collective-permute-start | bytes 1572872 | tf_op jit(solution)/shard_map/ppermute | solution.py:25
  75.2 9.5 %collective-permute-start.13 = (f32[2,256,256]{2,1,0:T(8,128)S(1)}, f32[2,256,256]{2,1,0:T(8,128)S(1)}, u32[]{:S(2)}, u32[]{:S(2)}) collective-permute-start(f32[2,256,256]{2,1,0:T(8,128)S(1)} %get-tuple-element.83.refs_1_), channel_id=1, source_target_pairs={{2,0},{3,1},{4,2},{5,3},{6,4},{7,5},{8,6},{9,7},{10,8},{11,9},{12,... | collective-permute-start | bytes 1572872 | tf_op jit(solution)/shard_map/ppermute | solution.py:25
  84.7 8.5 %collective-permute-done.12.refs_0_ = f32[2,256,256]{2,1,0:T(8,128)S(1)} collective-permute-done((f32[2,256,256]{2,1,0:T(8,128)S(1)}, f32[2,256,256]{2,1,0:T(8,128)S(1)}, u32[]{:S(2)}, u32[]{:S(2)}) %collective-permute-start.12) | collective-permute-done | bytes 524320 | tf_op jit(solution)/shard_map/ppermute | solution.py:25
  93.2 0.9 collective-permute-done.13.refs_2_
  94.1 2.7 %middle_round.3 = (f32[4,256,256]{2,1,0:T(8,128)S(1)}, f32[2,256,256]{2,1,0:T(8,128)S(1)}, f32[5,8,128]{2,1,0:T(8,128)S(1)}) custom-call(f32[3]{0:T(128)S(1)} %pad_maximum_fusion.2.base_ref, f32[2,256,256]{2,1,0:T(8,128)S(1)} %collective-permute-done.12.refs_0_, f32[2,256,256]{2,1,0:T(8,128)S(1)} %get-tuple-element.83.refs_1_, ...), custom_call_target="tpu_custom_call" | custom-call | flops 4000000 | bytes 5000000 | tf_op jit(solution)/shard_map/middle_round/pallas_call | solution.py:243
  96.8 1.9 %collective-permute-start.14 = (f32[2,256,256]{2,1,0:T(8,128)S(1)}, f32[2,256,256]{2,1,0:T(8,128)S(1)}, u32[]{:S(2)}, u32[]{:S(2)}) collective-permute-start(f32[2,256,256]{2,1,0:T(8,128)S(1)} %get-tuple-element.86.refs_1_), channel_id=1, source_target_pairs={{510,0},{511,1},{0,2},{1,3},{2,4},{3,5},{4,6},{5,7},{6,8},{7,9},{8... | collective-permute-start | bytes 1572872 | tf_op jit(solution)/shard_map/ppermute | solution.py:25
  98.8 9.5 %collective-permute-start.15 = (f32[2,256,256]{2,1,0:T(8,128)S(1)}, f32[2,256,256]{2,1,0:T(8,128)S(1)}, u32[]{:S(2)}, u32[]{:S(2)}) collective-permute-start(f32[2,256,256]{2,1,0:T(8,128)S(1)} %get-tuple-element.86.refs_1_), channel_id=1, source_target_pairs={{2,0},{3,1},{4,2},{5,3},{6,4},{7,5},{8,6},{9,7},{10,8},{11,9},{12,... | collective-permute-start | bytes 1572872 | tf_op jit(solution)/shard_map/ppermute | solution.py:25
  108.3 7.7 %collective-permute-done.14.refs_0_ = f32[2,256,256]{2,1,0:T(8,128)S(1)} collective-permute-done((f32[2,256,256]{2,1,0:T(8,128)S(1)}, f32[2,256,256]{2,1,0:T(8,128)S(1)}, u32[]{:S(2)}, u32[]{:S(2)}) %collective-permute-start.14) | collective-permute-done | bytes 524320 | tf_op jit(solution)/shard_map/ppermute | solution.py:25
  116.0 0.9 collective-permute-done.15.refs_2_
  116.9 2.7 %last_round.1.d_ref = f32[5,8,128]{2,1,0:T(8,128)S(1)} custom-call(f32[3]{0:T(128)S(1)} %pad_maximum_fusion.2.base_ref, f32[2,256,256]{2,1,0:T(8,128)S(1)} %collective-permute-done.14.refs_0_, f32[2,256,256]{2,1,0:T(8,128)S(1)} %get-tuple-element.86.refs_1_, f32[2,256,256]{2,1,0:T(8,128)S(1)} %collective-permute-done.15.refs_2_, ...), custom_call_target="tpu_custom_call" | custom-call | flops 4000000 | bytes 5000000 | tf_op jit(solution)/shard_map/last_round/pallas_call | solution.py:255
  119.7 11.6 %all_to_all.30 = f32[32,1,128]{2,1,0:T(1,128)S(1)} all-to-all(f32[32,1,128]{2,1,0:T(1,128)S(1)} %broadcast_in_dim.32), channel_id=1, replica_groups=mesh['slab_0'=8,'slab_1'=4,'slab_2'=8,'slab_3'=2] {'slab_0','slab_1'}, dimensions={0} | all-to-all | bytes 32768 | tf_op jit(solution)/shard_map/all_to_all | solution.py:453
  131.3 0.6 broadcast_in_dim.33
  131.9 13.0 %all-to-all-start.3 = ((f32[16,1,128]{2,1,0:T(1,128)}), f32[16,1,128]{2,1,0:T(1,128)S(1)}, u32[]{:S(2)}, u32[]{:S(2)}) async-start(f32[16,1,128]{2,1,0:T(1,128)} %broadcast_in_dim.33), calls=%async_computation.3 | async-start | bytes 16384 | tf_op jit(solution)/shard_map/all_to_all | solution.py:453
  144.8 7.1 %all-to-all-done.3 = f32[16,1,128]{2,1,0:T(1,128)S(1)} async-done(((f32[16,1,128]{2,1,0:T(1,128)}), f32[16,1,128]{2,1,0:T(1,128)S(1)}, u32[]{:S(2)}, u32[]{:S(2)}) %all-to-all-start.3) | async-done | bytes 8224 | tf_op jit(solution)/shard_map/all_to_all | solution.py:453
  151.9 1.9 %finish.1 = (f32[2,256,256]{2,1,0:T(8,128)}, f32[2,8]{1,0:T(2,128)S(1)}, f32[2,7]{1,0:T(2,128)S(1)}, f32[2,6]{1,0:T(2,128)S(1)}, s32[1]{0:T(128)}) custom-call(f32[3]{0:T(128)S(1)} %pad_maximum_fusion.2.base_ref, s32[1]{0:T(128)} %bitcast.22.side_ref, f32[16,128]{1,0:T(8,128)S(1)} %bitcast.53, f32[2,256,256]{2,1,0:T(8,128)S(1)} %bitcast.52, ...), custom_call_target="tpu_custom_call" | custom-call | tf_op jit(solution)/shard_map/finish/pallas_call | solution.py:438
  154.5 5.5 %conditional.1 = (f32[2,1,256,256]{3,2,1,0:T(8,128)S(1)}, f32[2,6]{1,0:T(2,128)S(1)}, f32[2,8]{1,0:T(2,128)S(1)}, f32[2,7]{1,0:T(2,128)S(1)}) conditional(s32[]{:T(128)} %bitcast.27, (s32[1,256,256]{2,1,0:T(8,128)S(1)}, f32[16]{0:T(128)S(1)}, f32[2,1,256,256]{3,2,1,0:T(8,128)}) %tuple.110, (f32[2,256,256]{2,1,0:T(8,128)}, f32[2,8]{1,0:T(2,128)S(1)}, ...), branch_computations={%region_3.34_spmd, %region_34.35_spmd} | conditional | flops 13959351 | bytes 59787852 | solution.py:495
  154.5 5.5 %all_to_all.29 = f32[1,2,256,256]{3,2,0,1:T(8,128)S(1)} all-to-all(f32[1,2,256,256]{3,2,0,1:T(8,128)} %bitcast.62), channel_id=1, replica_groups=mesh['slab_0'=8,'slab_1'=4,'slab_2'=8,'slab_3'=2] {'slab_3'}, dimensions={1} | all-to-all | bytes 1048576 | tf_op jit(solution)/shard_map/cond/branch_1_fun/all_to_all | solution.py:489
  160.0 0.8 copy.122
  (22 shorter events, 1.0 us)
Async XLA Ops:
  0.6 10.5 %copy-start.5 = (f32[16]{0:T(128)S(1)}, f32[16]{0:T(128)}, u32[]{:S(2)}) copy-start(f32[16]{0:T(128)} %energies_ref.1) | copy-start | bytes 196
  0.6 13.1 %copy-start.2 = (s32[1,256,256]{2,1,0:T(8,128)S(1)}, s32[1,256,256]{2,1,0:T(8,128)}, u32[]{:S(2)}) copy-start(s32[1,256,256]{2,1,0:T(8,128)} %levels_ref.1) | copy-start | bytes 786436
  0.7 16.3 %all-to-all-start.1 = ((f32[2,1,256,256]{3,2,1,0:T(8,128)}), f32[2,1,256,256]{3,2,1,0:T(8,128)S(1)}, u32[]{:S(2)}, u32[]{:S(2)}) async-start(f32[2,1,256,256]{3,2,1,0:T(8,128)} %param.7), calls=%async_computation.1 | async-start | bytes 1048576 | tf_op jit(solution)/shard_map/all_to_all | solution.py:470
  17.1 28.2 %collective-permute-start.8 = (f32[3,256,256]{2,1,0:T(8,128)S(1)}, f32[3,256,256]{2,1,0:T(8,128)S(1)}, u32[]{:S(2)}, u32[]{:S(2)}) collective-permute-start(f32[3,256,256]{2,1,0:T(8,128)S(1)} %get-tuple-element.247), channel_id=1, source_target_pairs={{510,0},{511,1},{0,2},{1,3},{2,4},{3,5},{4,6},{5,7},{6,8},{7,9},{8... | collective-permute-start | bytes 2359304 | tf_op jit(solution)/shard_map/ppermute | solution.py:25
  19.0 27.2 %collective-permute-start.9 = (f32[3,256,256]{2,1,0:T(8,128)S(1)}, f32[3,256,256]{2,1,0:T(8,128)S(1)}, u32[]{:S(2)}, u32[]{:S(2)}) collective-permute-start(f32[3,256,256]{2,1,0:T(8,128)S(1)} %get-tuple-element.246), channel_id=1, source_target_pairs={{2,0},{3,1},{4,2},{5,3},{6,4},{7,5},{8,6},{9,7},{10,8},{11,9},{12,... | collective-permute-start | bytes 2359304 | tf_op jit(solution)/shard_map/ppermute | solution.py:25
  48.8 24.4 %copy-start = (f32[2,256,256]{2,1,0:T(8,128)}, f32[2,256,256]{2,1,0:T(8,128)S(1)}, u32[]{:S(2)}) copy-start(f32[2,256,256]{2,1,0:T(8,128)S(1)} %get-tuple-element.79.refs_1_.p2) | copy-start | bytes 1572868
  48.8 20.8 %collective-permute-start.10 = (f32[2,256,256]{2,1,0:T(8,128)S(1)}, f32[2,256,256]{2,1,0:T(8,128)S(1)}, u32[]{:S(2)}, u32[]{:S(2)}) collective-permute-start(f32[2,256,256]{2,1,0:T(8,128)S(1)} %get-tuple-element.79.refs_1_.p2), channel_id=1, source_target_pairs={{510,0},{511,1},{0,2},{1,3},{2,4},{3,5},{4,6},{5,7},{6,8},{7,9},{8... | collective-permute-start | bytes 1572872 | tf_op jit(solution)/shard_map/ppermute | solution.py:25
  50.7 19.8 %collective-permute-start.11 = (f32[2,256,256]{2,1,0:T(8,128)S(1)}, f32[2,256,256]{2,1,0:T(8,128)S(1)}, u32[]{:S(2)}, u32[]{:S(2)}) collective-permute-start(f32[2,256,256]{2,1,0:T(8,128)S(1)} %get-tuple-element.79.refs_1_.p2), channel_id=1, source_target_pairs={{2,0},{3,1},{4,2},{5,3},{6,4},{7,5},{8,6},{9,7},{10,8},{11,9},{12,... | collective-permute-start | bytes 1572872 | tf_op jit(solution)/shard_map/ppermute | solution.py:25
  73.3 20.0 %collective-permute-start.12 = (f32[2,256,256]{2,1,0:T(8,128)S(1)}, f32[2,256,256]{2,1,0:T(8,128)S(1)}, u32[]{:S(2)}, u32[]{:S(2)}) collective-permute-start(f32[2,256,256]{2,1,0:T(8,128)S(1)} %get-tuple-element.83.refs_1_), channel_id=1, source_target_pairs={{510,0},{511,1},{0,2},{1,3},{2,4},{3,5},{4,6},{5,7},{6,8},{7,9},{8... | collective-permute-start | bytes 1572872 | tf_op jit(solution)/shard_map/ppermute | solution.py:25
  75.2 19.0 %collective-permute-start.13 = (f32[2,256,256]{2,1,0:T(8,128)S(1)}, f32[2,256,256]{2,1,0:T(8,128)S(1)}, u32[]{:S(2)}, u32[]{:S(2)}) collective-permute-start(f32[2,256,256]{2,1,0:T(8,128)S(1)} %get-tuple-element.83.refs_1_), channel_id=1, source_target_pairs={{2,0},{3,1},{4,2},{5,3},{6,4},{7,5},{8,6},{9,7},{10,8},{11,9},{12,... | collective-permute-start | bytes 1572872 | tf_op jit(solution)/shard_map/ppermute | solution.py:25
  96.8 19.1 %collective-permute-start.14 = (f32[2,256,256]{2,1,0:T(8,128)S(1)}, f32[2,256,256]{2,1,0:T(8,128)S(1)}, u32[]{:S(2)}, u32[]{:S(2)}) collective-permute-start(f32[2,256,256]{2,1,0:T(8,128)S(1)} %get-tuple-element.86.refs_1_), channel_id=1, source_target_pairs={{510,0},{511,1},{0,2},{1,3},{2,4},{3,5},{4,6},{5,7},{6,8},{7,9},{8... | collective-permute-start | bytes 1572872 | tf_op jit(solution)/shard_map/ppermute | solution.py:25
  98.8 18.1 %collective-permute-start.15 = (f32[2,256,256]{2,1,0:T(8,128)S(1)}, f32[2,256,256]{2,1,0:T(8,128)S(1)}, u32[]{:S(2)}, u32[]{:S(2)}) collective-permute-start(f32[2,256,256]{2,1,0:T(8,128)S(1)} %get-tuple-element.86.refs_1_), channel_id=1, source_target_pairs={{2,0},{3,1},{4,2},{5,3},{6,4},{7,5},{8,6},{9,7},{10,8},{11,9},{12,... | collective-permute-start | bytes 1572872 | tf_op jit(solution)/shard_map/ppermute | solution.py:25
  116.9 35.0 %copy-start.1 = (f32[2,256,256]{2,1,0:T(8,128)S(1)}, f32[2,256,256]{2,1,0:T(8,128)}, u32[]{:S(2)}) copy-start(f32[2,256,256]{2,1,0:T(8,128)} %copy-done) | copy-start | bytes 1572868
  131.9 20.0 %all-to-all-start.3 = ((f32[16,1,128]{2,1,0:T(1,128)}), f32[16,1,128]{2,1,0:T(1,128)S(1)}, u32[]{:S(2)}, u32[]{:S(2)}) async-start(f32[16,1,128]{2,1,0:T(1,128)} %broadcast_in_dim.33), calls=%async_computation.3 | async-start | bytes 16384 | tf_op jit(solution)/shard_map/all_to_all | solution.py:453
  160.0 0.8 copy-start.6
  160.0 0.8 copy-start.7
  160.0 0.8 copy-start.8

commit v2 on v1

--- a/solution.py
+++ b/solution.py
@@ -13,7 +13,7 @@
 ROWS = 32
 NUDGE = 1e-3
 ROUNDING = 2e-7
-TOLERANCE = 2e-5
+TOLERANCE = 1e-4
 VMEM = pl.BlockSpec(memory_space=pltpu.VMEM)
 SMEM = pl.BlockSpec(memory_space=pltpu.SMEM)
 PARAMS = pltpu.CompilerParams(vmem_limit_bytes=24 * 1024 * 1024)

time: 161 us -> 161 us (level)
  no operation moved by 1% of the time
where the time goes in v2:
time: 161 us
  starting transfers between devices  70.1 us (44%)
  waiting for transfers between devices  52 us (32%)
  blocking collectives  19.3 us (12%)
  Pallas kernels  13.6 us (8%)
  between operations  2.85 us (2%)
    ppermute x8, starting transfers between devices, from_behind(): return lax.ppermute(block, axis, route)  46.7 us
    ppermute x8, waiting for transfers between devices, from_behind(): return lax.ppermute(block, axis, route)  45 us
    all_to_all x1, starting transfers between devices, gathered(): return lax.all_to_all(copies, axes, 0, 0, tiled=True).reshape(count, 128)  13 us
    all_to_all x1, blocking collectives, gathered(): return lax.all_to_all(copies, axes, 0, 0, tiled=True).reshape(count, 128)  11.6 us
    all_to_all x1, starting transfers between devices, shards(): own = lax.all_to_all(start_vectors, 'slab_3', 0, 1, tiled=True)[0]  10.5 us
    all_to_all x1, waiting for transfers between devices, gathered(): return lax.all_to_all(copies, axes, 0, 0, tiled=True).reshape(count, 128)  7.05 us
    all_to_all x1, blocking collectives, accept(): out = lax.all_to_all(field[None], 'slab_3', 1, 0, tiled=True)  5.49 us
    pallas_call x2, Pallas kernels, middle_round(): pl.pallas_call(functools.partial(round_kernel, False, False), out_shape=(...  5.36 us
  transfers between devices with their start and end apart: 10, of which 9 were waited for; matrix products, arithmetic and copies ran while one was open for 1% of the time, Pallas kernels for 1%

profile of v2, /device:TPU:1, one launch (start us, length us, event | category | flops | bytes accessed | tf_op | source)
XLA Modules:
  0.0 160.8 jit_solution(4544733843837637347)
XLA Ops:
  0.7 10.5 %all-to-all-start.1 = ((f32[2,1,256,256]{3,2,1,0:T(8,128)}), f32[2,1,256,256]{3,2,1,0:T(8,128)S(1)}, u32[]{:S(2)}, u32[]{:S(2)}) async-start(f32[2,1,256,256]{3,2,1,0:T(8,128)} %param.7), calls=%async_computation.1 | async-start | bytes 1048576 | tf_op jit(solution)/shard_map/all_to_all | solution.py:470
  12.4 0.6 multiply_reduce_fusion.12
  13.8 0.9 onsite.1
  14.7 2.2 %all_gather.3.refs_3_ = f32[2,256,256]{2,1,0:T(8,128)S(1)} all-gather(f32[1,256,256]{2,1,0:T(8,128)S(1)} %onsite.1), channel_id=1, replica_groups=mesh['slab_0'=8,'slab_1'=4,'slab_2'=8,'slab_3'=2] {'slab_3'}, dimensions={0}, use_global_device_ids=true | all-gather | bytes 786432 | tf_op jit(solution)/shard_map/all_gather | solution.py:471
  17.1 1.9 %collective-permute-start.8 = (f32[3,256,256]{2,1,0:T(8,128)S(1)}, f32[3,256,256]{2,1,0:T(8,128)S(1)}, u32[]{:S(2)}, u32[]{:S(2)}) collective-permute-start(f32[3,256,256]{2,1,0:T(8,128)S(1)} %get-tuple-element.247), channel_id=1, source_target_pairs={{510,0},{511,1},{0,2},{1,3},{2,4},{3,5},{4,6},{5,7},{6,8},{7,9},{8... | collective-permute-start | bytes 2359304 | tf_op jit(solution)/shard_map/ppermute | solution.py:25
  19.0 10.4 %collective-permute-start.9 = (f32[3,256,256]{2,1,0:T(8,128)S(1)}, f32[3,256,256]{2,1,0:T(8,128)S(1)}, u32[]{:S(2)}, u32[]{:S(2)}) collective-permute-start(f32[3,256,256]{2,1,0:T(8,128)S(1)} %get-tuple-element.246), channel_id=1, source_target_pairs={{2,0},{3,1},{4,2},{5,3},{6,4},{7,5},{8,6},{9,7},{10,8},{11,9},{12,... | collective-permute-start | bytes 2359304 | tf_op jit(solution)/shard_map/ppermute | solution.py:25
  29.4 15.8 %collective-permute-done.8.refs_0_ = f32[3,256,256]{2,1,0:T(8,128)S(1)} collective-permute-done((f32[3,256,256]{2,1,0:T(8,128)S(1)}, f32[3,256,256]{2,1,0:T(8,128)S(1)}, u32[]{:S(2)}, u32[]{:S(2)}) %collective-permute-start.8) | collective-permute-done | bytes 786464 | tf_op jit(solution)/shard_map/ppermute | solution.py:25
  45.3 0.9 collective-permute-done.9.refs_2_
  46.2 2.6 %first_round.1 = (f32[4,256,256]{2,1,0:T(8,128)S(1)}, f32[2,256,256]{2,1,0:T(8,128)S(1)}, f32[4,256,256]{2,1,0:T(8,128)S(1)}, f32[5,8,128]{2,1,0:T(8,128)S(1)}) custom-call(f32[3]{0:T(128)S(1)} %pad_maximum_fusion.2.base_ref, f32[3,256,256]{2,1,0:T(8,128)S(1)} %collective-permute-done.8.refs_0_, f32[2,256,256]{2,1,0:T(8,128)S(1)} %bitcast.51, ...), custom_call_target="tpu_custom_call" | custom-call | flops 4000000 | bytes 5000000 | tf_op jit(solution)/shard_map/first_round/pallas_call | solution.py:229
  48.8 1.9 %collective-permute-start.10 = (f32[2,256,256]{2,1,0:T(8,128)S(1)}, f32[2,256,256]{2,1,0:T(8,128)S(1)}, u32[]{:S(2)}, u32[]{:S(2)}) collective-permute-start(f32[2,256,256]{2,1,0:T(8,128)S(1)} %get-tuple-element.79.refs_1_.p2), channel_id=1, source_target_pairs={{510,0},{511,1},{0,2},{1,3},{2,4},{3,5},{4,6},{5,7},{6,8},{7,9},{8... | collective-permute-start | bytes 1572872 | tf_op jit(solution)/shard_map/ppermute | solution.py:25
  50.7 9.5 %collective-permute-start.11 = (f32[2,256,256]{2,1,0:T(8,128)S(1)}, f32[2,256,256]{2,1,0:T(8,128)S(1)}, u32[]{:S(2)}, u32[]{:S(2)}) collective-permute-start(f32[2,256,256]{2,1,0:T(8,128)S(1)} %get-tuple-element.79.refs_1_.p2), channel_id=1, source_target_pairs={{2,0},{3,1},{4,2},{5,3},{6,4},{7,5},{8,6},{9,7},{10,8},{11,9},{12,... | collective-permute-start | bytes 1572872 | tf_op jit(solution)/shard_map/ppermute | solution.py:25
  60.3 9.4 %collective-permute-done.10.refs_0_ = f32[2,256,256]{2,1,0:T(8,128)S(1)} collective-permute-done((f32[2,256,256]{2,1,0:T(8,128)S(1)}, f32[2,256,256]{2,1,0:T(8,128)S(1)}, u32[]{:S(2)}, u32[]{:S(2)}) %collective-permute-start.10) | collective-permute-done | bytes 524320 | tf_op jit(solution)/shard_map/ppermute | solution.py:25
  69.7 0.9 collective-permute-done.11.refs_2_
  70.6 2.7 %middle_round.2 = (f32[4,256,256]{2,1,0:T(8,128)S(1)}, f32[2,256,256]{2,1,0:T(8,128)S(1)}, f32[5,8,128]{2,1,0:T(8,128)S(1)}) custom-call(f32[3]{0:T(128)S(1)} %pad_maximum_fusion.2.base_ref, f32[2,256,256]{2,1,0:T(8,128)S(1)} %collective-permute-done.10.refs_0_, f32[2,256,256]{2,1,0:T(8,128)S(1)} %get-tuple-element.79.refs_1_.p2, ...), custom_call_target="tpu_custom_call" | custom-call | flops 4000000 | bytes 5000000 | tf_op jit(solution)/shard_map/middle_round/pallas_call | solution.py:243
  73.3 1.9 %collective-permute-start.12 = (f32[2,256,256]{2,1,0:T(8,128)S(1)}, f32[2,256,256]{2,1,0:T(8,128)S(1)}, u32[]{:S(2)}, u32[]{:S(2)}) collective-permute-start(f32[2,256,256]{2,1,0:T(8,128)S(1)} %get-tuple-element.83.refs_1_), channel_id=1, source_target_pairs={{510,0},{511,1},{0,2},{1,3},{2,4},{3,5},{4,6},{5,7},{6,8},{7,9},{8... | collective-permute-start | bytes 1572872 | tf_op jit(solution)/shard_map/ppermute | solution.py:25
  75.2 9.5 %collective-permute-start.13 = (f32[2,256,256]{2,1,0:T(8,128)S(1)}, f32[2,256,256]{2,1,0:T(8,128)S(1)}, u32[]{:S(2)}, u32[]{:S(2)}) collective-permute-start(f32[2,256,256]{2,1,0:T(8,128)S(1)} %get-tuple-element.83.refs_1_), channel_id=1, source_target_pairs={{2,0},{3,1},{4,2},{5,3},{6,4},{7,5},{8,6},{9,7},{10,8},{11,9},{12,... | collective-permute-start | bytes 1572872 | tf_op jit(solution)/shard_map/ppermute | solution.py:25
  84.7 8.5 %collective-permute-done.12.refs_0_ = f32[2,256,256]{2,1,0:T(8,128)S(1)} collective-permute-done((f32[2,256,256]{2,1,0:T(8,128)S(1)}, f32[2,256,256]{2,1,0:T(8,128)S(1)}, u32[]{:S(2)}, u32[]{:S(2)}) %collective-permute-start.12) | collective-permute-done | bytes 524320 | tf_op jit(solution)/shard_map/ppermute | solution.py:25
  93.2 0.9 collective-permute-done.13.refs_2_
  94.1 2.7 %middle_round.3 = (f32[4,256,256]{2,1,0:T(8,128)S(1)}, f32[2,256,256]{2,1,0:T(8,128)S(1)}, f32[5,8,128]{2,1,0:T(8,128)S(1)}) custom-call(f32[3]{0:T(128)S(1)} %pad_maximum_fusion.2.base_ref, f32[2,256,256]{2,1,0:T(8,128)S(1)} %collective-permute-done.12.refs_0_, f32[2,256,256]{2,1,0:T(8,128)S(1)} %get-tuple-element.83.refs_1_, ...), custom_call_target="tpu_custom_call" | custom-call | flops 4000000 | bytes 5000000 | tf_op jit(solution)/shard_map/middle_round/pallas_call | solution.py:243
  96.8 1.9 %collective-permute-start.14 = (f32[2,256,256]{2,1,0:T(8,128)S(1)}, f32[2,256,256]{2,1,0:T(8,128)S(1)}, u32[]{:S(2)}, u32[]{:S(2)}) collective-permute-start(f32[2,256,256]{2,1,0:T(8,128)S(1)} %get-tuple-element.86.refs_1_), channel_id=1, source_target_pairs={{510,0},{511,1},{0,2},{1,3},{2,4},{3,5},{4,6},{5,7},{6,8},{7,9},{8... | collective-permute-start | bytes 1572872 | tf_op jit(solution)/shard_map/ppermute | solution.py:25
  98.8 9.5 %collective-permute-start.15 = (f32[2,256,256]{2,1,0:T(8,128)S(1)}, f32[2,256,256]{2,1,0:T(8,128)S(1)}, u32[]{:S(2)}, u32[]{:S(2)}) collective-permute-start(f32[2,256,256]{2,1,0:T(8,128)S(1)} %get-tuple-element.86.refs_1_), channel_id=1, source_target_pairs={{2,0},{3,1},{4,2},{5,3},{6,4},{7,5},{8,6},{9,7},{10,8},{11,9},{12,... | collective-permute-start | bytes 1572872 | tf_op jit(solution)/shard_map/ppermute | solution.py:25
  108.3 7.7 %collective-permute-done.14.refs_0_ = f32[2,256,256]{2,1,0:T(8,128)S(1)} collective-permute-done((f32[2,256,256]{2,1,0:T(8,128)S(1)}, f32[2,256,256]{2,1,0:T(8,128)S(1)}, u32[]{:S(2)}, u32[]{:S(2)}) %collective-permute-start.14) | collective-permute-done | bytes 524320 | tf_op jit(solution)/shard_map/ppermute | solution.py:25
  116.0 0.9 collective-permute-done.15.refs_2_
  116.9 2.7 %last_round.1.d_ref = f32[5,8,128]{2,1,0:T(8,128)S(1)} custom-call(f32[3]{0:T(128)S(1)} %pad_maximum_fusion.2.base_ref, f32[2,256,256]{2,1,0:T(8,128)S(1)} %collective-permute-done.14.refs_0_, f32[2,256,256]{2,1,0:T(8,128)S(1)} %get-tuple-element.86.refs_1_, f32[2,256,256]{2,1,0:T(8,128)S(1)} %collective-permute-done.15.refs_2_, ...), custom_call_target="tpu_custom_call" | custom-call | flops 4000000 | bytes 5000000 | tf_op jit(solution)/shard_map/last_round/pallas_call | solution.py:255
  119.7 11.6 %all_to_all.30 = f32[32,1,128]{2,1,0:T(1,128)S(1)} all-to-all(f32[32,1,128]{2,1,0:T(1,128)S(1)} %broadcast_in_dim.32), channel_id=1, replica_groups=mesh['slab_0'=8,'slab_1'=4,'slab_2'=8,'slab_3'=2] {'slab_0','slab_1'}, dimensions={0} | all-to-all | bytes 32768 | tf_op jit(solution)/shard_map/all_to_all | solution.py:453
  131.3 0.6 broadcast_in_dim.33
  131.9 13.0 %all-to-all-start.3 = ((f32[16,1,128]{2,1,0:T(1,128)}), f32[16,1,128]{2,1,0:T(1,128)S(1)}, u32[]{:S(2)}, u32[]{:S(2)}) async-start(f32[16,1,128]{2,1,0:T(1,128)} %broadcast_in_dim.33), calls=%async_computation.3 | async-start | bytes 16384 | tf_op jit(solution)/shard_map/all_to_all | solution.py:453
  144.8 7.1 %all-to-all-done.3 = f32[16,1,128]{2,1,0:T(1,128)S(1)} async-done(((f32[16,1,128]{2,1,0:T(1,128)}), f32[16,1,128]{2,1,0:T(1,128)S(1)}, u32[]{:S(2)}, u32[]{:S(2)}) %all-to-all-start.3) | async-done | bytes 8224 | tf_op jit(solution)/shard_map/all_to_all | solution.py:453
  151.9 1.9 %finish.1 = (f32[2,256,256]{2,1,0:T(8,128)}, f32[2,8]{1,0:T(2,128)S(1)}, f32[2,7]{1,0:T(2,128)S(1)}, f32[2,6]{1,0:T(2,128)S(1)}, s32[1]{0:T(128)}) custom-call(f32[3]{0:T(128)S(1)} %pad_maximum_fusion.2.base_ref, s32[1]{0:T(128)} %bitcast.22.side_ref, f32[16,128]{1,0:T(8,128)S(1)} %bitcast.53, f32[2,256,256]{2,1,0:T(8,128)S(1)} %bitcast.52, ...), custom_call_target="tpu_custom_call" | custom-call | tf_op jit(solution)/shard_map/finish/pallas_call | solution.py:438
  154.5 5.5 %conditional.1 = (f32[2,1,256,256]{3,2,1,0:T(8,128)S(1)}, f32[2,6]{1,0:T(2,128)S(1)}, f32[2,8]{1,0:T(2,128)S(1)}, f32[2,7]{1,0:T(2,128)S(1)}) conditional(s32[]{:T(128)} %bitcast.27, (s32[1,256,256]{2,1,0:T(8,128)S(1)}, f32[16]{0:T(128)S(1)}, f32[2,1,256,256]{3,2,1,0:T(8,128)}) %tuple.110, (f32[2,256,256]{2,1,0:T(8,128)}, f32[2,8]{1,0:T(2,128)S(1)}, ...), branch_computations={%region_3.34_spmd, %region_34.35_spmd} | conditional | flops 13959351 | bytes 59787852 | solution.py:495
  154.5 5.5 %all_to_all.29 = f32[1,2,256,256]{3,2,0,1:T(8,128)S(1)} all-to-all(f32[1,2,256,256]{3,2,0,1:T(8,128)} %bitcast.62), channel_id=1, replica_groups=mesh['slab_0'=8,'slab_1'=4,'slab_2'=8,'slab_3'=2] {'slab_3'}, dimensions={1} | all-to-all | bytes 1048576 | tf_op jit(solution)/shard_map/cond/branch_1_fun/all_to_all | solution.py:489
  160.0 0.8 copy.122
  (22 shorter events, 1.0 us)
Async XLA Ops:
  0.6 10.5 %copy-start.5 = (f32[16]{0:T(128)S(1)}, f32[16]{0:T(128)}, u32[]{:S(2)}) copy-start(f32[16]{0:T(128)} %energies_ref.1) | copy-start | bytes 196
  0.6 13.1 %copy-start.2 = (s32[1,256,256]{2,1,0:T(8,128)S(1)}, s32[1,256,256]{2,1,0:T(8,128)}, u32[]{:S(2)}) copy-start(s32[1,256,256]{2,1,0:T(8,128)} %levels_ref.1) | copy-start | bytes 786436
  0.7 16.3 %all-to-all-start.1 = ((f32[2,1,256,256]{3,2,1,0:T(8,128)}), f32[2,1,256,256]{3,2,1,0:T(8,128)S(1)}, u32[]{:S(2)}, u32[]{:S(2)}) async-start(f32[2,1,256,256]{3,2,1,0:T(8,128)} %param.7), calls=%async_computation.1 | async-start | bytes 1048576 | tf_op jit(solution)/shard_map/all_to_all | solution.py:470
  17.1 28.2 %collective-permute-start.8 = (f32[3,256,256]{2,1,0:T(8,128)S(1)}, f32[3,256,256]{2,1,0:T(8,128)S(1)}, u32[]{:S(2)}, u32[]{:S(2)}) collective-permute-start(f32[3,256,256]{2,1,0:T(8,128)S(1)} %get-tuple-element.247), channel_id=1, source_target_pairs={{510,0},{511,1},{0,2},{1,3},{2,4},{3,5},{4,6},{5,7},{6,8},{7,9},{8... | collective-permute-start | bytes 2359304 | tf_op jit(solution)/shard_map/ppermute | solution.py:25
  19.0 27.2 %collective-permute-start.9 = (f32[3,256,256]{2,1,0:T(8,128)S(1)}, f32[3,256,256]{2,1,0:T(8,128)S(1)}, u32[]{:S(2)}, u32[]{:S(2)}) collective-permute-start(f32[3,256,256]{2,1,0:T(8,128)S(1)} %get-tuple-element.246), channel_id=1, source_target_pairs={{2,0},{3,1},{4,2},{5,3},{6,4},{7,5},{8,6},{9,7},{10,8},{11,9},{12,... | collective-permute-start | bytes 2359304 | tf_op jit(solution)/shard_map/ppermute | solution.py:25
  48.8 24.4 %copy-start = (f32[2,256,256]{2,1,0:T(8,128)}, f32[2,256,256]{2,1,0:T(8,128)S(1)}, u32[]{:S(2)}) copy-start(f32[2,256,256]{2,1,0:T(8,128)S(1)} %get-tuple-element.79.refs_1_.p2) | copy-start | bytes 1572868
  48.8 20.8 %collective-permute-start.10 = (f32[2,256,256]{2,1,0:T(8,128)S(1)}, f32[2,256,256]{2,1,0:T(8,128)S(1)}, u32[]{:S(2)}, u32[]{:S(2)}) collective-permute-start(f32[2,256,256]{2,1,0:T(8,128)S(1)} %get-tuple-element.79.refs_1_.p2), channel_id=1, source_target_pairs={{510,0},{511,1},{0,2},{1,3},{2,4},{3,5},{4,6},{5,7},{6,8},{7,9},{8... | collective-permute-start | bytes 1572872 | tf_op jit(solution)/shard_map/ppermute | solution.py:25
  50.7 19.8 %collective-permute-start.11 = (f32[2,256,256]{2,1,0:T(8,128)S(1)}, f32[2,256,256]{2,1,0:T(8,128)S(1)}, u32[]{:S(2)}, u32[]{:S(2)}) collective-permute-start(f32[2,256,256]{2,1,0:T(8,128)S(1)} %get-tuple-element.79.refs_1_.p2), channel_id=1, source_target_pairs={{2,0},{3,1},{4,2},{5,3},{6,4},{7,5},{8,6},{9,7},{10,8},{11,9},{12,... | collective-permute-start | bytes 1572872 | tf_op jit(solution)/shard_map/ppermute | solution.py:25
  73.3 20.0 %collective-permute-start.12 = (f32[2,256,256]{2,1,0:T(8,128)S(1)}, f32[2,256,256]{2,1,0:T(8,128)S(1)}, u32[]{:S(2)}, u32[]{:S(2)}) collective-permute-start(f32[2,256,256]{2,1,0:T(8,128)S(1)} %get-tuple-element.83.refs_1_), channel_id=1, source_target_pairs={{510,0},{511,1},{0,2},{1,3},{2,4},{3,5},{4,6},{5,7},{6,8},{7,9},{8... | collective-permute-start | bytes 1572872 | tf_op jit(solution)/shard_map/ppermute | solution.py:25
  75.2 19.0 %collective-permute-start.13 = (f32[2,256,256]{2,1,0:T(8,128)S(1)}, f32[2,256,256]{2,1,0:T(8,128)S(1)}, u32[]{:S(2)}, u32[]{:S(2)}) collective-permute-start(f32[2,256,256]{2,1,0:T(8,128)S(1)} %get-tuple-element.83.refs_1_), channel_id=1, source_target_pairs={{2,0},{3,1},{4,2},{5,3},{6,4},{7,5},{8,6},{9,7},{10,8},{11,9},{12,... | collective-permute-start | bytes 1572872 | tf_op jit(solution)/shard_map/ppermute | solution.py:25
  96.8 19.1 %collective-permute-start.14 = (f32[2,256,256]{2,1,0:T(8,128)S(1)}, f32[2,256,256]{2,1,0:T(8,128)S(1)}, u32[]{:S(2)}, u32[]{:S(2)}) collective-permute-start(f32[2,256,256]{2,1,0:T(8,128)S(1)} %get-tuple-element.86.refs_1_), channel_id=1, source_target_pairs={{510,0},{511,1},{0,2},{1,3},{2,4},{3,5},{4,6},{5,7},{6,8},{7,9},{8... | collective-permute-start | bytes 1572872 | tf_op jit(solution)/shard_map/ppermute | solution.py:25
  98.8 18.1 %collective-permute-start.15 = (f32[2,256,256]{2,1,0:T(8,128)S(1)}, f32[2,256,256]{2,1,0:T(8,128)S(1)}, u32[]{:S(2)}, u32[]{:S(2)}) collective-permute-start(f32[2,256,256]{2,1,0:T(8,128)S(1)} %get-tuple-element.86.refs_1_), channel_id=1, source_target_pairs={{2,0},{3,1},{4,2},{5,3},{6,4},{7,5},{8,6},{9,7},{10,8},{11,9},{12,... | collective-permute-start | bytes 1572872 | tf_op jit(solution)/shard_map/ppermute | solution.py:25
  116.9 35.0 %copy-start.1 = (f32[2,256,256]{2,1,0:T(8,128)S(1)}, f32[2,256,256]{2,1,0:T(8,128)}, u32[]{:S(2)}) copy-start(f32[2,256,256]{2,1,0:T(8,128)} %copy-done) | copy-start | bytes 1572868
  131.9 20.0 %all-to-all-start.3 = ((f32[16,1,128]{2,1,0:T(1,128)}), f32[16,1,128]{2,1,0:T(1,128)S(1)}, u32[]{:S(2)}, u32[]{:S(2)}) async-start(f32[16,1,128]{2,1,0:T(1,128)} %broadcast_in_dim.33), calls=%async_computation.3 | async-start | bytes 16384 | tf_op jit(solution)/shard_map/all_to_all | solution.py:453
  160.0 0.8 copy-start.6
  160.0 0.8 copy-start.7
  160.0 0.8 copy-start.8

commit v3 on v2

v3 whole, which is shorter than its diff:
```python
import functools

import jax
import jax.numpy as jnp
from jax import lax
from jax.experimental import pallas as pl
from jax.experimental.pallas import tpu as pltpu
from jax.sharding import Mesh
from jax.sharding import PartitionSpec as P

LANCZOS = 8
SLAB = ("slab_0", "slab_1", "slab_2", "slab_3")
STAGES = (("slab_1", "slab_2"), ("slab_0", "slab_3"))
ROWS = 32
NUDGE = 1e-3
ROUNDING = 2e-7
TOLERANCE = 1e-4
VMEM = pl.BlockSpec(memory_space=pltpu.VMEM)
SMEM = pl.BlockSpec(memory_space=pltpu.SMEM)
PARAMS = pltpu.CompilerParams(vmem_limit_bytes=24 * 1024 * 1024)


def from_behind(block, axis, distance):
    devices = range(lax.axis_size(axis))
    route = [((i - distance) % len(devices), i) for i in devices]
    return lax.ppermute(block, axis, route)


def one_axis_at_a_time(value, axes):
    for axis in axes:
        value = lax.psum(value, axis)
    return value


def inner(first, second):
    return jnp.sum(first * second, axis=(1, 2, 3))


def expand(values):
    return values[:, None, None, None]


def hamiltonian(field, onsite):
    below = from_behind(field, SLAB, 1)
    above = from_behind(field, SLAB, -1)
    beside = jnp.roll(field, 1, 2) + jnp.roll(field, -1, 2)
    beside = beside + jnp.roll(field, 1, 3) + jnp.roll(field, -1, 3)
    return onsite[None] * field - (beside + below + above)


def stepwise(start_vectors, levels, energies):
    level_ids = lax.broadcasted_iota(jnp.int32, (energies.shape[0], 1, 1, 1), 0)
    onsite = jnp.sum(
        jnp.where(levels[None] == level_ids, energies[:, None, None, None], 0.0), axis=0
    )
    vec_count = start_vectors.shape[0]
    norm0 = one_axis_at_a_time(inner(start_vectors, start_vectors), SLAB)

    def lanczos(state, step):
        vector, previous, beta_prev = state
        work = hamiltonian(vector, onsite) - expand(beta_prev) * previous
        alpha = one_axis_at_a_time(inner(vector, work), SLAB)
        work = work - expand(alpha) * vector
        beta = jnp.sqrt(one_axis_at_a_time(inner(work, work), SLAB))
        return (work / expand(beta), vector, beta), (alpha, beta)

    vector = start_vectors / expand(jnp.sqrt(norm0))
    _, (alphas, betas) = lax.scan(
        lanczos,
        (vector, jnp.zeros_like(vector), jnp.zeros((vec_count,), jnp.float32)),
        None,
        length=LANCZOS,
    )
    diag = alphas.T
    offd = betas[: LANCZOS - 1].T
    zero_col = jnp.zeros((vec_count, 1), jnp.float32)
    left = jnp.concatenate([zero_col, offd], axis=1)
    right = jnp.concatenate([offd, zero_col], axis=1)
    emin = jnp.min(diag - left - right, axis=1)
    emax = jnp.max(diag + left + right, axis=1)
    center = expand((emax + emin) * 0.5)
    half = expand(0.55 * (emax - emin))

    def scaled(field):
        return (hamiltonian(field, onsite) - center * field) / half

    term1 = scaled(start_vectors)
    term2 = 2.0 * scaled(term1) - start_vectors
    term3 = 2.0 * scaled(term2) - term1
    local = jnp.stack(
        [
            inner(start_vectors, term1),
            inner(start_vectors, term2),
            inner(start_vectors, term3),
            inner(term2, term2),
            inner(term3, term2),
            inner(term3, term3),
        ],
        axis=0,
    )
    sums = one_axis_at_a_time(local, SLAB)
    moments = (
        jnp.stack(
            [
                sums[0],
                sums[1],
                sums[2],
                2.0 * sums[3] - norm0,
                2.0 * sums[4] - sums[0],
                2.0 * sums[5] - norm0,
            ],
            axis=1,
        )
        / norm0[:, None]
    )
    return (term3, diag, offd, moments)


def shape(*dims):
    return jax.ShapeDtypeStruct(dims, jnp.float32)


PLANES = shape(2, 256, 256)
CHUNKS = 256 // ROWS
PAIR_COST = pl.CostEstimate(flops=4_000_000, bytes_accessed=4_000_000, transcendentals=0)


def call(kernel, out_shape, in_specs, name, scratch=()):
    return pl.pallas_call(
        kernel,
        out_shape=out_shape,
        in_specs=in_specs,
        out_specs=jax.tree.map(
            lambda leaf: SMEM if leaf.dtype == jnp.int32 else VMEM, out_shape
        ),
        scratch_shapes=scratch,
        compiler_params=PARAMS,
        cost_estimate=PAIR_COST,
        name=name,
    )


def onsite_kernel(energies_ref, levels_ref, out_ref, base_ref):
    count = energies_ref.shape[0]
    row = jnp.zeros((1, 256), jnp.float32)
    values = [row + energies_ref[index] for index in range(count)]
    mean = functools.reduce(jnp.add, values) * (1.0 / count)
    spread = functools.reduce(jnp.add, [jnp.square(v - mean) for v in values])
    scale = 1.05 * jnp.sqrt(6.0 + spread * (1.0 / count))
    inverse = 1.0 / scale
    base_ref[0:1] = mean
    base_ref[1:2] = inverse
    base_ref[2:3] = scale
    base_ref[3:4] = inverse * inverse
    values = [(v - mean) * inverse for v in values]

    def rows_of(chunk, carry):
        rows = pl.ds(chunk * ROWS, ROWS)
        level = levels_ref[0, rows]
        value = jnp.zeros(level.shape, jnp.float32)
        for index in range(count):
            value = jnp.where(level == index, values[index], value)
        out_ref[0, rows] = value
        return carry

    lax.fori_loop(0, CHUNKS, rows_of, 0)


def in_plane(plane, chunk):
    rows = pl.ds(chunk * ROWS, ROWS)
    before = pl.ds(pl.multiple_of((chunk * ROWS + 248) % 256, 8), 8)
    after = pl.ds(pl.multiple_of((chunk * ROWS + ROWS) % 256, 8), 8)
    middle = plane[rows]
    tall = jnp.concatenate([plane[before], middle, plane[after]], axis=0)
    beside = pltpu.roll(tall, 1, 0)[8 : 8 + ROWS]
    beside = beside + pltpu.roll(tall, ROWS + 15, 0)[8 : 8 + ROWS]
    return beside + (pltpu.roll(middle, 1, 1) + pltpu.roll(middle, 255, 1)), middle


def folded(values):
    total = values[:, :128] + values[:, 128:]
    return jnp.sum(total.reshape(ROWS // 8, 8, 128), axis=0)


def chunks(body, count):
    zero = jnp.zeros((8, 128), jnp.float32)
    return lax.fori_loop(0, CHUNKS, body, (zero,) * count)


def before_kernel(first, base_ref, own, sites, *refs):
    if first:
        first_ref, second_ref, sums = refs
    else:
        prior, older, first_ref, second_ref, sums = refs
    inverse = base_ref[1:2]

    def once(chunk, carry):
        rows = pl.ds(chunk * ROWS, ROWS)
        for j in range(2):
            beside, middle = in_plane(own.at[j], chunk)
            value = sites[j, rows] * middle - inverse * (beside + own[1 - j, rows])
            if first:
                carry = (carry[0] + folded(middle * middle),)
            else:
                last = prior[j, rows]
                value = value - last
                carry = (
                    carry[0] + folded(last * older[j, rows]),
                    carry[1] + folded(last * last),
                    carry[2] + folded(middle * last),
                    carry[3] + folded(middle * middle),
                )
            first_ref[j, rows] = value
        return carry

    totals = chunks(once, 1 if first else 4)

    def twice(chunk, carry):
        rows = pl.ds(chunk * ROWS, ROWS)
        for j in range(2):
            beside, middle = in_plane(first_ref.at[j], chunk)
            beside = beside + first_ref[1 - j, rows]
            second_ref[j, rows] = sites[j, rows] * middle - inverse * beside - own[j, rows]
        return carry

    chunks(twice, 0)
    for index, total in enumerate(totals):
        sums[index] = total


def after_kernel(first, last, side_ref, base_ref, even_ref, odd_ref, own, sites, one, two, *refs):
    refs = list(refs)
    if not first:
        edge_sites, edge_prior = refs[:2]
        refs = refs[2:]
    if last:
        parts, row_ref = refs[:4], refs[4]
    else:
        new_one, new_two, new_edge = refs[:3]
        kept = refs[3] if first else None
    inverse, inverse2 = base_ref[1:2], base_ref[3:4]

    def run(low, high):
        def body(chunk, carry):
            rows = pl.ds(chunk * ROWS, ROWS)
            near, far = (low.at[1], high.at[0]), (low.at[0], high.at[1])
            found = [in_plane(plane, chunk) for plane in near]
            for j in range(2):
                beside, middle = found[j]
                if first:
                    site = (low if j == 0 else high)[2, rows]
                    kept[j, rows] = site
                else:
                    site = edge_sites[j, rows]
                mine = own[j, rows]
                edge = site * middle - inverse * (beside + far[j][rows] + mine)
                if not first:
                    edge = edge - edge_prior[j, rows]
                value = one[j, rows] - inverse * middle
                new = two[j, rows] - inverse * (sites[j, rows] * middle + edge)
                new = new + inverse2 * (beside + found[1 - j][1])
                if last:
                    carry = (
                        carry[0] + folded(value * mine),
                        carry[1] + folded(value * value),
                        carry[2] + folded(new * value),
                    )
                else:
                    new_one[j, rows] = value
                    new_two[j, rows] = new
                    new_edge[j, rows] = edge
            return carry

        totals = chunks(body, 3 if last else 0)
        if last:
            pack(parts, totals, row_ref)

    @pl.when(side_ref[1] == 0)
    def _():
        run(odd_ref, even_ref)

    @pl.when(side_ref[1] == 1)
    def _():
        run(even_ref, odd_ref)


def pack(parts, totals, row_ref):
    entries = [(0, parts[0][0])]
    for index in range(3):
        places = (8 + 2 * index, 2 * index + 1, 9 + 2 * index, 2 * index + 2)
        entries += [(place, parts[index + 1][k]) for k, place in enumerate(places)]
    entries += list(zip((14, 7, 15), totals))
    lane = lax.broadcasted_iota(jnp.int32, (1, 128), 1)
    row = jnp.zeros((1, 128), jnp.float32)
    for place, value in entries:
        total = jnp.sum(jnp.sum(value, axis=0, keepdims=True), axis=1, keepdims=True)
        row = jnp.where(lane == place, total, row)
    row_ref[...] = row


def swap_kernel(side_ref, p1, p2, p3, out_ref):
    other = 1 - side_ref[0]

    def body(chunk, carry):
        rows = pl.ds(chunk * ROWS, ROWS)
        for index, ref in enumerate((p1, p2, p3)):
            out_ref[index, rows] = ref[other, rows]
        return carry

    chunks(body, 0)


def finish_kernel(
    side_ref, base_ref, rows_ref, start, p1, p2, p3, swapped,
    field_ref, diag_ref, offd_ref, moments_ref, good_ref,
):
    shift, scale = base_ref[0:1, :128], base_ref[2:3, :128]
    lane = lax.broadcasted_iota(jnp.int32, (2, 128), 1)
    rows = rows_ref[...]
    sub = lax.broadcasted_iota(jnp.int32, rows.shape, 0)
    even = jnp.sum(jnp.where(sub % 2 == 0, rows, 0.0), axis=0, keepdims=True)
    odd = jnp.sum(jnp.where(sub % 2 == 1, rows, 0.0), axis=0, keepdims=True)
    total = jnp.concatenate([even, odd], axis=0)

    def column(index):
        return jnp.broadcast_to(total[:, index : index + 1], (2, 128))

    plain = [column(index) for index in range(8)]
    largest = [jnp.maximum(plain[k], plain[min(k + 1, 7)]) for k in range(8)]
    square = [
        plain[k] + jnp.where(lane == k + 1, NUDGE * plain[k], 0.0) for k in range(8)
    ]
    cross = [
        column(8 + k) + jnp.where(lane == k + 9, NUDGE * largest[k], 0.0) for k in range(8)
    ]
    moment = []
    for k in range(8):
        moment.append(square[k] - square[k - 1] if k else square[k])
        moment.append(cross[k] - cross[k - 1] if k else cross[k])
    norm0 = moment[0]
    sigma = [value / norm0 for value in moment]
    normal = list(sigma)
    zero = jnp.zeros_like(norm0)
    older = [zero] * len(sigma)
    alphas, betas = [], []
    weight = zero
    for k in range(LANCZOS):
        size = len(sigma)
        pushed = [
            (sigma[l + 1] + sigma[l - 1]) if l else sigma[1] for l in range(size - 1)
        ]
        ratio = (pushed[k] - weight * older[k]) / sigma[k]
        alphas.append(ratio)
        if k < LANCZOS - 1:
            fresh = [
                pushed[l] - ratio * sigma[l] - weight * older[l] for l in range(size - 1)
            ]
            weight = fresh[k + 1] / sigma[k]
            betas.append(jnp.sqrt(weight))
            older, sigma = sigma, fresh
    alphas = [scale * value + shift for value in alphas]
    betas = [scale * value for value in betas]

    def spread(values):
        error, norm = zero, zero
        for value in values:
            exact = jnp.broadcast_to(value[:, :1], value.shape)
            error = error + jnp.square(
                jnp.broadcast_to(
                    jnp.sum(jnp.abs(value - exact), axis=1, keepdims=True), value.shape
                )
            )
            norm = norm + jnp.square(exact)
        error = jnp.sum(error, axis=0, keepdims=True)
        norm = jnp.sum(norm, axis=0, keepdims=True)
        allowed = TOLERANCE * NUDGE / ROUNDING
        return jnp.where(error <= allowed * allowed * norm, 1, 0)

    fits = jnp.minimum(spread(alphas), spread(betas))
    good_ref[0] = jnp.min(fits)

    lows, highs = [], []
    for k in range(LANCZOS):
        left = betas[k - 1] if k else zero
        right = betas[k] if k < LANCZOS - 1 else zero
        lows.append(alphas[k] - left - right)
        highs.append(alphas[k] + left + right)
    emin = functools.reduce(jnp.minimum, lows)
    emax = functools.reduce(jnp.maximum, highs)
    center = (emax + emin) * 0.5
    half = 0.55 * (emax - emin)
    offset = (shift - center) / half
    factor = scale / half

    def apply(coefs):
        out = []
        for l in range(len(coefs) + 1):
            value = zero
            if l < len(coefs):
                value = value + offset * coefs[l]
            if l + 1 < len(coefs):
                value = value + factor * coefs[l + 1]
            if l:
                value = value + factor * coefs[l - 1]
            out.append(value)
        return out

    terms = [[zero + 1.0]]
    terms.append(apply(terms[0]))
    for m in range(2, 7):
        nxt = apply(terms[-1])
        old = terms[-2]
        terms.append(
            [2.0 * v - (old[l] if l < len(old) else zero) for l, v in enumerate(nxt)]
        )
    diag, offd, out = zero, zero, zero
    for k in range(LANCZOS):
        diag = jnp.where(lane == k, jnp.broadcast_to(alphas[k][:, :1], lane.shape), diag)
        if k < LANCZOS - 1:
            offd = jnp.where(lane == k, jnp.broadcast_to(betas[k][:, :1], lane.shape), offd)
    for m in range(1, 7):
        value = functools.reduce(
            jnp.add, [c * normal[l] for l, c in enumerate(terms[m])]
        )
        out = jnp.where(lane == m - 1, jnp.broadcast_to(value[:, :1], lane.shape), out)
    diag_ref[...] = diag[:, :8]
    offd_ref[...] = offd[:, :7]
    moments_ref[...] = out[:, :6]

    here = side_ref[0]
    wide = [
        jnp.concatenate([jnp.broadcast_to(terms[3][l][:, :1], lane.shape)] * 2, axis=1)
        for l in range(4)
    ]
    mine = [jnp.where(here == 1, w[1:2], w[0:1]) for w in wide]
    other = [jnp.where(here == 1, w[0:1], w[1:2]) for w in wide]

    def combine(chunk, carry):
        at = pl.ds(chunk * ROWS, ROWS)
        value = mine[0] * start[here, 0, at]
        for l, ref in enumerate((p1, p2, p3)):
            value = value + mine[l + 1] * ref[here, at]
        field_ref[here, 0, at] = value
        value = other[0] * start[1 - here, 0, at]
        for l in range(3):
            value = value + other[l + 1] * swapped[l, at]
        field_ref[1 - here, 0, at] = value
        return carry

    chunks(combine, 0)


def gathered(row, axes, count):
    copies = jnp.broadcast_to(row[None], (count,) + row.shape)
    return lax.all_to_all(copies, axes, 0, 0, tiled=True).reshape(count, 128)


def exchange(block, route):
    return lax.ppermute(block, SLAB, route)


def shards(start_vectors, levels, energies):
    devices = 512
    inside = [(i, i ^ 2) for i in range(devices)]
    across = [(i, (((i + 2) ^ 2) - 2) % devices) for i in range(devices)]
    partner = [(i, i ^ 1) for i in range(devices)]
    core = lax.axis_index("slab_3").astype(jnp.int32)
    parity = lax.axis_index("slab_2").astype(jnp.int32) % 2
    side = jnp.stack([core, parity])

    sites_here, base = call(
        onsite_kernel, (shape(1, 256, 256), shape(8, 256)), [SMEM, VMEM], "onsite"
    )(energies, levels)
    own = lax.all_to_all(start_vectors, "slab_3", 0, 1, tiled=True)[0]
    sites = lax.all_gather(sites_here, "slab_3", axis=0, tiled=True)
    top, bottom = sites[1:2], sites[0:1]
    even = jnp.concatenate([own, jnp.where(parity == 0, top, bottom)], axis=0)
    odd = jnp.concatenate([own, jnp.where(parity == 0, bottom, top)], axis=0)
    even, odd = exchange(even, inside), exchange(odd, across)
    one, two, part = call(
        functools.partial(before_kernel, True),
        (PLANES, PLANES, shape(1, 8, 128)), [VMEM] * 3, "before_first",
    )(base, own, sites)
    parts = [part]
    ones, twos = [], [own]
    one, two, edge, edge_sites = call(
        functools.partial(after_kernel, True, False),
        (PLANES,) * 4, [SMEM] + [VMEM] * 7, "after_first",
    )(side, base, even, odd, own, sites, one, two)
    swapped = None
    for step in range(1, 4):
        ones.append(one)
        twos.append(two)
        even, odd = exchange(two, inside), exchange(two, across)
        one, two, part = call(
            functools.partial(before_kernel, False),
            (PLANES, PLANES, shape(4, 8, 128)), [VMEM] * 5, "before",
        )(base, twos[-1], sites, ones[-1], twos[-2])
        parts.append(part)
        if step == 2:
            swapped = exchange(
                call(swap_kernel, shape(3, 256, 256), [SMEM] + [VMEM] * 3, "swap")(
                    side, ones[0], twos[1], ones[1]
                ),
                partner,
            )
        operands = (side, base, even, odd, twos[-1], sites, one, two, edge_sites, edge)
        if step < 3:
            one, two, edge = call(
                functools.partial(after_kernel, False, False),
                (PLANES,) * 3, [SMEM] + [VMEM] * 9, "after",
            )(*operands)
        else:
            row = call(
                functools.partial(after_kernel, False, True),
                shape(1, 128), [SMEM] + [VMEM] * 13, "after_last",
            )(*operands, *parts)
    rows = gathered(row, STAGES[0], 32)
    rows = gathered(jnp.sum(rows, axis=0, keepdims=True), STAGES[1], 16)
    field, diag, offd, moments, good = call(
        finish_kernel,
        (
            shape(2, 1, 256, 256), shape(2, 8), shape(2, 7), shape(2, 6),
            jax.ShapeDtypeStruct((1,), jnp.int32),
        ),
        [SMEM] + [VMEM] * 7, "finish",
    )(side, base, rows, start_vectors, ones[0], twos[1], ones[1], swapped)

    def accept(field, diag, offd, moments, *_):
        return (field, diag, offd, moments)

    def redo(field, diag, offd, moments, *inputs):
        return stepwise(*inputs)

    return lax.cond(
        good[0] == 1, accept, redo,
        field, diag, offd, moments, start_vectors, levels, energies,
    )


def solution(mesh):
    split = Mesh(mesh.devices.reshape(8, 4, 8, 2), SLAB)
    in_specs = (P(None, SLAB, None, None), P(SLAB, None, None), P())
    out_specs = (P(None, SLAB, None, None), P(), P(), P())
    return jax.shard_map(
        shards, mesh=split, in_specs=in_specs, out_specs=out_specs, check_vma=False
    )
```

time: 161 us -> 143 us (0.89)
  starting transfers between devices: 70.1 us -> 58.7 us
  blocking collectives: 19.3 us -> 13.8 us
  Pallas kernels: 13.6 us -> 18 us
  waiting for transfers between devices: 52 us -> 48.2 us
    ppermute x8 -> x9, starting transfers between devices: 46.7 us -> 39.1 us  [exchange(): return lax.ppermute(block, SLAB, route)]
    all_to_all x1 -> x0, blocking collectives: 5.49 us -> none  [accept(): out = lax.all_to_all(field[None], 'slab_3', 1, 0, tiled=True)]
    pallas_call x7 -> x11, Pallas kernels: 13.6 us -> 18 us  [the longest x3 5.22 us: shards(): call(functools.partial(before_kernel, False), (PLANES, PLANES, shape(4, 8...]
    all_to_all x1, starting transfers between devices: 13 us -> 9.14 us  [gathered(): return lax.all_to_all(copies, axes, 0, 0, tiled=True).reshape(count, 128)]
    ppermute x8 -> x9, waiting for transfers between devices: 45 us -> 41.2 us  [exchange(): return lax.ppermute(block, SLAB, route)]
  transfers between devices with their start and end apart: 10 -> 11, of which waited for: 9 -> 9; matrix products, arithmetic and copies ran while one was open for 1% -> 1% of each run, Pallas kernels for 1% -> 8%
where the time goes in v3:
time: 143 us
  starting transfers between devices  58.7 us (41%)
  waiting for transfers between devices  48.2 us (34%)
  Pallas kernels  18 us (13%)
  blocking collectives  13.8 us (10%)
  between operations  1.53 us (1%)
  other arithmetic  1.43 us (1%)
    ppermute x9, waiting for transfers between devices, exchange(): return lax.ppermute(block, SLAB, route)  41.2 us
    ppermute x9, starting transfers between devices, exchange(): return lax.ppermute(block, SLAB, route)  39.1 us
    all_to_all x1, blocking collectives, gathered(): return lax.all_to_all(copies, axes, 0, 0, tiled=True).reshape(count, 128)  11.6 us
    all_to_all x1, starting transfers between devices, shards(): own = lax.all_to_all(start_vectors, 'slab_3', 0, 1, tiled=True)[0]  10.5 us
    all_to_all x1, starting transfers between devices, gathered(): return lax.all_to_all(copies, axes, 0, 0, tiled=True).reshape(count, 128)  9.14 us
    all_to_all x1, waiting for transfers between devices, gathered(): return lax.all_to_all(copies, axes, 0, 0, tiled=True).reshape(count, 128)  6.96 us
    pallas_call x3, Pallas kernels, shards(): call(functools.partial(before_kernel, False), (PLANES, PLANES, shape(4, 8...  5.22 us
    pallas_call x2, Pallas kernels, shards(): call(functools.partial(after_kernel, False, False), (PLANES,) * 3, [SMEM]...  3.12 us
  transfers between devices with their start and end apart: 11, of which 9 were waited for; matrix products, arithmetic and copies ran while one was open for 1% of the time, Pallas kernels for 8%

profile of v3, /device:TPU:1, one launch (start us, length us, event | category | flops | bytes accessed | tf_op | source)
XLA Modules:
  0.0 142.9 jit_solution(1438783361998645865)
XLA Ops:
  0.7 10.5 %all-to-all-start = ((f32[2,1,256,256]{3,2,1,0:T(8,128)}), f32[2,1,256,256]{3,2,1,0:T(8,128)S(1)}, u32[]{:S(2)}, u32[]{:S(2)}) async-start(f32[2,1,256,256]{3,2,1,0:T(8,128)} %start.1), calls=%async_computation | async-start | bytes 1048576 | tf_op jit(solution)/shard_map/all_to_all | solution.py:474
  11.1 0.9 onsite.1
  12.0 2.2 %all_gather.3.sites = f32[2,256,256]{2,1,0:T(8,128)S(1)} all-gather(f32[1,256,256]{2,1,0:T(8,128)S(1)} %get-tuple-element.89), channel_id=1, replica_groups=mesh['slab_0'=8,'slab_1'=4,'slab_2'=8,'slab_3'=2] {'slab_3'}, dimensions={0}, use_global_device_ids=true | all-gather | bytes 786432 | tf_op jit(solution)/shard_map/all_gather | solution.py:475
  14.3 1.3 pad_maximum_fusion
  15.6 10.4 %collective-permute-start.9 = (f32[3,256,256]{2,1,0:T(8,128)}, f32[3,256,256]{2,1,0:T(8,128)S(1)}, u32[]{:S(2)}, u32[]{:S(2)}) collective-permute-start(f32[3,256,256]{2,1,0:T(8,128)} %get-tuple-element.258), channel_id=1, source_target_pairs={{0,510},{1,511},{2,4},{3,5},{4,2},{5,3},{6,8},{7,9},{8,6},{9,7},{1... | collective-permute-start | bytes 2359304 | tf_op jit(solution)/shard_map/ppermute | solution.py:459
  26.0 1.9 %collective-permute-start.8 = (f32[3,256,256]{2,1,0:T(8,128)}, f32[3,256,256]{2,1,0:T(8,128)}, u32[]{:S(2)}, u32[]{:S(2)}) collective-permute-start(f32[3,256,256]{2,1,0:T(8,128)} %get-tuple-element.259), channel_id=1, source_target_pairs={{0,2},{1,3},{2,0},{3,1},{4,6},{5,7},{6,4},{7,5},{8,10},{9,11},{10,... | collective-permute-start | bytes 2359304 | tf_op jit(solution)/shard_map/ppermute | solution.py:459
  27.9 1.7 %before_first.1 = (f32[2,256,256]{2,1,0:T(8,128)S(1)}, f32[2,256,256]{2,1,0:T(8,128)S(1)}, f32[1,8,128]{2,1,0:T(8,128)S(1)}) custom-call(f32[8,256]{1,0:T(8,128)S(1)} %get-tuple-element.88.base_ref, f32[2,256,256]{2,1,0:T(8,128)S(1)} %bitcast.45, f32[2,256,256]{2,1,0:T(8,128)S(1)} %all_gather.3.sites), custom_call_target="tpu_custom_call" | custom-call | flops 4000000 | bytes 4000000 | tf_op jit(solution)/shard_map/before_first/pallas_call | solution.py:480
  29.7 14.2 %collective-permute-done.9.odd_ref = f32[3,256,256]{2,1,0:T(8,128)S(1)} collective-permute-done((f32[3,256,256]{2,1,0:T(8,128)}, f32[3,256,256]{2,1,0:T(8,128)S(1)}, u32[]{:S(2)}, u32[]{:S(2)}) %collective-permute-start.9) | collective-permute-done | bytes 786464 | tf_op jit(solution)/shard_map/ppermute | solution.py:459
  44.0 2.9 %collective-permute-done.8.even_ref = f32[3,256,256]{2,1,0:T(8,128)} collective-permute-done((f32[3,256,256]{2,1,0:T(8,128)}, f32[3,256,256]{2,1,0:T(8,128)}, u32[]{:S(2)}, u32[]{:S(2)}) %collective-permute-start.8) | collective-permute-done | bytes 786464 | tf_op jit(solution)/shard_map/ppermute | solution.py:459
  46.9 2.1 %after_first.1 = (f32[2,256,256]{2,1,0:T(8,128)S(1)}, f32[2,256,256]{2,1,0:T(8,128)S(1)}, f32[2,256,256]{2,1,0:T(8,128)S(1)}, f32[2,256,256]{2,1,0:T(8,128)S(1)}) custom-call(s32[2]{0:T(128)S(1)} %pad_add_fusion.side_ref, f32[8,256]{1,0:T(8,128)S(1)} %get-tuple-element.88.base_ref, f32[3,256,256]{2,1,0:T(8,128)} %collective-permute-done.8.even_ref, ...), custom_call_target="tpu_custom_call" | custom-call | flops 4000000 | bytes 4000000 | tf_op jit(solution)/shard_map/after_first/pallas_call | solution.py:486
  49.0 5.6 %collective-permute-start.11 = (f32[2,256,256]{2,1,0:T(8,128)S(1)}, f32[2,256,256]{2,1,0:T(8,128)S(1)}, u32[]{:S(2)}, u32[]{:S(2)}) collective-permute-start(f32[2,256,256]{2,1,0:T(8,128)S(1)} %get-tuple-element.92.own.refs_1_.p2), channel_id=1, source_target_pairs={{0,510},{1,511},{2,4},{3,5},{4,2},{5,3},{6,8},{7,9},{8,6},{9,7},{1... | collective-permute-start | bytes 1572872 | tf_op jit(solution)/shard_map/ppermute | solution.py:459
  54.6 1.9 %collective-permute-start.10 = (f32[2,256,256]{2,1,0:T(8,128)S(1)}, f32[2,256,256]{2,1,0:T(8,128)S(1)}, u32[]{:S(2)}, u32[]{:S(2)}) collective-permute-start(f32[2,256,256]{2,1,0:T(8,128)S(1)} %get-tuple-element.92.own.refs_1_.p2), channel_id=1, source_target_pairs={{0,2},{1,3},{2,0},{3,1},{4,6},{5,7},{6,4},{7,5},{8,10},{9,11},{10,... | collective-permute-start | bytes 1572872 | tf_op jit(solution)/shard_map/ppermute | solution.py:459
  56.6 1.7 %before.3 = (f32[2,256,256]{2,1,0:T(8,128)S(1)}, f32[2,256,256]{2,1,0:T(8,128)S(1)}, f32[4,8,128]{2,1,0:T(8,128)S(1)}) custom-call(f32[8,256]{1,0:T(8,128)S(1)} %get-tuple-element.88.base_ref, f32[2,256,256]{2,1,0:T(8,128)S(1)} %get-tuple-element.92.own.refs_1_.p2, f32[2,256,256]{2,1,0:T(8,128)S(1)} %all_gather.3.sites, ...), custom_call_target="tpu_custom_call" | custom-call | flops 4000000 | bytes 4000000 | tf_op jit(solution)/shard_map/before/pallas_call | solution.py:495
  58.3 10.3 %collective-permute-done.11.odd_ref = f32[2,256,256]{2,1,0:T(8,128)S(1)} collective-permute-done((f32[2,256,256]{2,1,0:T(8,128)S(1)}, f32[2,256,256]{2,1,0:T(8,128)S(1)}, u32[]{:S(2)}, u32[]{:S(2)}) %collective-permute-start.11) | collective-permute-done | bytes 524320 | tf_op jit(solution)/shard_map/ppermute | solution.py:459
  68.7 1.6 %after.2 = (f32[2,256,256]{2,1,0:T(8,128)S(1)}, f32[2,256,256]{2,1,0:T(8,128)S(1)}, f32[2,256,256]{2,1,0:T(8,128)S(1)}) custom-call(s32[2]{0:T(128)S(1)} %pad_add_fusion.side_ref, f32[8,256]{1,0:T(8,128)S(1)} %get-tuple-element.88.base_ref, f32[2,256,256]{2,1,0:T(8,128)S(1)} %collective-permute-done.10.even_ref, ...), custom_call_target="tpu_custom_call" | custom-call | flops 4000000 | bytes 4000000 | tf_op jit(solution)/shard_map/after/pallas_call | solution.py:509
  70.3 5.7 %collective-permute-start.13 = (f32[2,256,256]{2,1,0:T(8,128)S(1)}, f32[2,256,256]{2,1,0:T(8,128)S(1)}, u32[]{:S(2)}, u32[]{:S(2)}) collective-permute-start(f32[2,256,256]{2,1,0:T(8,128)S(1)} %get-tuple-element.98.own.refs_1_), channel_id=1, source_target_pairs={{0,510},{1,511},{2,4},{3,5},{4,2},{5,3},{6,8},{7,9},{8,6},{9,7},{1... | collective-permute-start | bytes 1572872 | tf_op jit(solution)/shard_map/ppermute | solution.py:459
  76.0 1.9 %collective-permute-start.12 = (f32[2,256,256]{2,1,0:T(8,128)S(1)}, f32[2,256,256]{2,1,0:T(8,128)S(1)}, u32[]{:S(2)}, u32[]{:S(2)}) collective-permute-start(f32[2,256,256]{2,1,0:T(8,128)S(1)} %get-tuple-element.98.own.refs_1_), channel_id=1, source_target_pairs={{0,2},{1,3},{2,0},{3,1},{4,6},{5,7},{6,4},{7,5},{8,10},{9,11},{10,... | collective-permute-start | bytes 1572872 | tf_op jit(solution)/shard_map/ppermute | solution.py:459
  77.9 0.6 swap.1
  78.6 4.0 %collective-permute-start.16 = (f32[3,256,256]{2,1,0:T(8,128)S(1)}, f32[3,256,256]{2,1,0:T(8,128)}, u32[]{:S(2)}, u32[]{:S(2)}) collective-permute-start(f32[3,256,256]{2,1,0:T(8,128)S(1)} %swap.1), channel_id=1, source_target_pairs={{0,1},{1,0},{2,3},{3,2},{4,5},{5,4},{6,7},{7,6},{8,9},{9,8},{10,11... | collective-permute-start | bytes 2359304 | tf_op jit(solution)/shard_map/ppermute | solution.py:459
  82.6 1.7 %before.4 = (f32[2,256,256]{2,1,0:T(8,128)S(1)}, f32[2,256,256]{2,1,0:T(8,128)S(1)}, f32[4,8,128]{2,1,0:T(8,128)S(1)}) custom-call(f32[8,256]{1,0:T(8,128)S(1)} %get-tuple-element.88.base_ref, f32[2,256,256]{2,1,0:T(8,128)S(1)} %get-tuple-element.98.own.refs_1_, f32[2,256,256]{2,1,0:T(8,128)S(1)} %all_gather.3.sites, ...), custom_call_target="tpu_custom_call" | custom-call | flops 4000000 | bytes 4000000 | tf_op jit(solution)/shard_map/before/pallas_call | solution.py:495
  84.4 4.6 %collective-permute-done.13.odd_ref = f32[2,256,256]{2,1,0:T(8,128)S(1)} collective-permute-done((f32[2,256,256]{2,1,0:T(8,128)S(1)}, f32[2,256,256]{2,1,0:T(8,128)S(1)}, u32[]{:S(2)}, u32[]{:S(2)}) %collective-permute-start.13) | collective-permute-done | bytes 524320 | tf_op jit(solution)/shard_map/ppermute | solution.py:459
  89.3 1.6 %after.3 = (f32[2,256,256]{2,1,0:T(8,128)S(1)}, f32[2,256,256]{2,1,0:T(8,128)S(1)}, f32[2,256,256]{2,1,0:T(8,128)S(1)}) custom-call(s32[2]{0:T(128)S(1)} %pad_add_fusion.side_ref, f32[8,256]{1,0:T(8,128)S(1)} %get-tuple-element.88.base_ref, f32[2,256,256]{2,1,0:T(8,128)S(1)} %collective-permute-done.12.even_ref, ...), custom_call_target="tpu_custom_call" | custom-call | flops 4000000 | bytes 4000000 | tf_op jit(solution)/shard_map/after/pallas_call | solution.py:509
  90.8 5.7 %collective-permute-start.15 = (f32[2,256,256]{2,1,0:T(8,128)S(1)}, f32[2,256,256]{2,1,0:T(8,128)S(1)}, u32[]{:S(2)}, u32[]{:S(2)}) collective-permute-start(f32[2,256,256]{2,1,0:T(8,128)S(1)} %get-tuple-element.103.own), channel_id=1, source_target_pairs={{0,510},{1,511},{2,4},{3,5},{4,2},{5,3},{6,8},{7,9},{8,6},{9,7},{1... | collective-permute-start | bytes 1572872 | tf_op jit(solution)/shard_map/ppermute | solution.py:459
  96.5 1.9 %collective-permute-start.14 = (f32[2,256,256]{2,1,0:T(8,128)S(1)}, f32[2,256,256]{2,1,0:T(8,128)S(1)}, u32[]{:S(2)}, u32[]{:S(2)}) collective-permute-start(f32[2,256,256]{2,1,0:T(8,128)S(1)} %get-tuple-element.103.own), channel_id=1, source_target_pairs={{0,2},{1,3},{2,0},{3,1},{4,6},{5,7},{6,4},{7,5},{8,10},{9,11},{10,... | collective-permute-start | bytes 1572872 | tf_op jit(solution)/shard_map/ppermute | solution.py:459
  98.5 1.8 %before.5 = (f32[2,256,256]{2,1,0:T(8,128)S(1)}, f32[2,256,256]{2,1,0:T(8,128)S(1)}, f32[4,8,128]{2,1,0:T(8,128)S(1)}) custom-call(f32[8,256]{1,0:T(8,128)S(1)} %get-tuple-element.88.base_ref, f32[2,256,256]{2,1,0:T(8,128)S(1)} %get-tuple-element.103.own, f32[2,256,256]{2,1,0:T(8,128)S(1)} %all_gather.3.sites, ...), custom_call_target="tpu_custom_call" | custom-call | flops 4000000 | bytes 4000000 | tf_op jit(solution)/shard_map/before/pallas_call | solution.py:495
  100.2 8.4 %collective-permute-done.15.odd_ref = f32[2,256,256]{2,1,0:T(8,128)S(1)} collective-permute-done((f32[2,256,256]{2,1,0:T(8,128)S(1)}, f32[2,256,256]{2,1,0:T(8,128)S(1)}, u32[]{:S(2)}, u32[]{:S(2)}) %collective-permute-start.15) | collective-permute-done | bytes 524320 | tf_op jit(solution)/shard_map/ppermute | solution.py:459
  108.9 1.7 %after_last.1 = f32[1,128]{1,0:T(1,128)S(1)} custom-call(s32[2]{0:T(128)S(1)} %pad_add_fusion.side_ref, f32[8,256]{1,0:T(8,128)S(1)} %get-tuple-element.88.base_ref, f32[2,256,256]{2,1,0:T(8,128)S(1)} %collective-permute-done.14.even_ref, f32[2,256,256]{2,1,0:T(8,128)S(1)} %collective-permute-done.15.odd_ref, f32[2,256,256]{2,1,0:T(8,128)S(1)} %get-tuple-element.103.own, ...), custom_call_target="tpu_custom_call" | custom-call | flops 4000000 | bytes 4000000 | tf_op jit(solution)/shard_map/after_last/pallas_call | solution.py:514
  110.6 11.6 %all_to_all.19 = f32[32,1,128]{2,1,0:T(1,128)S(1)} all-to-all(f32[32,1,128]{2,1,0:T(1,128)S(1)} %broadcast_in_dim.30), channel_id=1, replica_groups=mesh['slab_0'=8,'slab_1'=4,'slab_2'=8,'slab_3'=2] {'slab_1','slab_2'}, dimensions={0} | all-to-all | bytes 32768 | tf_op jit(solution)/shard_map/all_to_all | solution.py:455
  122.3 0.6 broadcast_in_dim.31
  122.9 9.1 %all-to-all-start.2 = ((f32[16,1,128]{2,1,0:T(1,128)}), f32[16,1,128]{2,1,0:T(1,128)S(1)}, u32[]{:S(2)}, u32[]{:S(2)}) async-start(f32[16,1,128]{2,1,0:T(1,128)} %broadcast_in_dim.31), calls=%async_computation.2 | async-start | bytes 16384 | tf_op jit(solution)/shard_map/all_to_all | solution.py:455
  132.0 7.0 %all-to-all-done.2 = f32[16,1,128]{2,1,0:T(1,128)S(1)} async-done(((f32[16,1,128]{2,1,0:T(1,128)}), f32[16,1,128]{2,1,0:T(1,128)S(1)}, u32[]{:S(2)}, u32[]{:S(2)}) %all-to-all-start.2) | async-done | bytes 8224 | tf_op jit(solution)/shard_map/all_to_all | solution.py:455
  139.0 2.6 %finish.1 = (f32[2,1,256,256]{3,2,1,0:T(8,128)}, f32[2,8]{1,0:T(2,128)S(1)}, f32[2,7]{1,0:T(2,128)S(1)}, f32[2,6]{1,0:T(2,128)S(1)}, s32[1]{0:T(128)}) custom-call(s32[2]{0:T(128)S(1)} %pad_add_fusion.side_ref, f32[8,256]{1,0:T(8,128)S(1)} %get-tuple-element.88.base_ref, f32[16,128]{1,0:T(8,128)S(1)} %bitcast.48, f32[2,1,256,256]{3,2,1,0:T(8,128)S(1)} %copy-done, ...), custom_call_target="tpu_custom_call" | custom-call | flops 4000000 | bytes 4000000 | tf_op jit(solution)/shard_map/finish/pallas_call | solution.py:520
  (24 shorter events, 1.5 us)
Async XLA Ops:
  0.6 10.5 %copy-start.6 = (f32[16]{0:T(128)S(1)}, f32[16]{0:T(128)}, u32[]{:S(2)}) copy-start(f32[16]{0:T(128)} %energies_ref.1) | copy-start | bytes 196
  0.6 10.5 %copy-start.2 = (s32[1,256,256]{2,1,0:T(8,128)S(1)}, s32[1,256,256]{2,1,0:T(8,128)}, u32[]{:S(2)}) copy-start(s32[1,256,256]{2,1,0:T(8,128)} %levels_ref.1) | copy-start | bytes 786436
  0.7 13.6 %all-to-all-start = ((f32[2,1,256,256]{3,2,1,0:T(8,128)}), f32[2,1,256,256]{3,2,1,0:T(8,128)S(1)}, u32[]{:S(2)}, u32[]{:S(2)}) async-start(f32[2,1,256,256]{3,2,1,0:T(8,128)} %start.1), calls=%async_computation | async-start | bytes 1048576 | tf_op jit(solution)/shard_map/all_to_all | solution.py:474
  15.6 28.4 %collective-permute-start.9 = (f32[3,256,256]{2,1,0:T(8,128)}, f32[3,256,256]{2,1,0:T(8,128)S(1)}, u32[]{:S(2)}, u32[]{:S(2)}) collective-permute-start(f32[3,256,256]{2,1,0:T(8,128)} %get-tuple-element.258), channel_id=1, source_target_pairs={{0,510},{1,511},{2,4},{3,5},{4,2},{5,3},{6,8},{7,9},{8,6},{9,7},{1... | collective-permute-start | bytes 2359304 | tf_op jit(solution)/shard_map/ppermute | solution.py:459
  26.0 20.9 %collective-permute-start.8 = (f32[3,256,256]{2,1,0:T(8,128)}, f32[3,256,256]{2,1,0:T(8,128)}, u32[]{:S(2)}, u32[]{:S(2)}) collective-permute-start(f32[3,256,256]{2,1,0:T(8,128)} %get-tuple-element.259), channel_id=1, source_target_pairs={{0,2},{1,3},{2,0},{3,1},{4,6},{5,7},{6,4},{7,5},{8,10},{9,11},{10,... | collective-permute-start | bytes 2359304 | tf_op jit(solution)/shard_map/ppermute | solution.py:459
  49.0 19.5 %collective-permute-start.11 = (f32[2,256,256]{2,1,0:T(8,128)S(1)}, f32[2,256,256]{2,1,0:T(8,128)S(1)}, u32[]{:S(2)}, u32[]{:S(2)}) collective-permute-start(f32[2,256,256]{2,1,0:T(8,128)S(1)} %get-tuple-element.92.own.refs_1_.p2), channel_id=1, source_target_pairs={{0,510},{1,511},{2,4},{3,5},{4,2},{5,3},{6,8},{7,9},{8,6},{9,7},{1... | collective-permute-start | bytes 1572872 | tf_op jit(solution)/shard_map/ppermute | solution.py:459
  54.6 14.1 %collective-permute-start.10 = (f32[2,256,256]{2,1,0:T(8,128)S(1)}, f32[2,256,256]{2,1,0:T(8,128)S(1)}, u32[]{:S(2)}, u32[]{:S(2)}) collective-permute-start(f32[2,256,256]{2,1,0:T(8,128)S(1)} %get-tuple-element.92.own.refs_1_.p2), channel_id=1, source_target_pairs={{0,2},{1,3},{2,0},{3,1},{4,6},{5,7},{6,4},{7,5},{8,10},{9,11},{10,... | collective-permute-start | bytes 1572872 | tf_op jit(solution)/shard_map/ppermute | solution.py:459
  70.3 18.7 %collective-permute-start.13 = (f32[2,256,256]{2,1,0:T(8,128)S(1)}, f32[2,256,256]{2,1,0:T(8,128)S(1)}, u32[]{:S(2)}, u32[]{:S(2)}) collective-permute-start(f32[2,256,256]{2,1,0:T(8,128)S(1)} %get-tuple-element.98.own.refs_1_), channel_id=1, source_target_pairs={{0,510},{1,511},{2,4},{3,5},{4,2},{5,3},{6,8},{7,9},{8,6},{9,7},{1... | collective-permute-start | bytes 1572872 | tf_op jit(solution)/shard_map/ppermute | solution.py:459
  76.0 13.2 %collective-permute-start.12 = (f32[2,256,256]{2,1,0:T(8,128)S(1)}, f32[2,256,256]{2,1,0:T(8,128)S(1)}, u32[]{:S(2)}, u32[]{:S(2)}) collective-permute-start(f32[2,256,256]{2,1,0:T(8,128)S(1)} %get-tuple-element.98.own.refs_1_), channel_id=1, source_target_pairs={{0,2},{1,3},{2,0},{3,1},{4,6},{5,7},{6,4},{7,5},{8,10},{9,11},{10,... | collective-permute-start | bytes 1572872 | tf_op jit(solution)/shard_map/ppermute | solution.py:459
  78.6 53.5 %collective-permute-start.16 = (f32[3,256,256]{2,1,0:T(8,128)S(1)}, f32[3,256,256]{2,1,0:T(8,128)}, u32[]{:S(2)}, u32[]{:S(2)}) collective-permute-start(f32[3,256,256]{2,1,0:T(8,128)S(1)} %swap.1), channel_id=1, source_target_pairs={{0,1},{1,0},{2,3},{3,2},{4,5},{5,4},{6,7},{7,6},{8,9},{9,8},{10,11... | collective-permute-start | bytes 2359304 | tf_op jit(solution)/shard_map/ppermute | solution.py:459
  90.8 17.8 %collective-permute-start.15 = (f32[2,256,256]{2,1,0:T(8,128)S(1)}, f32[2,256,256]{2,1,0:T(8,128)S(1)}, u32[]{:S(2)}, u32[]{:S(2)}) collective-permute-start(f32[2,256,256]{2,1,0:T(8,128)S(1)} %get-tuple-element.103.own), channel_id=1, source_target_pairs={{0,510},{1,511},{2,4},{3,5},{4,2},{5,3},{6,8},{7,9},{8,6},{9,7},{1... | collective-permute-start | bytes 1572872 | tf_op jit(solution)/shard_map/ppermute | solution.py:459
  96.5 12.4 %collective-permute-start.14 = (f32[2,256,256]{2,1,0:T(8,128)S(1)}, f32[2,256,256]{2,1,0:T(8,128)S(1)}, u32[]{:S(2)}, u32[]{:S(2)}) collective-permute-start(f32[2,256,256]{2,1,0:T(8,128)S(1)} %get-tuple-element.103.own), channel_id=1, source_target_pairs={{0,2},{1,3},{2,0},{3,1},{4,6},{5,7},{6,4},{7,5},{8,10},{9,11},{10,... | collective-permute-start | bytes 1572872 | tf_op jit(solution)/shard_map/ppermute | solution.py:459
  108.9 30.1 %copy-start = (f32[2,1,256,256]{3,2,1,0:T(8,128)S(1)}, f32[2,1,256,256]{3,2,1,0:T(8,128)}, u32[]{:S(2)}) copy-start(f32[2,1,256,256]{3,2,1,0:T(8,128)} %start.1) | copy-start | bytes 1572868
  122.9 16.1 %all-to-all-start.2 = ((f32[16,1,128]{2,1,0:T(1,128)}), f32[16,1,128]{2,1,0:T(1,128)S(1)}, u32[]{:S(2)}, u32[]{:S(2)}) async-start(f32[16,1,128]{2,1,0:T(1,128)} %broadcast_in_dim.31), calls=%async_computation.2 | async-start | bytes 16384 | tf_op jit(solution)/shard_map/all_to_all | solution.py:455
  139.0 3.2 %copy-start.3 = (s32[1,256,256]{2,1,0:T(8,128)S(1)}, s32[1,256,256]{2,1,0:T(8,128)}, u32[]{:S(2)}) copy-start(s32[1,256,256]{2,1,0:T(8,128)} %levels_ref.1) | copy-start | bytes 786436
  142.3 0.6 copy-start.7
  142.3 0.6 copy-start.8
  142.3 0.6 copy-start.9

commit v4 on v3

--- a/solution.py
+++ b/solution.py
@@ -140,10 +140,12 @@
     )
 
 
-def onsite_kernel(energies_ref, levels_ref, out_ref, base_ref):
-    count = energies_ref.shape[0]
-    row = jnp.zeros((1, 256), jnp.float32)
-    values = [row + energies_ref[index] for index in range(count)]
+def onsite_kernel(energies_ref, levels_ref, start, out_ref, send_ref, base_ref):
+    count = energies_ref.shape[1]
+    values = [
+        jnp.broadcast_to(energies_ref[0:1, index : index + 1], (1, 256))
+        for index in range(count)
+    ]
     mean = functools.reduce(jnp.add, values) * (1.0 / count)
     spread = functools.reduce(jnp.add, [jnp.square(v - mean) for v in values])
     scale = 1.05 * jnp.sqrt(6.0 + spread * (1.0 / count))
@@ -153,6 +155,7 @@
     base_ref[2:3] = scale
     base_ref[3:4] = inverse * inverse
     values = [(v - mean) * inverse for v in values]
+    other = 1 - lax.axis_index(SLAB[3])
 
     def rows_of(chunk, carry):
         rows = pl.ds(chunk * ROWS, ROWS)
@@ -160,10 +163,38 @@
         value = jnp.zeros(level.shape, jnp.float32)
         for index in range(count):
             value = jnp.where(level == index, values[index], value)
-        out_ref[0, rows] = value
+        out_ref[rows] = value
+        send_ref[1, rows] = value
+        send_ref[0, rows] = start[other, 0, rows]
         return carry
 
     lax.fori_loop(0, CHUNKS, rows_of, 0)
+
+
+def assemble_kernel(start, sites_here, received, own_ref, sites_ref):
+    here = lax.axis_index(SLAB[3])
+
+    def body(chunk, carry):
+        rows = pl.ds(chunk * ROWS, ROWS)
+        own_ref[here, rows] = start[here, 0, rows]
+        own_ref[1 - here, rows] = received[0, rows]
+        sites_ref[here, rows] = sites_here[rows]
+        sites_ref[1 - here, rows] = received[1, rows]
+        return carry
+
+    chunks(body, 0)
+
+
+def join_kernel(mine, theirs, out_ref):
+    here = lax.axis_index(SLAB[3])
+
+    def body(chunk, carry):
+        rows = pl.ds(chunk * ROWS, ROWS)
+        out_ref[here, rows] = mine[rows]
+        out_ref[1 - here, rows] = theirs[rows]
+        return carry
+
+    chunks(body, 0)
 
 
 def in_plane(plane, chunk):
@@ -228,16 +259,15 @@
         sums[index] = total
 
 
-def after_kernel(first, last, side_ref, base_ref, even_ref, odd_ref, own, sites, one, two, *refs):
+def after_kernel(first, last, base_ref, even_ref, odd_ref, own, sites, one, two, *refs):
     refs = list(refs)
+    edge_sites = refs.pop(0)
     if not first:
-        edge_sites, edge_prior = refs[:2]
-        refs = refs[2:]
+        edge_prior = refs.pop(0)
     if last:
         parts, row_ref = refs[:4], refs[4]
     else:
-        new_one, new_two, new_edge = refs[:3]
-        kept = refs[3] if first else None
+        new_one, new_two, new_edge = refs
     inverse, inverse2 = base_ref[1:2], base_ref[3:4]
 
     def run(low, high):
@@ -247,11 +277,7 @@
             found = [in_plane(plane, chunk) for plane in near]
             for j in range(2):
                 beside, middle = found[j]
-                if first:
-                    site = (low if j == 0 else high)[2, rows]
-                    kept[j, rows] = site
-                else:
-                    site = edge_sites[j, rows]
+                site = edge_sites[j, rows]
                 mine = own[j, rows]
                 edge = site * middle - inverse * (beside + far[j][rows] + mine)
                 if not first:
@@ -275,11 +301,13 @@
         if last:
             pack(parts, totals, row_ref)
 
-    @pl.when(side_ref[1] == 0)
+    parity = lax.axis_index(SLAB[2]) % 2
+
+    @pl.when(parity == 0)
     def _():
         run(odd_ref, even_ref)
 
-    @pl.when(side_ref[1] == 1)
+    @pl.when(parity == 1)
     def _():
         run(even_ref, odd_ref)
 
@@ -298,8 +326,8 @@
     row_ref[...] = row
 
 
-def swap_kernel(side_ref, p1, p2, p3, out_ref):
-    other = 1 - side_ref[0]
+def swap_kernel(p1, p2, p3, out_ref):
+    other = 1 - lax.axis_index(SLAB[3])
 
     def body(chunk, carry):
         rows = pl.ds(chunk * ROWS, ROWS)
@@ -311,7 +339,7 @@
 
 
 def finish_kernel(
-    side_ref, base_ref, rows_ref, start, p1, p2, p3, swapped,
+    base_ref, rows_ref, start, p1, p2, p3, swapped,
     field_ref, diag_ref, offd_ref, moments_ref, good_ref,
 ):
     shift, scale = base_ref[0:1, :128], base_ref[2:3, :128]
@@ -427,7 +455,7 @@
     offd_ref[...] = offd[:, :7]
     moments_ref[...] = out[:, :6]
 
-    here = side_ref[0]
+    here = lax.axis_index(SLAB[3])
     wide = [
         jnp.concatenate([jnp.broadcast_to(terms[3][l][:, :1], lane.shape)] * 2, axis=1)
         for l in range(4)
@@ -464,29 +492,31 @@
     inside = [(i, i ^ 2) for i in range(devices)]
     across = [(i, (((i + 2) ^ 2) - 2) % devices) for i in range(devices)]
     partner = [(i, i ^ 1) for i in range(devices)]
-    core = lax.axis_index("slab_3").astype(jnp.int32)
-    parity = lax.axis_index("slab_2").astype(jnp.int32) % 2
-    side = jnp.stack([core, parity])
-
-    sites_here, base = call(
-        onsite_kernel, (shape(1, 256, 256), shape(8, 256)), [SMEM, VMEM], "onsite"
-    )(energies, levels)
-    own = lax.all_to_all(start_vectors, "slab_3", 0, 1, tiled=True)[0]
-    sites = lax.all_gather(sites_here, "slab_3", axis=0, tiled=True)
-    top, bottom = sites[1:2], sites[0:1]
-    even = jnp.concatenate([own, jnp.where(parity == 0, top, bottom)], axis=0)
-    odd = jnp.concatenate([own, jnp.where(parity == 0, bottom, top)], axis=0)
-    even, odd = exchange(even, inside), exchange(odd, across)
+    adjacent = [(i, (((i + 1) ^ 1) - 1) % devices) for i in range(devices)]
+
+    sites_here, send, base = call(
+        onsite_kernel, (shape(256, 256), PLANES, shape(8, 256)),
+        [VMEM] * 3, "onsite",
+    )(energies.reshape(1, -1), levels, start_vectors)
+    beyond = exchange(sites_here, adjacent)
+    own, sites = call(
+        assemble_kernel, (PLANES, PLANES), [VMEM] * 3, "assemble"
+    )(start_vectors, sites_here, exchange(send, partner))
+    even, odd = exchange(own, inside), exchange(own, across)
     one, two, part = call(
         functools.partial(before_kernel, True),
         (PLANES, PLANES, shape(1, 8, 128)), [VMEM] * 3, "before_first",
     )(base, own, sites)
+    beyond, part = lax.optimization_barrier((beyond, part))
+    edge_sites = call(join_kernel, PLANES, [VMEM] * 2, "join")(
+        beyond, exchange(beyond, partner)
+    )
     parts = [part]
     ones, twos = [], [own]
-    one, two, edge, edge_sites = call(
+    one, two, edge = call(
         functools.partial(after_kernel, True, False),
-        (PLANES,) * 4, [SMEM] + [VMEM] * 7, "after_first",
-    )(side, base, even, odd, own, sites, one, two)
+        (PLANES,) * 3, [VMEM] * 8, "after_first",
+    )(base, even, odd, own, sites, one, two, edge_sites)
     swapped = None
     for step in range(1, 4):
         ones.append(one)
@@ -499,21 +529,21 @@
         parts.append(part)
         if step == 2:
             swapped = exchange(
-                call(swap_kernel, shape(3, 256, 256), [SMEM] + [VMEM] * 3, "swap")(
-                    side, ones[0], twos[1], ones[1]
+                call(swap_kernel, shape(3, 256, 256), [VMEM] * 3, "swap")(
+                    ones[0], twos[1], ones[1]
                 ),
                 partner,
             )
-        operands = (side, base, even, odd, twos[-1], sites, one, two, edge_sites, edge)
+        operands = (base, even, odd, twos[-1], sites, one, two, edge_sites, edge)
         if step < 3:
             one, two, edge = call(
                 functools.partial(after_kernel, False, False),
-                (PLANES,) * 3, [SMEM] + [VMEM] * 9, "after",
+                (PLANES,) * 3, [VMEM] * 9, "after",
             )(*operands)
         else:
             row = call(
                 functools.partial(after_kernel, False, True),
-                shape(1, 128), [SMEM] + [VMEM] * 13, "after_last",
+                shape(1, 128), [VMEM] * 13, "after_last",
             )(*operands, *parts)
     rows = gathered(row, STAGES[0], 32)
     rows = gathered(jnp.sum(rows, axis=0, keepdims=True), STAGES[1], 16)
@@ -523,8 +553,8 @@
             shape(2, 1, 256, 256), shape(2, 8), shape(2, 7), shape(2, 6),
             jax.ShapeDtypeStruct((1,), jnp.int32),
         ),
-        [SMEM] + [VMEM] * 7, "finish",
-    )(side, base, rows, start_vectors, ones[0], twos[1], ones[1], swapped)
+        [VMEM] * 7, "finish",
+    )(base, rows, start_vectors, ones[0], twos[1], ones[1], swapped)
 
     def accept(field, diag, offd, moments, *_):
         return (field, diag, offd, moments)

time: 143 us -> 133 us (0.930)
  waiting for transfers between devices: 48.2 us -> 34.9 us
  starting transfers between devices: 58.7 us -> 67.6 us
  Pallas kernels: 18 us -> 15.5 us
  blocking collectives: 13.8 us -> 11.6 us
    ppermute x9 -> x12, starting transfers between devices: 39.1 us -> 56.2 us  [exchange(): return lax.ppermute(block, SLAB, route)]
    ppermute x9 -> x12, waiting for transfers between devices: 41.2 us -> 27.9 us  [exchange(): return lax.ppermute(block, SLAB, route)]
    all_to_all x1 -> x0, starting transfers between devices: 10.5 us -> none  [shards(): own = lax.all_to_all(start_vectors, 'slab_3', 0, 1, tiled=True)[0]]
    pallas_call x6 -> x8, Pallas kernels: 8.47 us -> 6.01 us  [the longest x2 2 us: shards(): call(functools.partial(after_kernel, False, False), (PLANES,) * 3, [VMEM]...]
    all_to_all x1, starting transfers between devices: 9.14 us -> 11.4 us  [gathered(): return lax.all_to_all(copies, axes, 0, 0, tiled=True).reshape(count, 128)]
    all_gather x1 -> x0, blocking collectives: 2.18 us -> none  [shards(): sites = lax.all_gather(sites_here, 'slab_3', axis=0, tiled=True)]
  transfers between devices with their start and end apart: 11 -> 13, of which waited for: 9 -> 10; matrix products, arithmetic and copies ran while one was open for 1% -> 0% of each run, Pallas kernels for 8% -> 7%
where the time goes in v4:
time: 133 us; the launch traced here: 132 us
  starting transfers between devices  67.6 us (51%)
  waiting for transfers between devices  34.9 us (26%)
  Pallas kernels  15.5 us (12%)
  blocking collectives  11.6 us (9%)
  between operations  1.58 us (1%)
    ppermute x12, starting transfers between devices, exchange(): return lax.ppermute(block, SLAB, route)  56.2 us
    ppermute x12, waiting for transfers between devices, exchange(): return lax.ppermute(block, SLAB, route)  27.9 us
    all_to_all x1, blocking collectives, gathered(): return lax.all_to_all(copies, axes, 0, 0, tiled=True).reshape(count, 128)  11.6 us
    all_to_all x1, starting transfers between devices, gathered(): return lax.all_to_all(copies, axes, 0, 0, tiled=True).reshape(count, 128)  11.4 us
    all_to_all x1, waiting for transfers between devices, gathered(): return lax.all_to_all(copies, axes, 0, 0, tiled=True).reshape(count, 128)  6.96 us
    pallas_call x3, Pallas kernels, shards(): call(functools.partial(before_kernel, False), (PLANES, PLANES, shape(4, 8...  5.24 us
  transfers between devices with their start and end apart: 13, of which 10 were waited for; matrix products, arithmetic and copies ran while one was open for 0% of the time, Pallas kernels for 7%

profile of v4, /device:TPU:1, one launch (start us, length us, event | category | flops | bytes accessed | tf_op | source)
XLA Modules:
  0.0 132.4 jit_solution(986234304058278391)
XLA Ops:
  0.6 1.6 %onsite.1 = (f32[256,256]{1,0:T(8,128)S(1)}, f32[2,256,256]{2,1,0:T(8,128)S(1)}, f32[8,256]{1,0:T(8,128)S(1)}) custom-call(f32[1,16]{1,0:T(1,128)} %bitcast.53, s32[1,256,256]{2,1,0:T(8,128)} %levels_ref.1, f32[2,1,256,256]{3,2,1,0:T(8,128)} %start.5), custom_call_target="tpu_custom_call" | custom-call | flops 4000000 | bytes 4000000 | tf_op jit(solution)/shard_map/onsite/pallas_call | solution.py:497
  2.3 8.7 %collective-permute-start.8 = (f32[2,256,256]{2,1,0:T(8,128)S(1)}, f32[2,256,256]{2,1,0:T(8,128)S(1)}, u32[]{:S(2)}, u32[]{:S(2)}) collective-permute-start(f32[2,256,256]{2,1,0:T(8,128)S(1)} %get-tuple-element.94), channel_id=1, source_target_pairs={{0,1},{1,0},{2,3},{3,2},{4,5},{5,4},{6,7},{7,6},{8,9},{9,8},{10,11... | collective-permute-start | bytes 1572872 | tf_op jit(solution)/shard_map/ppermute | solution.py:487
  11.0 1.9 %collective-permute-start.11 = (f32[256,256]{1,0:T(8,128)S(1)}, f32[256,256]{1,0:T(8,128)S(1)}, u32[]{:S(2)}, u32[]{:S(2)}) collective-permute-start(f32[256,256]{1,0:T(8,128)S(1)} %get-tuple-element.93.sites_here), channel_id=1, source_target_pairs={{0,511},{1,2},{2,1},{3,4},{4,3},{5,6},{6,5},{7,8},{8,7},{9,10},{10... | collective-permute-start | bytes 786440 | tf_op jit(solution)/shard_map/ppermute | solution.py:487
  13.1 10.4 %collective-permute-start.10 = (f32[2,256,256]{2,1,0:T(8,128)S(1)}, f32[2,256,256]{2,1,0:T(8,128)S(1)}, u32[]{:S(2)}, u32[]{:S(2)}) collective-permute-start(f32[2,256,256]{2,1,0:T(8,128)S(1)} %get-tuple-element.95.own.refs_1_), channel_id=1, source_target_pairs={{0,510},{1,511},{2,4},{3,5},{4,2},{5,3},{6,8},{7,9},{8,6},{9,7},{1... | collective-permute-start | bytes 1572872 | tf_op jit(solution)/shard_map/ppermute | solution.py:487
  23.5 1.9 %collective-permute-start.9 = (f32[2,256,256]{2,1,0:T(8,128)S(1)}, f32[2,256,256]{2,1,0:T(8,128)S(1)}, u32[]{:S(2)}, u32[]{:S(2)}) collective-permute-start(f32[2,256,256]{2,1,0:T(8,128)S(1)} %get-tuple-element.95.own.refs_1_), channel_id=1, source_target_pairs={{0,2},{1,3},{2,0},{3,1},{4,6},{5,7},{6,4},{7,5},{8,10},{9,11},{10,... | collective-permute-start | bytes 1572872 | tf_op jit(solution)/shard_map/ppermute | solution.py:487
  25.5 1.7 %before_first.1 = (f32[2,256,256]{2,1,0:T(8,128)S(1)}, f32[2,256,256]{2,1,0:T(8,128)S(1)}, f32[1,8,128]{2,1,0:T(8,128)S(1)}) custom-call(f32[8,256]{1,0:T(8,128)S(1)} %get-tuple-element.92.base_ref, f32[2,256,256]{2,1,0:T(8,128)S(1)} %get-tuple-element.95.own.refs_1_, f32[2,256,256]{2,1,0:T(8,128)S(1)} %get-tuple-element.96.sites), custom_call_target="tpu_custom_call" | custom-call | flops 4000000 | bytes 4000000 | tf_op jit(solution)/shard_map/before_first/pallas_call | solution.py:506
  27.2 3.6 %collective-permute-start.12 = (f32[256,256]{1,0:T(8,128)S(1)}, f32[256,256]{1,0:T(8,128)S(1)}, u32[]{:S(2)}, u32[]{:S(2)}) collective-permute-start(f32[256,256]{1,0:T(8,128)S(1)} %collective-permute-done.11.mine), channel_id=1, source_target_pairs={{0,1},{1,0},{2,3},{3,2},{4,5},{5,4},{6,7},{7,6},{8,9},{9,8},{10,11... | collective-permute-start | bytes 786440 | tf_op jit(solution)/shard_map/ppermute | solution.py:487
  30.9 1.1 collective-permute-done.12.theirs
  32.1 3.2 %collective-permute-done.10.odd_ref = f32[2,256,256]{2,1,0:T(8,128)S(1)} collective-permute-done((f32[2,256,256]{2,1,0:T(8,128)S(1)}, f32[2,256,256]{2,1,0:T(8,128)S(1)}, u32[]{:S(2)}, u32[]{:S(2)}) %collective-permute-start.10) | collective-permute-done | bytes 524320 | tf_op jit(solution)/shard_map/ppermute | solution.py:487
  35.3 1.9 %collective-permute-done.9.even_ref = f32[2,256,256]{2,1,0:T(8,128)S(1)} collective-permute-done((f32[2,256,256]{2,1,0:T(8,128)S(1)}, f32[2,256,256]{2,1,0:T(8,128)S(1)}, u32[]{:S(2)}, u32[]{:S(2)}) %collective-permute-start.9) | collective-permute-done | bytes 524320 | tf_op jit(solution)/shard_map/ppermute | solution.py:487
  37.2 1.0 after_first.1
  38.2 7.6 %collective-permute-start.14 = (f32[2,256,256]{2,1,0:T(8,128)S(1)}, f32[2,256,256]{2,1,0:T(8,128)S(1)}, u32[]{:S(2)}, u32[]{:S(2)}) collective-permute-start(f32[2,256,256]{2,1,0:T(8,128)S(1)} %get-tuple-element.101.own.refs_1_.p2), channel_id=1, source_target_pairs={{0,510},{1,511},{2,4},{3,5},{4,2},{5,3},{6,8},{7,9},{8,6},{9,7},{1... | collective-permute-start | bytes 1572872 | tf_op jit(solution)/shard_map/ppermute | solution.py:487
  45.8 1.9 %collective-permute-start.13 = (f32[2,256,256]{2,1,0:T(8,128)S(1)}, f32[2,256,256]{2,1,0:T(8,128)S(1)}, u32[]{:S(2)}, u32[]{:S(2)}) collective-permute-start(f32[2,256,256]{2,1,0:T(8,128)S(1)} %get-tuple-element.101.own.refs_1_.p2), channel_id=1, source_target_pairs={{0,2},{1,3},{2,0},{3,1},{4,6},{5,7},{6,4},{7,5},{8,10},{9,11},{10,... | collective-permute-start | bytes 1572872 | tf_op jit(solution)/shard_map/ppermute | solution.py:487
  47.7 1.7 %before.3 = (f32[2,256,256]{2,1,0:T(8,128)S(1)}, f32[2,256,256]{2,1,0:T(8,128)S(1)}, f32[4,8,128]{2,1,0:T(8,128)S(1)}) custom-call(f32[8,256]{1,0:T(8,128)S(1)} %get-tuple-element.92.base_ref, f32[2,256,256]{2,1,0:T(8,128)S(1)} %get-tuple-element.101.own.refs_1_.p2, f32[2,256,256]{2,1,0:T(8,128)S(1)} %get-tuple-element.96.sites, ...), custom_call_target="tpu_custom_call" | custom-call | flops 4000000 | bytes 4000000 | tf_op jit(solution)/shard_map/before/pallas_call | solution.py:525
  49.5 6.9 %collective-permute-done.14.odd_ref = f32[2,256,256]{2,1,0:T(8,128)S(1)} collective-permute-done((f32[2,256,256]{2,1,0:T(8,128)S(1)}, f32[2,256,256]{2,1,0:T(8,128)S(1)}, u32[]{:S(2)}, u32[]{:S(2)}) %collective-permute-start.14) | collective-permute-done | bytes 524320 | tf_op jit(solution)/shard_map/ppermute | solution.py:487
  56.4 2.8 %collective-permute-done.13.even_ref = f32[2,256,256]{2,1,0:T(8,128)S(1)} collective-permute-done((f32[2,256,256]{2,1,0:T(8,128)S(1)}, f32[2,256,256]{2,1,0:T(8,128)S(1)}, u32[]{:S(2)}, u32[]{:S(2)}) %collective-permute-start.13) | collective-permute-done | bytes 524320 | tf_op jit(solution)/shard_map/ppermute | solution.py:487
  59.2 1.0 after.2
  60.2 5.7 %collective-permute-start.16 = (f32[2,256,256]{2,1,0:T(8,128)S(1)}, f32[2,256,256]{2,1,0:T(8,128)S(1)}, u32[]{:S(2)}, u32[]{:S(2)}) collective-permute-start(f32[2,256,256]{2,1,0:T(8,128)S(1)} %get-tuple-element.106.own.refs_1_), channel_id=1, source_target_pairs={{0,510},{1,511},{2,4},{3,5},{4,2},{5,3},{6,8},{7,9},{8,6},{9,7},{1... | collective-permute-start | bytes 1572872 | tf_op jit(solution)/shard_map/ppermute | solution.py:487
  65.9 1.9 %collective-permute-start.15 = (f32[2,256,256]{2,1,0:T(8,128)S(1)}, f32[2,256,256]{2,1,0:T(8,128)S(1)}, u32[]{:S(2)}, u32[]{:S(2)}) collective-permute-start(f32[2,256,256]{2,1,0:T(8,128)S(1)} %get-tuple-element.106.own.refs_1_), channel_id=1, source_target_pairs={{0,2},{1,3},{2,0},{3,1},{4,6},{5,7},{6,4},{7,5},{8,10},{9,11},{10,... | collective-permute-start | bytes 1572872 | tf_op jit(solution)/shard_map/ppermute | solution.py:487
  68.0 4.8 %collective-permute-start.19 = (f32[3,256,256]{2,1,0:T(8,128)S(1)}, f32[3,256,256]{2,1,0:T(8,128)S(1)}, u32[]{:S(2)}, u32[]{:S(2)}) collective-permute-start(f32[3,256,256]{2,1,0:T(8,128)S(1)} %swap.1), channel_id=1, source_target_pairs={{0,1},{1,0},{2,3},{3,2},{4,5},{5,4},{6,7},{7,6},{8,9},{9,8},{10,11... | collective-permute-start | bytes 2359304 | tf_op jit(solution)/shard_map/ppermute | solution.py:487
  72.7 1.7 %before.4 = (f32[2,256,256]{2,1,0:T(8,128)S(1)}, f32[2,256,256]{2,1,0:T(8,128)S(1)}, f32[4,8,128]{2,1,0:T(8,128)S(1)}) custom-call(f32[8,256]{1,0:T(8,128)S(1)} %get-tuple-element.92.base_ref, f32[2,256,256]{2,1,0:T(8,128)S(1)} %get-tuple-element.106.own.refs_1_, f32[2,256,256]{2,1,0:T(8,128)S(1)} %get-tuple-element.96.sites, ...), custom_call_target="tpu_custom_call" | custom-call | flops 4000000 | bytes 4000000 | tf_op jit(solution)/shard_map/before/pallas_call | solution.py:525
  74.5 3.7 %collective-permute-done.16.odd_ref = f32[2,256,256]{2,1,0:T(8,128)S(1)} collective-permute-done((f32[2,256,256]{2,1,0:T(8,128)S(1)}, f32[2,256,256]{2,1,0:T(8,128)S(1)}, u32[]{:S(2)}, u32[]{:S(2)}) %collective-permute-start.16) | collective-permute-done | bytes 524320 | tf_op jit(solution)/shard_map/ppermute | solution.py:487
  78.5 1.0 after.3
  79.5 5.7 %collective-permute-start.18 = (f32[2,256,256]{2,1,0:T(8,128)S(1)}, f32[2,256,256]{2,1,0:T(8,128)S(1)}, u32[]{:S(2)}, u32[]{:S(2)}) collective-permute-start(f32[2,256,256]{2,1,0:T(8,128)S(1)} %get-tuple-element.111.own), channel_id=1, source_target_pairs={{0,510},{1,511},{2,4},{3,5},{4,2},{5,3},{6,8},{7,9},{8,6},{9,7},{1... | collective-permute-start | bytes 1572872 | tf_op jit(solution)/shard_map/ppermute | solution.py:487
  85.2 1.9 %collective-permute-start.17 = (f32[2,256,256]{2,1,0:T(8,128)S(1)}, f32[2,256,256]{2,1,0:T(8,128)S(1)}, u32[]{:S(2)}, u32[]{:S(2)}) collective-permute-start(f32[2,256,256]{2,1,0:T(8,128)S(1)} %get-tuple-element.111.own), channel_id=1, source_target_pairs={{0,2},{1,3},{2,0},{3,1},{4,6},{5,7},{6,4},{7,5},{8,10},{9,11},{10,... | collective-permute-start | bytes 1572872 | tf_op jit(solution)/shard_map/ppermute | solution.py:487
  87.1 1.7 %before.5 = (f32[2,256,256]{2,1,0:T(8,128)S(1)}, f32[2,256,256]{2,1,0:T(8,128)S(1)}, f32[4,8,128]{2,1,0:T(8,128)S(1)}) custom-call(f32[8,256]{1,0:T(8,128)S(1)} %get-tuple-element.92.base_ref, f32[2,256,256]{2,1,0:T(8,128)S(1)} %get-tuple-element.111.own, f32[2,256,256]{2,1,0:T(8,128)S(1)} %get-tuple-element.96.sites, ...), custom_call_target="tpu_custom_call" | custom-call | flops 4000000 | bytes 4000000 | tf_op jit(solution)/shard_map/before/pallas_call | solution.py:525
  88.9 7.7 %collective-permute-done.18.odd_ref = f32[2,256,256]{2,1,0:T(8,128)S(1)} collective-permute-done((f32[2,256,256]{2,1,0:T(8,128)S(1)}, f32[2,256,256]{2,1,0:T(8,128)S(1)}, u32[]{:S(2)}, u32[]{:S(2)}) %collective-permute-start.18) | collective-permute-done | bytes 524320 | tf_op jit(solution)/shard_map/ppermute | solution.py:487
  96.8 1.1 after_last.1
  98.0 11.6 %all_to_all.10 = f32[32,1,128]{2,1,0:T(1,128)S(1)} all-to-all(f32[32,1,128]{2,1,0:T(1,128)S(1)} %broadcast_in_dim.30), channel_id=1, replica_groups=mesh['slab_0'=8,'slab_1'=4,'slab_2'=8,'slab_3'=2] {'slab_1','slab_2'}, dimensions={0} | all-to-all | bytes 32768 | tf_op jit(solution)/shard_map/all_to_all | solution.py:483
  110.3 11.4 %all-to-all-start.1 = ((f32[16,1,128]{2,1,0:T(1,128)}), f32[16,1,128]{2,1,0:T(1,128)S(1)}, u32[]{:S(2)}, u32[]{:S(2)}) async-start(f32[16,1,128]{2,1,0:T(1,128)} %broadcast_in_dim.31), calls=%async_computation.1 | async-start | bytes 16384 | tf_op jit(solution)/shard_map/all_to_all | solution.py:483
  121.6 7.0 %all-to-all-done.1 = f32[16,1,128]{2,1,0:T(1,128)S(1)} async-done(((f32[16,1,128]{2,1,0:T(1,128)}), f32[16,1,128]{2,1,0:T(1,128)S(1)}, u32[]{:S(2)}, u32[]{:S(2)}) %all-to-all-start.1) | async-done | bytes 8224 | tf_op jit(solution)/shard_map/all_to_all | solution.py:483
  128.6 2.5 %finish.1 = (f32[2,1,256,256]{3,2,1,0:T(8,128)}, f32[2,8]{1,0:T(2,128)S(1)}, f32[2,7]{1,0:T(2,128)S(1)}, f32[2,6]{1,0:T(2,128)S(1)}, s32[1]{0:T(128)}) custom-call(f32[8,256]{1,0:T(8,128)S(1)} %get-tuple-element.92.base_ref, f32[16,128]{1,0:T(8,128)S(1)} %bitcast.42, f32[2,1,256,256]{3,2,1,0:T(8,128)} %start.5, ...), custom_call_target="tpu_custom_call" | custom-call | flops 4000000 | bytes 4000000 | tf_op jit(solution)/shard_map/finish/pallas_call | solution.py:550
  (24 shorter events, 2.1 us)
Async XLA Ops:
  0.6 12.4 %copy-start = (f32[2,1,256,256]{3,2,1,0:T(8,128)S(1)}, f32[2,1,256,256]{3,2,1,0:T(8,128)}, u32[]{:S(2)}) copy-start(f32[2,1,256,256]{3,2,1,0:T(8,128)} %start.5) | copy-start | bytes 1572868
  2.3 10.7 %collective-permute-start.8 = (f32[2,256,256]{2,1,0:T(8,128)S(1)}, f32[2,256,256]{2,1,0:T(8,128)S(1)}, u32[]{:S(2)}, u32[]{:S(2)}) collective-permute-start(f32[2,256,256]{2,1,0:T(8,128)S(1)} %get-tuple-element.94), channel_id=1, source_target_pairs={{0,1},{1,0},{2,3},{3,2},{4,5},{5,4},{6,7},{7,6},{8,9},{9,8},{10,11... | collective-permute-start | bytes 1572872 | tf_op jit(solution)/shard_map/ppermute | solution.py:487
  11.0 16.2 %collective-permute-start.11 = (f32[256,256]{1,0:T(8,128)S(1)}, f32[256,256]{1,0:T(8,128)S(1)}, u32[]{:S(2)}, u32[]{:S(2)}) collective-permute-start(f32[256,256]{1,0:T(8,128)S(1)} %get-tuple-element.93.sites_here), channel_id=1, source_target_pairs={{0,511},{1,2},{2,1},{3,4},{4,3},{5,6},{6,5},{7,8},{8,7},{9,10},{10... | collective-permute-start | bytes 786440 | tf_op jit(solution)/shard_map/ppermute | solution.py:487
  13.1 22.2 %collective-permute-start.10 = (f32[2,256,256]{2,1,0:T(8,128)S(1)}, f32[2,256,256]{2,1,0:T(8,128)S(1)}, u32[]{:S(2)}, u32[]{:S(2)}) collective-permute-start(f32[2,256,256]{2,1,0:T(8,128)S(1)} %get-tuple-element.95.own.refs_1_), channel_id=1, source_target_pairs={{0,510},{1,511},{2,4},{3,5},{4,2},{5,3},{6,8},{7,9},{8,6},{9,7},{1... | collective-permute-start | bytes 1572872 | tf_op jit(solution)/shard_map/ppermute | solution.py:487
  23.5 13.6 %collective-permute-start.9 = (f32[2,256,256]{2,1,0:T(8,128)S(1)}, f32[2,256,256]{2,1,0:T(8,128)S(1)}, u32[]{:S(2)}, u32[]{:S(2)}) collective-permute-start(f32[2,256,256]{2,1,0:T(8,128)S(1)} %get-tuple-element.95.own.refs_1_), channel_id=1, source_target_pairs={{0,2},{1,3},{2,0},{3,1},{4,6},{5,7},{6,4},{7,5},{8,10},{9,11},{10,... | collective-permute-start | bytes 1572872 | tf_op jit(solution)/shard_map/ppermute | solution.py:487
  27.2 4.8 %collective-permute-start.12 = (f32[256,256]{1,0:T(8,128)S(1)}, f32[256,256]{1,0:T(8,128)S(1)}, u32[]{:S(2)}, u32[]{:S(2)}) collective-permute-start(f32[256,256]{1,0:T(8,128)S(1)} %collective-permute-done.11.mine), channel_id=1, source_target_pairs={{0,1},{1,0},{2,3},{3,2},{4,5},{5,4},{6,7},{7,6},{8,9},{9,8},{10,11... | collective-permute-start | bytes 786440 | tf_op jit(solution)/shard_map/ppermute | solution.py:487
  38.2 18.2 %collective-permute-start.14 = (f32[2,256,256]{2,1,0:T(8,128)S(1)}, f32[2,256,256]{2,1,0:T(8,128)S(1)}, u32[]{:S(2)}, u32[]{:S(2)}) collective-permute-start(f32[2,256,256]{2,1,0:T(8,128)S(1)} %get-tuple-element.101.own.refs_1_.p2), channel_id=1, source_target_pairs={{0,510},{1,511},{2,4},{3,5},{4,2},{5,3},{6,8},{7,9},{8,6},{9,7},{1... | collective-permute-start | bytes 1572872 | tf_op jit(solution)/shard_map/ppermute | solution.py:487
  45.8 13.4 %collective-permute-start.13 = (f32[2,256,256]{2,1,0:T(8,128)S(1)}, f32[2,256,256]{2,1,0:T(8,128)S(1)}, u32[]{:S(2)}, u32[]{:S(2)}) collective-permute-start(f32[2,256,256]{2,1,0:T(8,128)S(1)} %get-tuple-element.101.own.refs_1_.p2), channel_id=1, source_target_pairs={{0,2},{1,3},{2,0},{3,1},{4,6},{5,7},{6,4},{7,5},{8,10},{9,11},{10,... | collective-permute-start | bytes 1572872 | tf_op jit(solution)/shard_map/ppermute | solution.py:487
  60.2 18.0 %collective-permute-start.16 = (f32[2,256,256]{2,1,0:T(8,128)S(1)}, f32[2,256,256]{2,1,0:T(8,128)S(1)}, u32[]{:S(2)}, u32[]{:S(2)}) collective-permute-start(f32[2,256,256]{2,1,0:T(8,128)S(1)} %get-tuple-element.106.own.refs_1_), channel_id=1, source_target_pairs={{0,510},{1,511},{2,4},{3,5},{4,2},{5,3},{6,8},{7,9},{8,6},{9,7},{1... | collective-permute-start | bytes 1572872 | tf_op jit(solution)/shard_map/ppermute | solution.py:487
  65.9 12.5 %collective-permute-start.15 = (f32[2,256,256]{2,1,0:T(8,128)S(1)}, f32[2,256,256]{2,1,0:T(8,128)S(1)}, u32[]{:S(2)}, u32[]{:S(2)}) collective-permute-start(f32[2,256,256]{2,1,0:T(8,128)S(1)} %get-tuple-element.106.own.refs_1_), channel_id=1, source_target_pairs={{0,2},{1,3},{2,0},{3,1},{4,6},{5,7},{6,4},{7,5},{8,10},{9,11},{10,... | collective-permute-start | bytes 1572872 | tf_op jit(solution)/shard_map/ppermute | solution.py:487
  68.0 53.7 %collective-permute-start.19 = (f32[3,256,256]{2,1,0:T(8,128)S(1)}, f32[3,256,256]{2,1,0:T(8,128)S(1)}, u32[]{:S(2)}, u32[]{:S(2)}) collective-permute-start(f32[3,256,256]{2,1,0:T(8,128)S(1)} %swap.1), channel_id=1, source_target_pairs={{0,1},{1,0},{2,3},{3,2},{4,5},{5,4},{6,7},{7,6},{8,9},{9,8},{10,11... | collective-permute-start | bytes 2359304 | tf_op jit(solution)/shard_map/ppermute | solution.py:487
  79.5 17.1 %collective-permute-start.18 = (f32[2,256,256]{2,1,0:T(8,128)S(1)}, f32[2,256,256]{2,1,0:T(8,128)S(1)}, u32[]{:S(2)}, u32[]{:S(2)}) collective-permute-start(f32[2,256,256]{2,1,0:T(8,128)S(1)} %get-tuple-element.111.own), channel_id=1, source_target_pairs={{0,510},{1,511},{2,4},{3,5},{4,2},{5,3},{6,8},{7,9},{8,6},{9,7},{1... | collective-permute-start | bytes 1572872 | tf_op jit(solution)/shard_map/ppermute | solution.py:487
  85.2 11.7 %collective-permute-start.17 = (f32[2,256,256]{2,1,0:T(8,128)S(1)}, f32[2,256,256]{2,1,0:T(8,128)S(1)}, u32[]{:S(2)}, u32[]{:S(2)}) collective-permute-start(f32[2,256,256]{2,1,0:T(8,128)S(1)} %get-tuple-element.111.own), channel_id=1, source_target_pairs={{0,2},{1,3},{2,0},{3,1},{4,6},{5,7},{6,4},{7,5},{8,10},{9,11},{10,... | collective-permute-start | bytes 1572872 | tf_op jit(solution)/shard_map/ppermute | solution.py:487
  110.3 18.3 %all-to-all-start.1 = ((f32[16,1,128]{2,1,0:T(1,128)}), f32[16,1,128]{2,1,0:T(1,128)S(1)}, u32[]{:S(2)}, u32[]{:S(2)}) async-start(f32[16,1,128]{2,1,0:T(1,128)} %broadcast_in_dim.31), calls=%async_computation.1 | async-start | bytes 16384 | tf_op jit(solution)/shard_map/all_to_all | solution.py:483
  128.6 3.2 %copy-start.1 = (f32[2,1,256,256]{3,2,1,0:T(8,128)S(1)}, f32[2,1,256,256]{3,2,1,0:T(8,128)}, u32[]{:S(2)}) copy-start(f32[2,1,256,256]{3,2,1,0:T(8,128)} %start.5) | copy-start | bytes 1572868
  128.6 3.2 %copy-start.6 = (f32[16]{0:T(128)S(1)}, f32[16]{0:T(128)}, u32[]{:S(2)}) copy-start(f32[16]{0:T(128)} %param.9) | copy-start | bytes 196
  131.8 0.6 copy-start.7
  131.8 0.6 copy-start.8
  131.8 0.6 copy-start.9

commit v5 on v3

--- a/solution.py
+++ b/solution.py
@@ -11,12 +11,11 @@
 LANCZOS = 8
 SLAB = ("slab_0", "slab_1", "slab_2", "slab_3")
 STAGES = (("slab_1", "slab_2"), ("slab_0", "slab_3"))
-ROWS = 32
+ROWS = 64
 NUDGE = 1e-3
 ROUNDING = 2e-7
 TOLERANCE = 1e-4
 VMEM = pl.BlockSpec(memory_space=pltpu.VMEM)
-SMEM = pl.BlockSpec(memory_space=pltpu.SMEM)
 PARAMS = pltpu.CompilerParams(vmem_limit_bytes=24 * 1024 * 1024)
 
 
@@ -130,9 +129,7 @@
         kernel,
         out_shape=out_shape,
         in_specs=in_specs,
-        out_specs=jax.tree.map(
-            lambda leaf: SMEM if leaf.dtype == jnp.int32 else VMEM, out_shape
-        ),
+        out_specs=jax.tree.map(lambda leaf: VMEM, out_shape),
         scratch_shapes=scratch,
         compiler_params=PARAMS,
         cost_estimate=PAIR_COST,
@@ -140,10 +137,18 @@
     )
 
 
-def onsite_kernel(energies_ref, levels_ref, out_ref, base_ref):
-    count = energies_ref.shape[0]
-    row = jnp.zeros((1, 256), jnp.float32)
-    values = [row + energies_ref[index] for index in range(count)]
+def sides():
+    parity = lax.axis_index(SLAB[2]) % 2
+    core = lax.axis_index(SLAB[3])
+    return parity, core, jnp.where(core == parity, 0, 1)
+
+
+def onsite_kernel(energies_ref, levels_ref, start, out_ref, send_ref, base_ref):
+    count = energies_ref.shape[1]
+    values = [
+        jnp.broadcast_to(energies_ref[0:1, index : index + 1], (1, 256))
+        for index in range(count)
+    ]
     mean = functools.reduce(jnp.add, values) * (1.0 / count)
     spread = functools.reduce(jnp.add, [jnp.square(v - mean) for v in values])
     scale = 1.05 * jnp.sqrt(6.0 + spread * (1.0 / count))
@@ -151,8 +156,8 @@
     base_ref[0:1] = mean
     base_ref[1:2] = inverse
     base_ref[2:3] = scale
-    base_ref[3:4] = inverse * inverse
     values = [(v - mean) * inverse for v in values]
+    core = lax.axis_index(SLAB[3])
 
     def rows_of(chunk, carry):
         rows = pl.ds(chunk * ROWS, ROWS)
@@ -161,6 +166,9 @@
         for index in range(count):
             value = jnp.where(level == index, values[index], value)
         out_ref[0, rows] = value
+        out_ref[1, rows] = start[core, 0, rows]
+        send_ref[1, rows] = value
+        send_ref[0, rows] = start[1 - core, 0, rows]
         return carry
 
     lax.fori_loop(0, CHUNKS, rows_of, 0)
@@ -187,131 +195,132 @@
     return lax.fori_loop(0, CHUNKS, body, (zero,) * count)
 
 
-def before_kernel(first, base_ref, own, sites, *refs):
-    if first:
-        first_ref, second_ref, sums = refs
+def partial(fields, sites, prior, inverse):
+    def body(chunk, carry):
+        rows = pl.ds(chunk * ROWS, ROWS)
+        for s in range(2):
+            beside, middle = in_plane(fields[s].at[0], chunk)
+            value = sites[s, rows] * middle - inverse * (beside + fields[1 - s][0, rows])
+            if prior is not None:
+                value = value - prior[s, rows]
+            fields[s][1, rows] = value
+        return carry
+
+    chunks(body, 0)
+
+
+def assemble_kernel(base_ref, here_ref, received, across_ref, inside_ref, sites_ref):
+    mine = sides()[2]
+
+    def body(chunk, carry):
+        rows = pl.ds(chunk * ROWS, ROWS)
+        kept, taken = here_ref[1, rows], received[0, rows]
+        across_ref[0, rows] = jnp.where(mine == 0, kept, taken)
+        inside_ref[0, rows] = jnp.where(mine == 0, taken, kept)
+        sites_ref[mine, rows] = here_ref[0, rows]
+        sites_ref[1 - mine, rows] = received[1, rows]
+        return carry
+
+    chunks(body, 0)
+    partial((across_ref, inside_ref), sites_ref, None, base_ref[1:2])
+
+
+def round_kernel(last, base_ref, across, inside, from_across, from_inside, sites, *refs):
+    if last:
+        parts, row_ref, one = refs[:3], refs[3], refs[4]
     else:
-        prior, older, first_ref, second_ref, sums = refs
+        one, new_across, new_inside = refs
+        fields = (new_across, new_inside)
+    own, got = (across, inside), (from_across, from_inside)
     inverse = base_ref[1:2]
 
-    def once(chunk, carry):
-        rows = pl.ds(chunk * ROWS, ROWS)
-        for j in range(2):
-            beside, middle = in_plane(own.at[j], chunk)
-            value = sites[j, rows] * middle - inverse * (beside + own[1 - j, rows])
+    def first(chunk, carry):
+        rows = pl.ds(chunk * ROWS, ROWS)
+        for s in range(2):
+            value = own[s][1, rows] - inverse * got[s][0, rows]
+            one[s, rows] = value
+            if last:
+                carry = (
+                    carry[0] + folded(value * own[s][0, rows]),
+                    carry[1] + folded(value * value),
+                )
+        return carry
+
+    totals = chunks(first, 2 if last else 0)
+
+    def second(chunk, carry):
+        rows = pl.ds(chunk * ROWS, ROWS)
+        for s in range(2):
+            beside, middle = in_plane(one.at[s], chunk)
+            field = own[s][0, rows]
+            edge = got[s][1, rows] - inverse * field
+            beside = beside + (one[1 - s, rows] + edge)
+            value = sites[s, rows] * middle - inverse * beside - field
+            if last:
+                carry = (carry[0] + folded(value * middle),)
+            else:
+                fields[s][0, rows] = value
+        return carry
+
+    final = chunks(second, 1 if last else 0)
+    if last:
+        pack(parts, tuple(totals) + tuple(final), row_ref)
+    else:
+        partial(fields, sites, one, inverse)
+
+
+def sums_kernel(first, across, inside, one, new_across, new_inside, sums):
+    old, new = (across, inside), (new_across, new_inside)
+
+    def body(chunk, carry):
+        rows = pl.ds(chunk * ROWS, ROWS)
+        for s in range(2):
+            field, value, later = old[s][0, rows], one[s, rows], new[s][0, rows]
+            terms = [value * field, value * value, later * value, later * later]
             if first:
-                carry = (carry[0] + folded(middle * middle),)
-            else:
-                last = prior[j, rows]
-                value = value - last
-                carry = (
-                    carry[0] + folded(last * older[j, rows]),
-                    carry[1] + folded(last * last),
-                    carry[2] + folded(middle * last),
-                    carry[3] + folded(middle * middle),
-                )
-            first_ref[j, rows] = value
-        return carry
-
-    totals = chunks(once, 1 if first else 4)
-
-    def twice(chunk, carry):
-        rows = pl.ds(chunk * ROWS, ROWS)
-        for j in range(2):
-            beside, middle = in_plane(first_ref.at[j], chunk)
-            beside = beside + first_ref[1 - j, rows]
-            second_ref[j, rows] = sites[j, rows] * middle - inverse * beside - own[j, rows]
-        return carry
-
-    chunks(twice, 0)
-    for index, total in enumerate(totals):
+                terms.append(field * field)
+            carry = tuple(c + folded(t) for c, t in zip(carry, terms))
+        return carry
+
+    for index, total in enumerate(chunks(body, 5 if first else 4)):
         sums[index] = total
 
 
-def after_kernel(first, last, side_ref, base_ref, even_ref, odd_ref, own, sites, one, two, *refs):
-    refs = list(refs)
-    if not first:
-        edge_sites, edge_prior = refs[:2]
-        refs = refs[2:]
-    if last:
-        parts, row_ref = refs[:4], refs[4]
-    else:
-        new_one, new_two, new_edge = refs[:3]
-        kept = refs[3] if first else None
-    inverse, inverse2 = base_ref[1:2], base_ref[3:4]
-
-    def run(low, high):
-        def body(chunk, carry):
-            rows = pl.ds(chunk * ROWS, ROWS)
-            near, far = (low.at[1], high.at[0]), (low.at[0], high.at[1])
-            found = [in_plane(plane, chunk) for plane in near]
-            for j in range(2):
-                beside, middle = found[j]
-                if first:
-                    site = (low if j == 0 else high)[2, rows]
-                    kept[j, rows] = site
-                else:
-                    site = edge_sites[j, rows]
-                mine = own[j, rows]
-                edge = site * middle - inverse * (beside + far[j][rows] + mine)
-                if not first:
-                    edge = edge - edge_prior[j, rows]
-                value = one[j, rows] - inverse * middle
-                new = two[j, rows] - inverse * (sites[j, rows] * middle + edge)
-                new = new + inverse2 * (beside + found[1 - j][1])
-                if last:
-                    carry = (
-                        carry[0] + folded(value * mine),
-                        carry[1] + folded(value * value),
-                        carry[2] + folded(new * value),
-                    )
-                else:
-                    new_one[j, rows] = value
-                    new_two[j, rows] = new
-                    new_edge[j, rows] = edge
-            return carry
-
-        totals = chunks(body, 3 if last else 0)
-        if last:
-            pack(parts, totals, row_ref)
-
-    @pl.when(side_ref[1] == 0)
-    def _():
-        run(odd_ref, even_ref)
-
-    @pl.when(side_ref[1] == 1)
-    def _():
-        run(even_ref, odd_ref)
-
-
 def pack(parts, totals, row_ref):
-    entries = [(0, parts[0][0])]
+    entries = [(0, parts[0][4])]
     for index in range(3):
         places = (8 + 2 * index, 2 * index + 1, 9 + 2 * index, 2 * index + 2)
-        entries += [(place, parts[index + 1][k]) for k, place in enumerate(places)]
+        entries += [(place, parts[index][k]) for k, place in enumerate(places)]
     entries += list(zip((14, 7, 15), totals))
     lane = lax.broadcasted_iota(jnp.int32, (1, 128), 1)
     row = jnp.zeros((1, 128), jnp.float32)
     for place, value in entries:
         total = jnp.sum(jnp.sum(value, axis=0, keepdims=True), axis=1, keepdims=True)
         row = jnp.where(lane == place, total, row)
-    row_ref[...] = row
-
-
-def swap_kernel(side_ref, p1, p2, p3, out_ref):
-    other = 1 - side_ref[0]
+    row_ref[...] = jnp.broadcast_to(row, row_ref.shape)
+
+
+def total_kernel(rows_ref, out_ref):
+    total = jnp.sum(rows_ref[...], axis=0, keepdims=True)
+    out_ref[...] = jnp.broadcast_to(total, out_ref.shape)
+
+
+def swap_kernel(p0_across, p0_inside, p1, p2_across, p2_inside, p3, out_ref):
+    other = 1 - sides()[2]
 
     def body(chunk, carry):
         rows = pl.ds(chunk * ROWS, ROWS)
-        for index, ref in enumerate((p1, p2, p3)):
-            out_ref[index, rows] = ref[other, rows]
+        out_ref[0, rows] = jnp.where(other == 0, p0_across[0, rows], p0_inside[0, rows])
+        out_ref[1, rows] = p1[other, rows]
+        out_ref[2, rows] = jnp.where(other == 0, p2_across[0, rows], p2_inside[0, rows])
+        out_ref[3, rows] = p3[other, rows]
         return carry
 
     chunks(body, 0)
 
 
 def finish_kernel(
-    side_ref, base_ref, rows_ref, start, p1, p2, p3, swapped,
+    base_ref, rows_ref, p0_across, p0_inside, p1, p2_across, p2_inside, p3, swapped,
     field_ref, diag_ref, offd_ref, moments_ref, good_ref,
 ):
     shift, scale = base_ref[0:1, :128], base_ref[2:3, :128]
@@ -377,7 +386,7 @@
         return jnp.where(error <= allowed * allowed * norm, 1, 0)
 
     fits = jnp.minimum(spread(alphas), spread(betas))
-    good_ref[0] = jnp.min(fits)
+    good_ref[...] = jnp.broadcast_to(fits[0:1], good_ref.shape)
 
     lows, highs = [], []
     for k in range(LANCZOS):
@@ -427,32 +436,32 @@
     offd_ref[...] = offd[:, :7]
     moments_ref[...] = out[:, :6]
 
-    here = side_ref[0]
+    _, core, side = sides()
     wide = [
         jnp.concatenate([jnp.broadcast_to(terms[3][l][:, :1], lane.shape)] * 2, axis=1)
         for l in range(4)
     ]
-    mine = [jnp.where(here == 1, w[1:2], w[0:1]) for w in wide]
-    other = [jnp.where(here == 1, w[0:1], w[1:2]) for w in wide]
+    mine = [jnp.where(core == 1, w[1:2], w[0:1]) for w in wide]
+    other = [jnp.where(core == 1, w[0:1], w[1:2]) for w in wide]
 
     def combine(chunk, carry):
         at = pl.ds(chunk * ROWS, ROWS)
-        value = mine[0] * start[here, 0, at]
-        for l, ref in enumerate((p1, p2, p3)):
-            value = value + mine[l + 1] * ref[here, at]
-        field_ref[here, 0, at] = value
-        value = other[0] * start[1 - here, 0, at]
-        for l in range(3):
-            value = value + other[l + 1] * swapped[l, at]
-        field_ref[1 - here, 0, at] = value
+        p2 = jnp.where(side == 0, p2_across[0, at], p2_inside[0, at])
+        p0 = jnp.where(side == 0, p0_across[0, at], p0_inside[0, at])
+        value = mine[0] * p0 + mine[1] * p1[side, at]
+        field_ref[core, 0, at] = value + mine[2] * p2 + mine[3] * p3[side, at]
+        value = other[0] * swapped[0, at]
+        for l in range(1, 4):
+            value = value + other[l] * swapped[l, at]
+        field_ref[1 - core, 0, at] = value
         return carry
 
     chunks(combine, 0)
 
 
-def gathered(row, axes, count):
-    copies = jnp.broadcast_to(row[None], (count,) + row.shape)
-    return lax.all_to_all(copies, axes, 0, 0, tiled=True).reshape(count, 128)
+def gathered(copies, axes):
+    count = copies.shape[0]
+    return lax.all_to_all(copies[:, None], axes, 0, 0, tiled=True).reshape(count, 128)
 
 
 def exchange(block, route):
@@ -464,67 +473,56 @@
     inside = [(i, i ^ 2) for i in range(devices)]
     across = [(i, (((i + 2) ^ 2) - 2) % devices) for i in range(devices)]
     partner = [(i, i ^ 1) for i in range(devices)]
-    core = lax.axis_index("slab_3").astype(jnp.int32)
-    parity = lax.axis_index("slab_2").astype(jnp.int32) % 2
-    side = jnp.stack([core, parity])
-
-    sites_here, base = call(
-        onsite_kernel, (shape(1, 256, 256), shape(8, 256)), [SMEM, VMEM], "onsite"
-    )(energies, levels)
-    own = lax.all_to_all(start_vectors, "slab_3", 0, 1, tiled=True)[0]
-    sites = lax.all_gather(sites_here, "slab_3", axis=0, tiled=True)
-    top, bottom = sites[1:2], sites[0:1]
-    even = jnp.concatenate([own, jnp.where(parity == 0, top, bottom)], axis=0)
-    odd = jnp.concatenate([own, jnp.where(parity == 0, bottom, top)], axis=0)
-    even, odd = exchange(even, inside), exchange(odd, across)
-    one, two, part = call(
-        functools.partial(before_kernel, True),
-        (PLANES, PLANES, shape(1, 8, 128)), [VMEM] * 3, "before_first",
-    )(base, own, sites)
-    parts = [part]
-    ones, twos = [], [own]
-    one, two, edge, edge_sites = call(
-        functools.partial(after_kernel, True, False),
-        (PLANES,) * 4, [SMEM] + [VMEM] * 7, "after_first",
-    )(side, base, even, odd, own, sites, one, two)
+
+    def pair(left, right):
+        return exchange(left, across), exchange(right, inside)
+
+    here, send, base = call(
+        onsite_kernel, (PLANES, PLANES, shape(8, 256)), [VMEM] * 3, "onsite"
+    )(energies.reshape(1, -1), levels, start_vectors)
+    left, right, sites = call(assemble_kernel, (PLANES,) * 3, [VMEM] * 3, "assemble")(
+        base, here, exchange(send, partner)
+    )
+    parts, ones, twos = [], [], [(left, right)]
     swapped = None
-    for step in range(1, 4):
-        ones.append(one)
-        twos.append(two)
-        even, odd = exchange(two, inside), exchange(two, across)
-        one, two, part = call(
-            functools.partial(before_kernel, False),
-            (PLANES, PLANES, shape(4, 8, 128)), [VMEM] * 5, "before",
-        )(base, twos[-1], sites, ones[-1], twos[-2])
-        parts.append(part)
+    for step in range(3):
+        got = pair(left, right)
+        if step:
+            parts.append(summed)
         if step == 2:
             swapped = exchange(
-                call(swap_kernel, shape(3, 256, 256), [SMEM] + [VMEM] * 3, "swap")(
-                    side, ones[0], twos[1], ones[1]
+                call(swap_kernel, shape(4, 256, 256), [VMEM] * 6, "swap")(
+                    *twos[0], ones[0], *twos[1], ones[1]
                 ),
                 partner,
             )
-        operands = (side, base, even, odd, twos[-1], sites, one, two, edge_sites, edge)
-        if step < 3:
-            one, two, edge = call(
-                functools.partial(after_kernel, False, False),
-                (PLANES,) * 3, [SMEM] + [VMEM] * 9, "after",
-            )(*operands)
-        else:
-            row = call(
-                functools.partial(after_kernel, False, True),
-                shape(1, 128), [SMEM] + [VMEM] * 13, "after_last",
-            )(*operands, *parts)
-    rows = gathered(row, STAGES[0], 32)
-    rows = gathered(jnp.sum(rows, axis=0, keepdims=True), STAGES[1], 16)
+        one, new_left, new_right = call(
+            functools.partial(round_kernel, False), (PLANES,) * 3, [VMEM] * 6, "round"
+        )(base, left, right, *got, sites)
+        summed = call(
+            functools.partial(sums_kernel, step == 0),
+            shape(5 if step == 0 else 4, 8, 128), [VMEM] * 5, "sums",
+        )(left, right, one, new_left, new_right)
+        ones.append(one)
+        left, right = new_left, new_right
+        twos.append((left, right))
+    parts.append(summed)
+    got = pair(left, right)
+    rows = call(
+        functools.partial(round_kernel, True),
+        shape(32, 128), [VMEM] * 9, "round_last", [pltpu.VMEM((2, 256, 256), jnp.float32)],
+    )(base, left, right, *got, sites, *parts)
+    rows = gathered(rows, STAGES[0])
+    rows = call(total_kernel, shape(16, 128), [VMEM], "total")(rows)
+    rows = gathered(rows, STAGES[1])
     field, diag, offd, moments, good = call(
         finish_kernel,
         (
             shape(2, 1, 256, 256), shape(2, 8), shape(2, 7), shape(2, 6),
-            jax.ShapeDtypeStruct((1,), jnp.int32),
+            jax.ShapeDtypeStruct((1, 128), jnp.int32),
         ),
-        [SMEM] + [VMEM] * 7, "finish",
-    )(side, base, rows, start_vectors, ones[0], twos[1], ones[1], swapped)
+        [VMEM] * 9, "finish",
+    )(base, rows, *twos[0], ones[0], *twos[1], ones[1], swapped)
 
     def accept(field, diag, offd, moments, *_):
         return (field, diag, offd, moments)
@@ -533,7 +531,7 @@
         return stepwise(*inputs)
 
     return lax.cond(
-        good[0] == 1, accept, redo,
+        good[0, 0] == 1, accept, redo,
         field, diag, offd, moments, start_vectors, levels, energies,
     )
 

time: 143 us -> 132 us (0.923)
  Pallas kernels: 18 us -> 11.9 us
  blocking collectives: 13.8 us -> 11.6 us
  other arithmetic: 1.43 us -> 0 us
    all_to_all x2 -> x1, starting transfers between devices: 19.6 us -> 9.37 us  [gathered(): lax.all_to_all(copies[:, None], axes, 0, 0, tiled=True).reshape(count, 128)]
    ppermute x9 -> x10, starting transfers between devices: 39.1 us -> 48.2 us  [exchange(): return lax.ppermute(block, SLAB, route)]
    pallas_call x10 -> x11, Pallas kernels: 15.4 us -> 9.33 us  [the longest x3 3.89 us: shards(): call(functools.partial(round_kernel, False), (PLANES,) * 3, [VMEM] * 6, '...]
    all_gather x1 -> x0, blocking collectives: 2.18 us -> none  [shards(): sites = lax.all_gather(sites_here, 'slab_3', axis=0, tiled=True)]
    ppermute x9 -> x10, waiting for transfers between devices: 41.2 us -> 41.5 us  [exchange(): return lax.ppermute(block, SLAB, route)]
    all_to_all x2 -> x1, waiting for transfers between devices: 6.97 us -> 6.96 us  [gathered(): lax.all_to_all(copies[:, None], axes, 0, 0, tiled=True).reshape(count, 128)]
  transfers between devices with their start and end apart: 11 -> 11, of which waited for: 9 -> 10; matrix products, arithmetic and copies ran while one was open for 1% -> 0% of each run, Pallas kernels for 8% -> 3%
where the time goes in v5:
time: 132 us; the launch traced here: 131 us
  starting transfers between devices  57.6 us (44%)
  waiting for transfers between devices  48.5 us (37%)
  Pallas kernels  11.9 us (9%)
  blocking collectives  11.6 us (9%)
    ppermute x10, starting transfers between devices, exchange(): return lax.ppermute(block, SLAB, route)  48.2 us
    ppermute x10, waiting for transfers between devices, exchange(): return lax.ppermute(block, SLAB, route)  41.5 us
    all_to_all x1, blocking collectives, gathered(): lax.all_to_all(copies[:, None], axes, 0, 0, tiled=True).reshape(count, 128)  11.6 us
    all_to_all x1, starting transfers between devices, gathered(): lax.all_to_all(copies[:, None], axes, 0, 0, tiled=True).reshape(count, 128)  9.37 us
    all_to_all x1, waiting for transfers between devices, gathered(): lax.all_to_all(copies[:, None], axes, 0, 0, tiled=True).reshape(count, 128)  6.96 us
    pallas_call x3, Pallas kernels, shards(): call(functools.partial(round_kernel, False), (PLANES,) * 3, [VMEM] * 6, '...  3.89 us
  transfers between devices with their start and end apart: 11, of which 10 were waited for; matrix products, arithmetic and copies ran while one was open for 0% of the time, Pallas kernels for 3%

profile of v5, /device:TPU:1, one launch (start us, length us, event | category | flops | bytes accessed | tf_op | source)
XLA Modules:
  0.0 131.1 jit_solution(12692759387055934112)
XLA Ops:
  0.6 1.6 %onsite.1 = (f32[2,256,256]{2,1,0:T(8,128)S(1)}, f32[2,256,256]{2,1,0:T(8,128)S(1)}, f32[8,256]{1,0:T(8,128)S(1)}) custom-call(f32[1,16]{1,0:T(1,128)} %bitcast.60, s32[1,256,256]{2,1,0:T(8,128)} %levels_ref.1, f32[2,1,256,256]{3,2,1,0:T(8,128)} %start.1), custom_call_target="tpu_custom_call" | custom-call | flops 4000000 | bytes 4000000 | tf_op jit(solution)/shard_map/onsite/pallas_call | solution.py:480
  2.2 8.7 %collective-permute-start.8 = (f32[2,256,256]{2,1,0:T(8,128)S(1)}, f32[2,256,256]{2,1,0:T(8,128)S(1)}, u32[]{:S(2)}, u32[]{:S(2)}) collective-permute-start(f32[2,256,256]{2,1,0:T(8,128)S(1)} %get-tuple-element.81), channel_id=1, source_target_pairs={{0,1},{1,0},{2,3},{3,2},{4,5},{5,4},{6,7},{7,6},{8,9},{9,8},{10,11... | collective-permute-start | bytes 1572872 | tf_op jit(solution)/shard_map/ppermute | solution.py:468
  11.0 1.5 %collective-permute-done.8.received = f32[2,256,256]{2,1,0:T(8,128)S(1)} collective-permute-done((f32[2,256,256]{2,1,0:T(8,128)S(1)}, f32[2,256,256]{2,1,0:T(8,128)S(1)}, u32[]{:S(2)}, u32[]{:S(2)}) %collective-permute-start.8) | collective-permute-done | bytes 524320 | tf_op jit(solution)/shard_map/ppermute | solution.py:468
  12.5 0.7 assemble.1
  13.1 10.4 %collective-permute-start.9 = (f32[2,256,256]{2,1,0:T(8,128)S(1)}, f32[2,256,256]{2,1,0:T(8,128)S(1)}, u32[]{:S(2)}, u32[]{:S(2)}) collective-permute-start(f32[2,256,256]{2,1,0:T(8,128)S(1)} %get-tuple-element.82.across.p0_across), channel_id=1, source_target_pairs={{0,510},{1,511},{2,4},{3,5},{4,2},{5,3},{6,8},{7,9},{8,6},{9,7},{1... | collective-permute-start | bytes 1572872 | tf_op jit(solution)/shard_map/ppermute | solution.py:468
  23.6 1.9 %collective-permute-start.10 = (f32[2,256,256]{2,1,0:T(8,128)S(1)}, f32[2,256,256]{2,1,0:T(8,128)S(1)}, u32[]{:S(2)}, u32[]{:S(2)}) collective-permute-start(f32[2,256,256]{2,1,0:T(8,128)S(1)} %get-tuple-element.83.inside.p0_inside), channel_id=1, source_target_pairs={{0,2},{1,3},{2,0},{3,1},{4,6},{5,7},{6,4},{7,5},{8,10},{9,11},{10,... | collective-permute-start | bytes 1572872 | tf_op jit(solution)/shard_map/ppermute | solution.py:468
  25.5 10.0 %collective-permute-done.9.from_across = f32[2,256,256]{2,1,0:T(8,128)S(1)} collective-permute-done((f32[2,256,256]{2,1,0:T(8,128)S(1)}, f32[2,256,256]{2,1,0:T(8,128)S(1)}, u32[]{:S(2)}, u32[]{:S(2)}) %collective-permute-start.9) | collective-permute-done | bytes 524320 | tf_op jit(solution)/shard_map/ppermute | solution.py:468
  35.5 2.8 %collective-permute-done.10.from_inside = f32[2,256,256]{2,1,0:T(8,128)S(1)} collective-permute-done((f32[2,256,256]{2,1,0:T(8,128)S(1)}, f32[2,256,256]{2,1,0:T(8,128)S(1)}, u32[]{:S(2)}, u32[]{:S(2)}) %collective-permute-start.10) | collective-permute-done | bytes 524320 | tf_op jit(solution)/shard_map/ppermute | solution.py:468
  38.3 1.3 round.3
  39.6 5.7 %collective-permute-start.11 = (f32[2,256,256]{2,1,0:T(8,128)S(1)}, f32[2,256,256]{2,1,0:T(8,128)S(1)}, u32[]{:S(2)}, u32[]{:S(2)}) collective-permute-start(f32[2,256,256]{2,1,0:T(8,128)S(1)} %get-tuple-element.85.across.new_across.p2_across), channel_id=1, source_target_pairs={{0,510},{1,511},{2,4},{3,5},{4,2},{5,3},{6,8},{7,9},{8,6},{9,7},{1... | collective-permute-start | bytes 1572872 | tf_op jit(solution)/shard_map/ppermute | solution.py:468
  45.3 1.9 %collective-permute-start.12 = (f32[2,256,256]{2,1,0:T(8,128)S(1)}, f32[2,256,256]{2,1,0:T(8,128)S(1)}, u32[]{:S(2)}, u32[]{:S(2)}) collective-permute-start(f32[2,256,256]{2,1,0:T(8,128)S(1)} %get-tuple-element.86.inside.new_inside.p2_inside), channel_id=1, source_target_pairs={{0,2},{1,3},{2,0},{3,1},{4,6},{5,7},{6,4},{7,5},{8,10},{9,11},{10,... | collective-permute-start | bytes 1572872 | tf_op jit(solution)/shard_map/ppermute | solution.py:468
  47.2 11.6 %collective-permute-done.11.from_across = f32[2,256,256]{2,1,0:T(8,128)S(1)} collective-permute-done((f32[2,256,256]{2,1,0:T(8,128)S(1)}, f32[2,256,256]{2,1,0:T(8,128)S(1)}, u32[]{:S(2)}, u32[]{:S(2)}) %collective-permute-start.11) | collective-permute-done | bytes 524320 | tf_op jit(solution)/shard_map/ppermute | solution.py:468
  58.9 0.3 collective-permute-done.12.from_inside
  59.2 1.3 round.4
  60.5 5.7 %collective-permute-start.13 = (f32[2,256,256]{2,1,0:T(8,128)S(1)}, f32[2,256,256]{2,1,0:T(8,128)S(1)}, u32[]{:S(2)}, u32[]{:S(2)}) collective-permute-start(f32[2,256,256]{2,1,0:T(8,128)S(1)} %get-tuple-element.87.across.new_across), channel_id=1, source_target_pairs={{0,510},{1,511},{2,4},{3,5},{4,2},{5,3},{6,8},{7,9},{8,6},{9,7},{1... | collective-permute-start | bytes 1572872 | tf_op jit(solution)/shard_map/ppermute | solution.py:468
  66.2 1.9 %collective-permute-start.14 = (f32[2,256,256]{2,1,0:T(8,128)S(1)}, f32[2,256,256]{2,1,0:T(8,128)S(1)}, u32[]{:S(2)}, u32[]{:S(2)}) collective-permute-start(f32[2,256,256]{2,1,0:T(8,128)S(1)} %get-tuple-element.88.inside.new_inside), channel_id=1, source_target_pairs={{0,2},{1,3},{2,0},{3,1},{4,6},{5,7},{6,4},{7,5},{8,10},{9,11},{10,... | collective-permute-start | bytes 1572872 | tf_op jit(solution)/shard_map/ppermute | solution.py:468
  68.1 1.1 swap.1
  69.2 4.3 %collective-permute-start.17 = (f32[4,256,256]{2,1,0:T(8,128)}, f32[4,256,256]{2,1,0:T(8,128)}, u32[]{:S(2)}, u32[]{:S(2)}) collective-permute-start(f32[4,256,256]{2,1,0:T(8,128)} %swap.1), channel_id=1, source_target_pairs={{0,1},{1,0},{2,3},{3,2},{4,5},{5,4},{6,7},{7,6},{8,9},{9,8},{10,11... | collective-permute-start | bytes 3145736 | tf_op jit(solution)/shard_map/ppermute | solution.py:468
  73.5 5.4 %collective-permute-done.13.from_across = f32[2,256,256]{2,1,0:T(8,128)S(1)} collective-permute-done((f32[2,256,256]{2,1,0:T(8,128)S(1)}, f32[2,256,256]{2,1,0:T(8,128)S(1)}, u32[]{:S(2)}, u32[]{:S(2)}) %collective-permute-start.13) | collective-permute-done | bytes 524320 | tf_op jit(solution)/shard_map/ppermute | solution.py:468
  78.9 0.3 collective-permute-done.14.from_inside
  79.2 1.3 round.5
  80.5 5.7 %collective-permute-start.15 = (f32[2,256,256]{2,1,0:T(8,128)S(1)}, f32[2,256,256]{2,1,0:T(8,128)S(1)}, u32[]{:S(2)}, u32[]{:S(2)}) collective-permute-start(f32[2,256,256]{2,1,0:T(8,128)S(1)} %get-tuple-element.89.new_across.across), channel_id=1, source_target_pairs={{0,510},{1,511},{2,4},{3,5},{4,2},{5,3},{6,8},{7,9},{8,6},{9,7},{1... | collective-permute-start | bytes 1572872 | tf_op jit(solution)/shard_map/ppermute | solution.py:468
  86.2 1.9 %collective-permute-start.16 = (f32[2,256,256]{2,1,0:T(8,128)S(1)}, f32[2,256,256]{2,1,0:T(8,128)S(1)}, u32[]{:S(2)}, u32[]{:S(2)}) collective-permute-start(f32[2,256,256]{2,1,0:T(8,128)S(1)} %get-tuple-element.90.new_inside.inside), channel_id=1, source_target_pairs={{0,2},{1,3},{2,0},{3,1},{4,6},{5,7},{6,4},{7,5},{8,10},{9,11},{10,... | collective-permute-start | bytes 1572872 | tf_op jit(solution)/shard_map/ppermute | solution.py:468
  88.8 9.3 %collective-permute-done.15.from_across = f32[2,256,256]{2,1,0:T(8,128)S(1)} collective-permute-done((f32[2,256,256]{2,1,0:T(8,128)S(1)}, f32[2,256,256]{2,1,0:T(8,128)S(1)}, u32[]{:S(2)}, u32[]{:S(2)}) %collective-permute-start.15) | collective-permute-done | bytes 524320 | tf_op jit(solution)/shard_map/ppermute | solution.py:468
  98.1 0.3 collective-permute-done.16.from_inside
  98.4 0.9 round_last.1
  99.3 11.6 %all_to_all.10 = f32[32,1,128]{2,1,0:T(1,128)S(1)} all-to-all(f32[32,1,128]{2,1,0:T(1,128)S(1)} %bitcast.48), channel_id=1, replica_groups=mesh['slab_0'=8,'slab_1'=4,'slab_2'=8,'slab_3'=2] {'slab_1','slab_2'}, dimensions={0} | all-to-all | bytes 32768 | tf_op jit(solution)/shard_map/all_to_all | solution.py:464
  110.9 0.6 total.1
  111.5 9.4 %all-to-all-start.1 = ((f32[16,1,128]{2,1,0:T(1,128)}), f32[16,1,128]{2,1,0:T(1,128)S(1)}, u32[]{:S(2)}, u32[]{:S(2)}) async-start(f32[16,1,128]{2,1,0:T(1,128)} %bitcast.20), calls=%async_computation.1 | async-start | bytes 16384 | tf_op jit(solution)/shard_map/all_to_all | solution.py:464
  120.9 7.0 %all-to-all-done.1 = f32[16,1,128]{2,1,0:T(1,128)S(1)} async-done(((f32[16,1,128]{2,1,0:T(1,128)}), f32[16,1,128]{2,1,0:T(1,128)S(1)}, u32[]{:S(2)}, u32[]{:S(2)}) %all-to-all-start.1) | async-done | bytes 8224 | tf_op jit(solution)/shard_map/all_to_all | solution.py:464
  127.9 2.6 %finish.1 = (f32[2,1,256,256]{3,2,1,0:T(8,128)}, f32[2,8]{1,0:T(2,128)S(1)}, f32[2,7]{1,0:T(2,128)S(1)}, f32[2,6]{1,0:T(2,128)S(1)}, s32[1,128]{1,0:T(1,128)S(1)}) custom-call(f32[8,256]{1,0:T(8,128)S(1)} %get-tuple-element.79.base_ref, f32[16,128]{1,0:T(8,128)S(1)} %bitcast.50, f32[2,256,256]{2,1,0:T(8,128)S(1)} %get-tuple-element.82.across.p0_across, ...), custom_call_target="tpu_custom_call" | custom-call | flops 4000000 | bytes 4000000 | tf_op jit(solution)/shard_map/finish/pallas_call | solution.py:518
  130.6 0.5 copy-done.4
  (14 shorter events, 0.7 us)
Async XLA Ops:
  2.2 10.3 %collective-permute-start.8 = (f32[2,256,256]{2,1,0:T(8,128)S(1)}, f32[2,256,256]{2,1,0:T(8,128)S(1)}, u32[]{:S(2)}, u32[]{:S(2)}) collective-permute-start(f32[2,256,256]{2,1,0:T(8,128)S(1)} %get-tuple-element.81), channel_id=1, source_target_pairs={{0,1},{1,0},{2,3},{3,2},{4,5},{5,4},{6,7},{7,6},{8,9},{9,8},{10,11... | collective-permute-start | bytes 1572872 | tf_op jit(solution)/shard_map/ppermute | solution.py:468
  13.1 22.3 %collective-permute-start.9 = (f32[2,256,256]{2,1,0:T(8,128)S(1)}, f32[2,256,256]{2,1,0:T(8,128)S(1)}, u32[]{:S(2)}, u32[]{:S(2)}) collective-permute-start(f32[2,256,256]{2,1,0:T(8,128)S(1)} %get-tuple-element.82.across.p0_across), channel_id=1, source_target_pairs={{0,510},{1,511},{2,4},{3,5},{4,2},{5,3},{6,8},{7,9},{8,6},{9,7},{1... | collective-permute-start | bytes 1572872 | tf_op jit(solution)/shard_map/ppermute | solution.py:468
  23.6 14.7 %collective-permute-start.10 = (f32[2,256,256]{2,1,0:T(8,128)S(1)}, f32[2,256,256]{2,1,0:T(8,128)S(1)}, u32[]{:S(2)}, u32[]{:S(2)}) collective-permute-start(f32[2,256,256]{2,1,0:T(8,128)S(1)} %get-tuple-element.83.inside.p0_inside), channel_id=1, source_target_pairs={{0,2},{1,3},{2,0},{3,1},{4,6},{5,7},{6,4},{7,5},{8,10},{9,11},{10,... | collective-permute-start | bytes 1572872 | tf_op jit(solution)/shard_map/ppermute | solution.py:468
  39.6 19.3 %collective-permute-start.11 = (f32[2,256,256]{2,1,0:T(8,128)S(1)}, f32[2,256,256]{2,1,0:T(8,128)S(1)}, u32[]{:S(2)}, u32[]{:S(2)}) collective-permute-start(f32[2,256,256]{2,1,0:T(8,128)S(1)} %get-tuple-element.85.across.new_across.p2_across), channel_id=1, source_target_pairs={{0,510},{1,511},{2,4},{3,5},{4,2},{5,3},{6,8},{7,9},{8,6},{9,7},{1... | collective-permute-start | bytes 1572872 | tf_op jit(solution)/shard_map/ppermute | solution.py:468
  45.3 13.9 %collective-permute-start.12 = (f32[2,256,256]{2,1,0:T(8,128)S(1)}, f32[2,256,256]{2,1,0:T(8,128)S(1)}, u32[]{:S(2)}, u32[]{:S(2)}) collective-permute-start(f32[2,256,256]{2,1,0:T(8,128)S(1)} %get-tuple-element.86.inside.new_inside.p2_inside), channel_id=1, source_target_pairs={{0,2},{1,3},{2,0},{3,1},{4,6},{5,7},{6,4},{7,5},{8,10},{9,11},{10,... | collective-permute-start | bytes 1572872 | tf_op jit(solution)/shard_map/ppermute | solution.py:468
  60.5 18.4 %collective-permute-start.13 = (f32[2,256,256]{2,1,0:T(8,128)S(1)}, f32[2,256,256]{2,1,0:T(8,128)S(1)}, u32[]{:S(2)}, u32[]{:S(2)}) collective-permute-start(f32[2,256,256]{2,1,0:T(8,128)S(1)} %get-tuple-element.87.across.new_across), channel_id=1, source_target_pairs={{0,510},{1,511},{2,4},{3,5},{4,2},{5,3},{6,8},{7,9},{8,6},{9,7},{1... | collective-permute-start | bytes 1572872 | tf_op jit(solution)/shard_map/ppermute | solution.py:468
  66.2 13.0 %collective-permute-start.14 = (f32[2,256,256]{2,1,0:T(8,128)S(1)}, f32[2,256,256]{2,1,0:T(8,128)S(1)}, u32[]{:S(2)}, u32[]{:S(2)}) collective-permute-start(f32[2,256,256]{2,1,0:T(8,128)S(1)} %get-tuple-element.88.inside.new_inside), channel_id=1, source_target_pairs={{0,2},{1,3},{2,0},{3,1},{4,6},{5,7},{6,4},{7,5},{8,10},{9,11},{10,... | collective-permute-start | bytes 1572872 | tf_op jit(solution)/shard_map/ppermute | solution.py:468
  69.2 51.6 %collective-permute-start.17 = (f32[4,256,256]{2,1,0:T(8,128)}, f32[4,256,256]{2,1,0:T(8,128)}, u32[]{:S(2)}, u32[]{:S(2)}) collective-permute-start(f32[4,256,256]{2,1,0:T(8,128)} %swap.1), channel_id=1, source_target_pairs={{0,1},{1,0},{2,3},{3,2},{4,5},{5,4},{6,7},{7,6},{8,9},{9,8},{10,11... | collective-permute-start | bytes 3145736 | tf_op jit(solution)/shard_map/ppermute | solution.py:468
  80.5 17.6 %collective-permute-start.15 = (f32[2,256,256]{2,1,0:T(8,128)S(1)}, f32[2,256,256]{2,1,0:T(8,128)S(1)}, u32[]{:S(2)}, u32[]{:S(2)}) collective-permute-start(f32[2,256,256]{2,1,0:T(8,128)S(1)} %get-tuple-element.89.new_across.across), channel_id=1, source_target_pairs={{0,510},{1,511},{2,4},{3,5},{4,2},{5,3},{6,8},{7,9},{8,6},{9,7},{1... | collective-permute-start | bytes 1572872 | tf_op jit(solution)/shard_map/ppermute | solution.py:468
  86.2 12.2 %collective-permute-start.16 = (f32[2,256,256]{2,1,0:T(8,128)S(1)}, f32[2,256,256]{2,1,0:T(8,128)S(1)}, u32[]{:S(2)}, u32[]{:S(2)}) collective-permute-start(f32[2,256,256]{2,1,0:T(8,128)S(1)} %get-tuple-element.90.new_inside.inside), channel_id=1, source_target_pairs={{0,2},{1,3},{2,0},{3,1},{4,6},{5,7},{6,4},{7,5},{8,10},{9,11},{10,... | collective-permute-start | bytes 1572872 | tf_op jit(solution)/shard_map/ppermute | solution.py:468
  111.5 16.3 %all-to-all-start.1 = ((f32[16,1,128]{2,1,0:T(1,128)}), f32[16,1,128]{2,1,0:T(1,128)S(1)}, u32[]{:S(2)}, u32[]{:S(2)}) async-start(f32[16,1,128]{2,1,0:T(1,128)} %bitcast.20), calls=%async_computation.1 | async-start | bytes 16384 | tf_op jit(solution)/shard_map/all_to_all | solution.py:464
  127.9 2.7 %copy-start.2 = (s32[1,256,256]{2,1,0:T(8,128)S(1)}, s32[1,256,256]{2,1,0:T(8,128)}, u32[]{:S(2)}) copy-start(s32[1,256,256]{2,1,0:T(8,128)} %levels_ref.1) | copy-start | bytes 786436
  127.9 2.7 %copy-start.3 = (f32[16]{0:T(128)S(1)}, f32[16]{0:T(128)}, u32[]{:S(2)}) copy-start(f32[16]{0:T(128)} %param.9) | copy-start | bytes 196
  130.5 0.6 copy-start.4
  130.6 0.6 copy-start.5
  130.6 0.6 copy-start.6
